TPU v7x, 128 devices: a whole 4x4x4 slice. The times are simulated.
128 devices in a mesh: seq: 16 (over z, y), head: 8 (over x, core).
Axes of the slice: x: 4, y: 4, z: 4, core: 2. Of those that a mesh axis runs over, the one named last changes fastest.
Arguments:
- prompt_tokens: bfloat16 [2, 4096, 8192], P(None, ('seq', 'head')), may hold values from -6 to 6
- prompt_write: bfloat16 [2, 4096, 1024], P(None, 'seq', 'head'), may hold values from -0.47851562 to 0.47851562
- prompt_read: bfloat16 [2, 4096, 1024], P(None, 'seq', 'head'), may hold values from -0.47851562 to 0.47851562
- prompt_decay: float32 [2, 128, 4096], P(None, 'head', 'seq'), may hold values from -1 to 0, as said below
- prompt_cotangent: bfloat16 [2, 4096, 8192], P(None, 'seq', 'head'), may hold values from -6 to 6
- answer_tokens: bfloat16 [16, 256, 8192], P('seq', 'head'), may hold values from -6 to 6
- answer_write: bfloat16 [16, 256, 1024], P('seq', None, 'head'), may hold values from -0.47851562 to 0.47851562
- answer_read: bfloat16 [16, 256, 1024], P('seq', None, 'head'), may hold values from -0.47851562 to 0.47851562
- answer_decay: float32 [16, 128, 256], P('seq', 'head'), may hold values from -1 to 0, as said below
- answer_cotangent: bfloat16 [16, 256, 8192], P('seq', None, 'head'), may hold values from -6 to 6
- group_sizes: int32 [2], replicated, may hold values from 4 to 12, as said below
- answer_lengths: int32 [16], P('seq'), may hold values from 1 to 256, 2560 in all
Outputs:
- prompt_output: bfloat16 [2, 4096, 8192], P(None, 'seq', 'head')
- prompt_tokens_adjoint: bfloat16 [2, 4096, 8192], P(None, ('seq', 'head'))
- prompt_write_adjoint: bfloat16 [2, 4096, 1024], P(None, 'seq', 'head')
- prompt_read_adjoint: bfloat16 [2, 4096, 1024], P(None, 'seq', 'head')
- prompt_decay_adjoint: float32 [2, 128, 4096], P(None, 'head', 'seq')
- answer_output: bfloat16 [16, 256, 8192], P('seq', None, 'head')
- answer_tokens_adjoint: bfloat16 [16, 256, 8192], P('seq', 'head')
- answer_write_adjoint: bfloat16 [16, 256, 1024], P('seq', None, 'head')
- answer_read_adjoint: bfloat16 [16, 256, 1024], P('seq', None, 'head')
- answer_decay_adjoint: float32 [16, 128, 256], P('seq', 'head')
Inputs may be any that keep to these rules, and one draw needn't show every extreme that they name: Completions are stored in prompt order: the first group_sizes[0] completions follow prompt 0, the next group_sizes[1] prompt 1, and so on; the sizes sum to 16, and one prompt has exactly 12. Completion i has loss and outputs at its first answer_lengths[i] positions only. `prompt_decay`: log decays are negative. `answer_decay`: log decays are negative.
All inputs are finite; a program needn't handle non-finite values. No bound on the sum of `answer_lengths` on one device may be relied on, other than what follows from the above.
Results may differ from a plain program's by a relative error of at most 0.015.
Values may be sent and summed in bfloat16 or wider, within the bound.
No kernel may reach another device: no remote copies, remote signals or barrier semaphores. Data moves between devices by JAX's collectives and lax.ppermute only.
A program may use at most 128 MiB of HBM per device.

v0:
```python
import jax
import jax.numpy as jnp
from jax import lax
from jax.experimental import pallas as pl
from jax.experimental.pallas import tpu as pltpu
from jax.sharding import PartitionSpec as P


HD = 64
N = 128
B = 256
H = 16
L = H * HD
SHARDS = 16
GROUP = 8
ROWS = B // GROUP
HALF = L // 2
F32 = jnp.float32
BF16 = jnp.bfloat16


def nn(a, b):
    return lax.dot_general(a, b, (((1,), (0,)), ((), ())), preferred_element_type=F32)


def nt(a, b):
    return lax.dot_general(a, b, (((1,), (1,)), ((), ())), preferred_element_type=F32)


def tn(a, b):
    return lax.dot_general(a, b, (((0,), (0,)), ((), ())), preferred_element_type=F32)


def iota(shape, axis):
    return lax.broadcasted_iota(jnp.int32, shape, axis)


def terms(value):
    high = value.astype(BF16)
    rest = value - high.astype(F32)
    middle = rest.astype(BF16)
    return high, middle, (rest - middle.astype(F32)).astype(BF16)


def upper():
    return (iota((B, B), 0) <= iota((B, B), 1)).astype(BF16)


def lower():
    return (iota((B, B), 1) <= iota((B, B), 0)).astype(BF16)


def running_rows(decay):
    parts = nn(jnp.concatenate([part.astype(F32) for part in terms(decay)], axis=0).astype(BF16), upper())
    return parts[:H] + parts[H : 2 * H] + parts[2 * H :]


def running_columns(decay):
    tri = lower()
    total = None
    for part in terms(decay):
        wide = part.astype(F32)
        added = nt(tri, jnp.concatenate([wide, wide, wide], axis=0).astype(BF16))
        total = added if total is None else total + added
    return total


def widened(columns):
    lane = iota(columns.shape, 1)
    high = columns.astype(BF16).astype(F32)
    rest = columns - high
    middle = rest.astype(BF16).astype(F32)
    packed = jnp.where(lane < H, high, jnp.where(lane < 2 * H, middle, rest - middle)).astype(BF16)
    member = (iota((3 * H, L), 1) // HD == iota((3 * H, L), 0) % H).astype(BF16)
    return nn(packed, member)


def grown(decay):
    return widened(jnp.exp(running_columns(decay)))


def closing_weight(decay):
    columns = running_columns(decay)
    return widened(jnp.exp(columns[B - 1 : B, :] - columns))


def head_sums(values):
    member = (iota((L, H), 0) // HD == iota((L, H), 1)).astype(BF16)
    high = values.astype(BF16)
    low = (values - high.astype(F32)).astype(BF16)
    return nn(high, member) + nn(low, member)


def live_rows(value, length):
    return jnp.where(iota(value.shape, 0) < length, value, jnp.zeros_like(value))


def piece(d):
    return slice(16 * (d // 2), 16 * (d // 2) + 16), slice(HALF * (d % 2), HALF * (d % 2) + HALF)


def scattered(out, state, first):
    for d in range(SHARDS):
        rows, lanes = piece(d)
        out[16 * d : 16 * d + 16, first : first + HALF] = state[rows, lanes].astype(BF16)


def gathered(m, place):
    for d in range(SHARDS):
        rows, lanes = piece(d)
        place[rows, lanes] = m[16 * d : 16 * d + 16, :]


def assembled(me, chunks, x):
    for k in range(GROUP):
        there = pl.multiple_of((me[0] ^ k) * ROWS, ROWS)
        x[pl.ds(there, ROWS), :] = chunks[k][0]


def reach_kernel(length, pr, pd, pc, ar, ad, ac, out, factors):
    b = pl.program_id(0)

    @pl.when(b < 3)
    def _():
        answer = b == 2
        read = jnp.where(answer, ar[0], pr[0])
        decay = jnp.where(answer, ad[0], pd[0])
        alive = jnp.where(answer, length[0], B)
        cot = live_rows(jnp.where(answer, ac[0], pc[0]).astype(F32), alive)
        growth = grown(decay)
        scattered(out, tn(read, (cot * growth).astype(BF16)), 0)
        last = growth[B - 1 : B, :]
        high = last.astype(BF16).astype(F32)
        row = iota((16, L), 0) - 2 * b
        part = jnp.where(row == 0, high, jnp.where(row == 1, last - high, 0.0))
        factors[...] = jnp.where(b == 0, part, jnp.where(answer, factors[...], factors[...] + part))

    @pl.when(b == 3)
    def _():
        for d in range(SHARDS):
            out[16 * d : 16 * d + 16, :] = factors[:, piece(d)[1]].astype(BF16)


def split_kernel(me, pt, at, *outs):
    b = pl.program_id(0)
    for k in range(GROUP):
        there = pl.multiple_of((me[0] ^ k) * L, L)
        outs[k][0] = jnp.where(b == 2, at[0, :, pl.ds(there, L)], pt[0, :, pl.ds(there, L)])


def join_kernel(me, *refs):
    b = pl.program_id(0)
    ins, (pt, at) = refs[:GROUP], refs[GROUP:]
    for k in range(GROUP):
        there = pl.multiple_of((me[0] ^ k) * L, L)

        @pl.when(b < 2)
        def _():
            pt[0, :, pl.ds(there, L)] = ins[k][0]

        @pl.when(b == 2)
        def _():
            at[0, :, pl.ds(there, L)] = ins[k][0]


def shard_factor(factors, k, q):
    part = factors[16 * k : 16 * k + 16, :].astype(F32)
    row = iota((16, HALF), 0) - 2 * q
    return jnp.sum(jnp.where((row == 0) | (row == 1), part, 0.0), axis=0, keepdims=True)


def owner_of(sizes, k):
    return (sizes[0] <= k).astype(jnp.int32) + (sizes[0] + sizes[1] <= k).astype(jnp.int32)


def close_kernel(me, sizes, reach, answers, factors, pw, pd, *refs):
    q = pl.program_id(0)
    chunks, (out, x) = refs[:GROUP], refs[GROUP:]
    assembled(me, chunks, x)
    weighted = (x[...].astype(F32) * closing_weight(pd[0])).astype(BF16)
    scattered(out, tn(pw[0], weighted), HALF)
    grad = jnp.zeros((16, HALF), F32)
    for k in range(SHARDS):
        part = answers[16 * k : 16 * k + 16, :].astype(F32)
        grad = grad + part * (owner_of(sizes, k) == q).astype(F32)
    for k in reversed(range(SHARDS)):
        out[16 * k : 16 * k + 16, :HALF] = grad.astype(BF16)
        grad = reach[16 * k : 16 * k + 16, :].astype(F32) + shard_factor(factors, k, q) * grad


def start_kernel(sizes, factors, first, second, out):
    ends = []
    for q, local in enumerate((first, second)):
        state = jnp.zeros((16, HALF), F32)
        for k in range(SHARDS):
            out[16 * k : 16 * k + 16, q * HALF : (q + 1) * HALF] = state.astype(BF16)
            state = shard_factor(factors, k, q) * state + local[16 * k : 16 * k + 16, :].astype(F32)
        ends.append(state)
    for k in range(SHARDS):
        owner = owner_of(sizes, k)
        mine = ends[0] * (owner == 0).astype(F32) + ends[1] * (owner == 1).astype(F32)
        out[16 * k : 16 * k + 16, 2 * HALF : 3 * HALF] = mine.astype(BF16)


def inside_kernel(length, me, pw, pr, pd, pc, aw, ar, ad, ac, *refs):
    chunks, (y_out, dx_out, dr_out, dw_out, adw, z_out, x, zs) = refs[:GROUP], refs[GROUP:]
    b = pl.program_id(0)
    answer = b == 2
    write = jnp.where(answer, aw[0], pw[0])
    read = jnp.where(answer, ar[0], pr[0])
    decay = jnp.where(answer, ad[0], pd[0])
    alive = jnp.where(answer, length[0], B)
    cot32 = live_rows(jnp.where(answer, ac[0], pc[0]).astype(F32), alive)
    cot_t = cot32.T.astype(BF16)
    assembled(me, chunks, x)
    rows = running_rows(decay)
    columns = running_columns(decay)
    scores = nt(read, write)
    causal = iota((B, B), 0) >= iota((B, B), 1)
    first = iota((B, 2 * HD), 1) < HD
    grad = jnp.zeros((B, B), F32)
    for pair in range(H // 2):
        lanes = slice(2 * HD * pair, 2 * HD * pair + 2 * HD)
        xs = x[:, lanes]
        cs = cot32[:, lanes]
        ys, dxs = [], []
        for s in range(2):
            h = 2 * pair + s
            gap = columns[:, h : h + 1] - rows[h : h + 1, :]
            weight = jnp.exp(jnp.where(causal, gap, -1e30))
            mixing = (weight * scores).astype(BF16)
            ys.append(nn(mixing, xs))
            dxs.append(nn(cot_t[HD * h : HD * h + HD, :], mixing))
            own = jnp.where(first if s == 0 else jnp.logical_not(first), cs, 0.0).astype(BF16)
            grad = grad + nt(own, xs) * weight
        y = jnp.where(first, ys[0], ys[1])
        dx = jnp.concatenate(dxs, axis=0).T
        y_out[0, :, lanes] = y.astype(BF16)
        dx_out[0, :, lanes] = dx.astype(BF16)
        zs[:, lanes] = cs * y - xs.astype(F32) * dx
    z_out[0] = head_sums(zs[...])
    grad = grad.astype(BF16)
    dr_out[0] = nn(grad, write)
    dw = tn(grad, read)

    @pl.when(b < 2)
    def _():
        dw_out[0] = dw

    @pl.when(answer)
    def _():
        adw[0] = dw.astype(BF16)


def token_kernel(me, m2, pw, pd, dxi, *refs):
    outs, (ends, full) = refs[:GROUP], refs[GROUP:]
    b = pl.program_id(0)

    @pl.when(b < 2)
    def _():
        gathered(m2, ends)
        full[...] = (dxi[0].astype(F32) + nn(pw[0], ends[...]) * closing_weight(pd[0])).astype(BF16)

    @pl.when(b == 2)
    def _():
        full[...] = dxi[0]

    for k in range(GROUP):
        there = pl.multiple_of((me[0] ^ k) * ROWS, ROWS)
        outs[k][0] = full[pl.ds(there, ROWS), :]


def write_kernel(me, m2, pw, pd, dwi, *refs):
    chunks, (pdw, z, closing, x, ends) = refs[:GROUP], refs[GROUP:]
    assembled(me, chunks, x)
    gathered(m2, ends)
    xs = x[...].astype(F32)
    to_close = closing_weight(pd[0])
    weighted = (xs * to_close).astype(BF16)
    pdw[0] = (dwi[0] + nt(weighted, ends[...])).astype(BF16)
    tail = xs * (nn(pw[0], ends[...]) * to_close)
    closing[0] = jnp.broadcast_to(jnp.sum(tail, axis=0, keepdims=True), (8, L))
    z[0] = head_sums(tail)


def output_kernel(
    length, m2, m3, pr, pd, pc, ar, ad, ac, yi, dri, zi, z, closing, py, pdr, pdd, ay, adr, add, start, ends
):
    b = pl.program_id(0)
    answer = b == 2
    gathered(m3, start)
    read = jnp.where(answer, ar[0], pr[0])
    decay = jnp.where(answer, ad[0], pd[0])
    alive = jnp.where(answer, length[0], B)
    cot = live_rows(jnp.where(answer, ac[0], pc[0]).astype(F32), alive)
    growth = grown(decay)
    outside = nn(read, start[...]) * growth
    y = yi[0].astype(F32) + outside
    dr = dri[0] + nt((cot * growth).astype(BF16), start[...])
    zs = zi[0] + head_sums(cot * outside) - jnp.where(answer, 0.0, z[0])
    tri = lower()
    dd = sum(tn(part, tri) for part in terms(zs))

    @pl.when(b < 2)
    def _():
        gathered(m2, ends)
        inner = jnp.sum(ends[...].astype(F32) * start[...].astype(F32), axis=0, keepdims=True)
        last = closing[0] + inner * growth[B - 1 : B, :]
        member = (iota((H, L), 1) // HD == iota((H, L), 0)).astype(BF16)
        total = sum(nt(member, part) for part in terms(last))
        py[0] = y.astype(BF16)
        pdr[0] = dr.astype(BF16)
        pdd[0] = dd + total[:, 0:1]

    @pl.when(answer)
    def _():
        ay[0] = live_rows(y, length[0]).astype(BF16)
        adr[0] = dr.astype(BF16)
        add[0] = dd


SMEM = pl.BlockSpec(memory_space=pltpu.SMEM)


def own(*dims):
    return pl.BlockSpec((1, *dims), lambda b: (jnp.minimum(b, 1), 0, 0))


def one(*dims):
    return pl.BlockSpec((1, *dims), lambda b: (0, 0, 0))


def each(*dims):
    return pl.BlockSpec((1, *dims), lambda b: (b, 0, 0))


def column(width, index):
    return pl.BlockSpec((B, width), lambda b: (0, index(b)))


def shape(dims, dtype=BF16):
    return jax.ShapeDtypeStruct(dims, dtype)


def call(kernel, steps, ins, outs, args, scratch=(), flops=1e9):
    return pl.pallas_call(
        kernel,
        grid=(steps,),
        in_specs=ins,
        out_specs=[spec for spec, _ in outs],
        out_shape=[struct for _, struct in outs],
        scratch_shapes=scratch,
        cost_estimate=pl.CostEstimate(flops=int(flops), bytes_accessed=4000000, transcendentals=0),
    )(*args)


def exchange(chunks):
    sent = [chunks[0]]
    for k in range(1, GROUP):
        sent.append(lax.ppermute(chunks[k], "head", [(i, i ^ k) for i in range(GROUP)]))
    return sent


def transposed(message):
    return lax.all_to_all(message, "seq", split_axis=0, concat_axis=0, tiled=True)


def per_device(pt, pw, pr, pd, pc, at, aw, ar, ad, ac, sizes, length):
    me = lax.axis_index("head").astype(jnp.int32).reshape(1)
    state = pltpu.VMEM((N, L), BF16)
    block = pltpu.VMEM((B, L), BF16)
    chunk = [(each(ROWS, L), shape((3, ROWS, L))) for _ in range(GROUP)]
    pieces = [each(ROWS, L)] * GROUP
    prompt_side = [own(B, N), own(H, B), own(B, L)]
    answer_side = [one(B, N), one(H, B), one(B, L)]
    (m1,) = call(
        reach_kernel,
        4,
        [SMEM, *prompt_side, *answer_side],
        [(column(HALF, lambda b: b), shape((B, 4 * HALF)))],
        (length, pr, pd, pc, ar, ad, ac),
        (pltpu.VMEM((16, L), F32),),
    )
    m1 = transposed(m1)
    cut = call(split_kernel, 3, [SMEM, own(ROWS, GROUP * L), one(ROWS, GROUP * L)], chunk, (me, pt, at))
    cut = exchange(cut)
    (m2,) = call(
        close_kernel,
        2,
        [
            SMEM,
            SMEM,
            column(HALF, lambda q: q),
            column(HALF, lambda q: 2),
            column(HALF, lambda q: 3),
            each(B, N),
            each(H, B),
            *pieces,
        ],
        [(column(2 * HALF, lambda q: q), shape((B, 4 * HALF)))],
        (me, sizes, m1, m1, m1, pw, pd, *cut),
        (block,),
    )
    m2 = transposed(m2)
    yi, dxi, dri, dwi, adw, zi = call(
        inside_kernel,
        3,
        [SMEM, SMEM, own(B, N), *prompt_side, one(B, N), *answer_side, *pieces],
        [
            (each(B, L), shape((3, B, L))),
            (each(B, L), shape((3, B, L))),
            (each(B, N), shape((3, B, N), F32)),
            (own(B, N), shape((2, B, N), F32)),
            (one(B, N), shape((1, B, N))),
            (each(B, H), shape((3, B, H), F32)),
        ],
        (length, me, pw, pr, pd, pc, aw, ar, ad, ac, *cut),
        (block, pltpu.VMEM((B, L), F32)),
        8e9,
    )
    (m3,) = call(
        start_kernel,
        1,
        [SMEM, column(HALF, lambda b: 3), column(HALF, lambda b: 1), column(HALF, lambda b: 3)],
        [(column(3 * HALF, lambda b: 0), shape((B, 3 * HALF)))],
        (sizes, m1, m2, m2),
    )
    m3 = transposed(m3)
    back = call(
        token_kernel,
        3,
        [SMEM, column(HALF, lambda b: 2 * jnp.minimum(b, 1)), own(B, N), own(H, B), each(B, L)],
        chunk,
        (me, m2, pw, pd, dxi),
        (state, block),
    )
    back = exchange(back)
    pdw, z, closing = call(
        write_kernel,
        2,
        [SMEM, column(HALF, lambda q: 2 * q), each(B, N), each(H, B), each(B, N), *pieces],
        [
            (each(B, N), shape((2, B, N))),
            (each(B, H), shape((2, B, H), F32)),
            (each(8, L), shape((2, 8, L), F32)),
        ],
        (me, m2, pw, pd, dwi, *cut),
        (block, state),
    )
    py, pdr, pdd, ay, adr, add = call(
        output_kernel,
        3,
        [
            SMEM,
            column(HALF, lambda b: 2 * jnp.minimum(b, 1)),
            column(HALF, lambda b: b),
            *prompt_side,
            *answer_side,
            each(B, L),
            each(B, N),
            each(B, H),
            own(B, H),
            own(8, L),
        ],
        [
            (own(B, L), shape((2, B, L))),
            (own(B, N), shape((2, B, N))),
            (own(H, B), shape((2, H, B), F32)),
            (one(B, L), shape((1, B, L))),
            (one(B, N), shape((1, B, N))),
            (one(H, B), shape((1, H, B), F32)),
        ],
        (length, m2, m3, pr, pd, pc, ar, ad, ac, yi, dri, zi, z, closing),
        (state, state),
    )
    pdx, adx = call(
        join_kernel,
        3,
        [SMEM, *pieces],
        [
            (own(ROWS, GROUP * L), shape((2, ROWS, GROUP * L))),
            (one(ROWS, GROUP * L), shape((1, ROWS, GROUP * L))),
        ],
        (me, *back),
    )
    return py, pdx, pdw, pdr, pdd, ay, adx, adw, adr, add


def solution(mesh):
    split_positions = P(None, ("seq", "head"), None)
    prompt = P(None, "seq", "head")
    answer = P("seq", None, "head")
    return jax.shard_map(
        per_device,
        mesh=mesh,
        in_specs=(
            split_positions,
            prompt,
            prompt,
            P(None, "head", "seq"),
            prompt,
            P("seq", "head", None),
            answer,
            answer,
            P("seq", "head", None),
            answer,
            P(),
            P("seq"),
        ),
        out_specs=(
            prompt,
            split_positions,
            prompt,
            prompt,
            P(None, "head", "seq"),
            answer,
            P("seq", "head", None),
            answer,
            answer,
            P("seq", "head", None),
        ),
        check_vma=False,
    )
```

profile of v0, /device:TPU:1, one launch (start us, length us, event | category | flops | bytes accessed | tf_op | source)
XLA Modules:
  0.0 135.5 jit_solution(13697071137220973276)
XLA Ops:
  1.3 4.7 %shard_map.195 = bf16[256,2048]{1,0:T(8,128)(2,1)} custom-call(s32[1]{0:T(128)S(6)} %copy.22.length, bf16[2,256,128]{2,1,0:T(8,128)(2,1)} %pr.5, f32[2,16,256]{2,1,0:T(8,128)} %pd.11, bf16[2,256,1024]{2,1,0:T(8,128)(2,1)} %pc.5, bf16[1,256,128]{2,1,0:T(8,128)(2,1)} %ar.5, f32[1,16,256]{2,1,0:T(8,128)} %ad.5, bf16[1,256,1024]{2,1,0:T(8,128)(2,1)} %ac.5), custom_call_target="tpu_custom_call" | custom-call | flops 1000000000 | bytes 4000000 | tf_op jit(solution)/shard_map/pallas_call | solution.py:346
  6.0 8.6 %all-to-all-start = ((bf16[16,16,2048]{2,1,0:T(8,128)(2,1)}), bf16[16,16,2048]{2,1,0:T(8,128)(2,1)S(1)}, u32[]{:S(2)}, u32[]{:S(2)}) async-start(bf16[16,16,2048]{2,1,0:T(8,128)(2,1)} %bitcast.19), calls=%async_computation | async-start | bytes 2097152 | tf_op jit(solution)/shard_map/all_to_all | solution.py:365
  14.6 2.9 %shard_map.196 = (bf16[3,32,1024]{2,1,0:T(8,128)(2,1)}, bf16[3,32,1024]{2,1,0:T(8,128)(2,1)}, bf16[3,32,1024]{2,1,0:T(8,128)(2,1)}, bf16[3,32,1024]{2,1,0:T(8,12...) custom-call(s32[1]{0:T(128)} %bitcast.me, ...), custom_call_target="tpu_custom_call" | custom-call | flops 1000000000 | bytes 4000000 | tf_op jit(solution)/shard_map/pallas_call | solution.py:346
  17.5 1.0 collective-permute-start
  18.6 1.2 collective-permute-start.1
  19.8 0.5 collective-permute-start.2
  20.3 2.7 %collective-permute-start.3 = (bf16[3,32,1024]{2,1,0:T(8,128)(2,1)}, bf16[3,32,1024]{2,1,0:T(8,128)(2,1)S(1)}, u32[]{:S(2)}, u32[]{:S(2)}) collective-permute-start(bf16[3,32,1024]{2,1,0:T(8,128)(2,1)} %get-tuple-element.47), channel_id=1, source_target_pairs={{0,4},{1,5},{2,6},{3,7},{4,0},{5,1},{6,2},{7,3},{8,12},{9,13},{10,... | collective-permute-start | bytes 589832 | tf_op jit(solution)/shard_map/ppermute | solution.py:360
  23.0 0.5 collective-permute-start.4
  23.6 0.0 collective-permute-done.refs_1_
  23.6 0.0 copy-start.2
  23.6 2.5 %collective-permute-start.5 = (bf16[3,32,1024]{2,1,0:T(8,128)(2,1)}, bf16[3,32,1024]{2,1,0:T(8,128)(2,1)S(1)}, u32[]{:S(2)}, u32[]{:S(2)}) collective-permute-start(bf16[3,32,1024]{2,1,0:T(8,128)(2,1)} %get-tuple-element.49), channel_id=1, source_target_pairs={{0,6},{1,7},{2,4},{3,5},{4,2},{5,3},{6,0},{7,1},{8,14},{9,15},{10,... | collective-permute-start | bytes 589832 | tf_op jit(solution)/shard_map/ppermute | solution.py:360
  26.0 0.0 collective-permute-done.1.refs_2_
  26.0 0.0 copy-start.3
  26.1 3.0 %collective-permute-start.6 = (bf16[3,32,1024]{2,1,0:T(8,128)(2,1)}, bf16[3,32,1024]{2,1,0:T(8,128)(2,1)S(1)}, u32[]{:S(2)}, u32[]{:S(2)}) collective-permute-start(bf16[3,32,1024]{2,1,0:T(8,128)(2,1)} %get-tuple-element.50), channel_id=1, source_target_pairs={{0,7},{1,6},{2,5},{3,4},{4,3},{5,2},{6,1},{7,0},{8,15},{9,14},{10,... | collective-permute-start | bytes 589832 | tf_op jit(solution)/shard_map/ppermute | solution.py:360
  29.0 1.5 %collective-permute-done.2.refs_3_ = bf16[3,32,1024]{2,1,0:T(8,128)(2,1)S(1)} collective-permute-done((bf16[3,32,1024]{2,1,0:T(8,128)(2,1)}, bf16[3,32,1024]{2,1,0:T(8,128)(2,1)S(1)}, u32[]{:S(2)}, u32[]{:S(2)}) %collective-permute-start.2) | collective-permute-done | bytes 196640 | tf_op jit(solution)/shard_map/ppermute | solution.py:360
  30.5 0.0 copy-start.4
  30.5 5.3 %collective-permute-done.3.refs_4_ = bf16[3,32,1024]{2,1,0:T(8,128)(2,1)S(1)} collective-permute-done((bf16[3,32,1024]{2,1,0:T(8,128)(2,1)}, bf16[3,32,1024]{2,1,0:T(8,128)(2,1)S(1)}, u32[]{:S(2)}, u32[]{:S(2)}) %collective-permute-start.3) | collective-permute-done | bytes 196640 | tf_op jit(solution)/shard_map/ppermute | solution.py:360
  35.8 0.0 copy-start.5
  35.8 4.5 %collective-permute-done.4.refs_5_ = bf16[3,32,1024]{2,1,0:T(8,128)(2,1)S(1)} collective-permute-done((bf16[3,32,1024]{2,1,0:T(8,128)(2,1)}, bf16[3,32,1024]{2,1,0:T(8,128)(2,1)S(1)}, u32[]{:S(2)}, u32[]{:S(2)}) %collective-permute-start.4) | collective-permute-done | bytes 196640 | tf_op jit(solution)/shard_map/ppermute | solution.py:360
  40.3 0.0 collective-permute-done.5.refs_6_
  40.3 3.9 %collective-permute-done.6.refs_7_ = bf16[3,32,1024]{2,1,0:T(8,128)(2,1)S(1)} collective-permute-done((bf16[3,32,1024]{2,1,0:T(8,128)(2,1)}, bf16[3,32,1024]{2,1,0:T(8,128)(2,1)S(1)}, u32[]{:S(2)}, u32[]{:S(2)}) %collective-permute-start.6) | collective-permute-done | bytes 196640 | tf_op jit(solution)/shard_map/ppermute | solution.py:360
  44.3 0.0 all-to-all-done
  44.3 0.0 copy-done.2
  44.3 0.0 copy-done.3
  44.3 0.0 copy-done.4
  44.3 0.0 copy-done.5
  44.3 0.0 copy-done.6
  44.3 0.0 copy-done.7
  44.3 0.6 copy-done.8
  44.9 0.4 copy-done
  45.3 4.4 %shard_map.197 = bf16[256,2048]{1,0:T(8,128)(2,1)} custom-call(s32[1]{0:T(128)} %bitcast.me, s32[2]{0:T(128)} %sizes.3, bf16[256,2048]{1,0:T(8,128)(2,1)} %bitcast.7, bf16[256,2048]{1,0:T(8,128)(2,1)} %bitcast.8, bf16[256,2048]{1,0:T(8,128)(2,1)} %bitcast.9, bf16[2,256,128]{2,1,0:T(8,128)(2,1)} %pw.7, f32[2,16,256]{2,1,0:T(8,128)} %pd.11, ...), custom_call_target="tpu_custom_call" | custom-call | flops 1000000000 | bytes 4000000 | tf_op jit(solution)/shard_map/pallas_call | solution.py:346
  49.7 23.6 %all_to_all.33 = bf16[16,16,2048]{2,1,0:T(8,128)(2,1)} all-to-all(bf16[16,16,2048]{2,1,0:T(8,128)(2,1)} %bitcast.16), channel_id=1, replica_groups=mesh['seq'=16,'head'=8] {'seq'}, dimensions={0} | all-to-all | bytes 2097152 | tf_op jit(solution)/shard_map/all_to_all | solution.py:365
  73.3 2.3 %shard_map.198 = bf16[256,1536]{1,0:T(8,128)(2,1)} custom-call(s32[2]{0:T(128)} %sizes.3, bf16[256,2048]{1,0:T(8,128)(2,1)} %bitcast.10, bf16[256,2048]{1,0:T(8,128)(2,1)} %bitcast.11, bf16[256,2048]{1,0:T(8,128)(2,1)} %bitcast.12), custom_call_target="tpu_custom_call" | custom-call | flops 1000000000 | bytes 4000000 | tf_op jit(solution)/shard_map/pallas_call | solution.py:346
  75.6 3.6 %all-to-all-start.2 = ((bf16[16,16,1536]{2,1,0:T(8,128)(2,1)}), bf16[16,16,1536]{2,1,0:T(8,128)(2,1)S(1)}, u32[]{:S(2)}, u32[]{:S(2)}) async-start(bf16[16,16,1536]{2,1,0:T(8,128)(2,1)} %bitcast.18), calls=%async_computation.2 | async-start | bytes 1572864 | tf_op jit(solution)/shard_map/all_to_all | solution.py:365
  79.2 11.2 %shard_map.199 = (bf16[3,256,1024]{2,1,0:T(8,128)(2,1)}, bf16[3,256,1024]{2,1,0:T(8,128)(2,1)}, f32[3,256,128]{2,1,0:T(8,128)}, f32[2,256,128]{2,1,0:T(8,128)}, ...) custom-call(s32[1]{0:T(128)S(6)} %copy.22.length, s32[1]{0:T(128)} %bitcast.me, bf16[2,256,128]{2,1,0:T(8,128)(2,1)} %pw.7, ...), custom_call_target="tpu_custom_call" | custom-call | flops 8000000000 | bytes 4000000 | tf_op jit(solution)/shard_map/pallas_call | solution.py:346
  90.5 4.2 %shard_map.202 = (bf16[3,32,1024]{2,1,0:T(8,128)(2,1)}, bf16[3,32,1024]{2,1,0:T(8,128)(2,1)}, bf16[3,32,1024]{2,1,0:T(8,128)(2,1)}, bf16[3,32,1024]{2,1,0:T(8,12...) custom-call(s32[1]{0:T(128)} %bitcast.me, ...), custom_call_target="tpu_custom_call" | custom-call | flops 1000000000 | bytes 4000000 | tf_op jit(solution)/shard_map/pallas_call | solution.py:346
  94.6 1.6 %collective-permute-start.7 = (bf16[3,32,1024]{2,1,0:T(8,128)(2,1)}, bf16[3,32,1024]{2,1,0:T(8,128)(2,1)S(1)}, u32[]{:S(2)}, u32[]{:S(2)}) collective-permute-start(bf16[3,32,1024]{2,1,0:T(8,128)(2,1)} %get-tuple-element.60), channel_id=1, source_target_pairs={{0,1},{1,0},{2,3},{3,2},{4,5},{5,4},{6,7},{7,6},{8,9},{9,8},{10,11... | collective-permute-start | bytes 589832 | tf_op jit(solution)/shard_map/ppermute | solution.py:360
  96.3 0.0 collective-permute-start.8
  96.3 1.7 %collective-permute-start.9 = (bf16[3,32,1024]{2,1,0:T(8,128)(2,1)}, bf16[3,32,1024]{2,1,0:T(8,128)(2,1)S(1)}, u32[]{:S(2)}, u32[]{:S(2)}) collective-permute-start(bf16[3,32,1024]{2,1,0:T(8,128)(2,1)} %get-tuple-element.62), channel_id=1, source_target_pairs={{0,3},{1,2},{2,1},{3,0},{4,7},{5,6},{6,5},{7,4},{8,11},{9,10},{10,... | collective-permute-start | bytes 589832 | tf_op jit(solution)/shard_map/ppermute | solution.py:360
  98.0 2.0 %collective-permute-start.10 = (bf16[3,32,1024]{2,1,0:T(8,128)(2,1)}, bf16[3,32,1024]{2,1,0:T(8,128)(2,1)S(1)}, u32[]{:S(2)}, u32[]{:S(2)}) collective-permute-start(bf16[3,32,1024]{2,1,0:T(8,128)(2,1)} %get-tuple-element.63), channel_id=1, source_target_pairs={{0,4},{1,5},{2,6},{3,7},{4,0},{5,1},{6,2},{7,3},{8,12},{9,13},{10,... | collective-permute-start | bytes 589832 | tf_op jit(solution)/shard_map/ppermute | solution.py:360
  100.0 1.3 collective-permute-start.11
  101.3 0.0 collective-permute-done.7.refs_1_
  101.3 2.5 %collective-permute-start.12 = (bf16[3,32,1024]{2,1,0:T(8,128)(2,1)}, bf16[3,32,1024]{2,1,0:T(8,128)(2,1)S(1)}, u32[]{:S(2)}, u32[]{:S(2)}) collective-permute-start(bf16[3,32,1024]{2,1,0:T(8,128)(2,1)} %get-tuple-element.65), channel_id=1, source_target_pairs={{0,6},{1,7},{2,4},{3,5},{4,2},{5,3},{6,0},{7,1},{8,14},{9,15},{10,... | collective-permute-start | bytes 589832 | tf_op jit(solution)/shard_map/ppermute | solution.py:360
  103.8 0.0 collective-permute-done.8.refs_2_
  103.8 3.0 %collective-permute-start.13 = (bf16[3,32,1024]{2,1,0:T(8,128)(2,1)}, bf16[3,32,1024]{2,1,0:T(8,128)(2,1)S(1)}, u32[]{:S(2)}, u32[]{:S(2)}) collective-permute-start(bf16[3,32,1024]{2,1,0:T(8,128)(2,1)} %get-tuple-element.66), channel_id=1, source_target_pairs={{0,7},{1,6},{2,5},{3,4},{4,3},{5,2},{6,1},{7,0},{8,15},{9,14},{10,... | collective-permute-start | bytes 589832 | tf_op jit(solution)/shard_map/ppermute | solution.py:360
  106.7 4.7 %shard_map.200 = (bf16[2,256,128]{2,1,0:T(8,128)(2,1)}, f32[2,256,16]{2,1,0:T(8,128)}, f32[2,8,1024]{2,1,0:T(8,128)}) custom-call(s32[1]{0:T(128)} %bitcast.me, bf16[256,2048]{1,0:T(8,128)(2,1)} %bitcast.14, bf16[2,256,128]{2,1,0:T(8,128)(2,1)} %pw.7, f32[2,16,256]{2,1,0:T(8,128)} %pd.11, f32[2,256,128]{2,1,0:T(8,128)} %get-tuple-element.54.dwi, ...), custom_call_target="tpu_custom_call" | custom-call | flops 1000000000 | bytes 4000000 | tf_op jit(solution)/shard_map/pallas_call | solution.py:346
  111.4 0.0 copy-done.9
  111.4 0.0 copy-done.10
  111.5 0.0 collective-permute-done.9.refs_3_
  111.5 0.0 copy-start.11
  111.5 2.1 %collective-permute-done.10.refs_4_ = bf16[3,32,1024]{2,1,0:T(8,128)(2,1)S(1)} collective-permute-done((bf16[3,32,1024]{2,1,0:T(8,128)(2,1)}, bf16[3,32,1024]{2,1,0:T(8,128)(2,1)S(1)}, u32[]{:S(2)}, u32[]{:S(2)}) %collective-permute-start.10) | collective-permute-done | bytes 196640 | tf_op jit(solution)/shard_map/ppermute | solution.py:360
  113.5 4.5 %collective-permute-done.11.refs_5_ = bf16[3,32,1024]{2,1,0:T(8,128)(2,1)S(1)} collective-permute-done((bf16[3,32,1024]{2,1,0:T(8,128)(2,1)}, bf16[3,32,1024]{2,1,0:T(8,128)(2,1)S(1)}, u32[]{:S(2)}, u32[]{:S(2)}) %collective-permute-start.11) | collective-permute-done | bytes 196640 | tf_op jit(solution)/shard_map/ppermute | solution.py:360
  118.1 0.0 collective-permute-done.12.refs_6_
  118.1 3.9 %collective-permute-done.13.refs_7_ = bf16[3,32,1024]{2,1,0:T(8,128)(2,1)S(1)} collective-permute-done((bf16[3,32,1024]{2,1,0:T(8,128)(2,1)}, bf16[3,32,1024]{2,1,0:T(8,128)(2,1)S(1)}, u32[]{:S(2)}, u32[]{:S(2)}) %collective-permute-start.13) | collective-permute-done | bytes 196640 | tf_op jit(solution)/shard_map/ppermute | solution.py:360
  122.0 0.0 copy-done.11
  122.0 0.0 copy-done.12
  122.0 0.0 copy-done.13
  122.0 0.0 copy-done.14
  122.0 0.6 copy-done.15
  122.7 3.5 %shard_map.203 = (bf16[2,32,8192]{2,1,0:T(8,128)(2,1)}, bf16[1,32,8192]{2,1,0:T(8,128)(2,1)}) custom-call(s32[1]{0:T(128)} %bitcast.me, bf16[3,32,1024]{2,1,0:T(8,128)(2,1)} %get-tuple-element.59.refs_0_, bf16[3,32,1024]{2,1,0:T(8,128)(2,1)} %copy-done.9, bf16[3,32,1024]{2,1,0:T(8,128)(2,1)} %copy-done.10, bf16[3,32,1024]{2,1,0:T(8,128)(2,1)} %copy-done.11, ...), custom_call_target="tpu_custom_call" | custom-call | flops 1000000000 | bytes 4000000 | tf_op jit(solution)/shard_map/pallas_call | solution.py:346
  126.1 0.0 all-to-all-done.2
  126.1 0.0 copy-start.1
  126.1 0.9 copy-done.1
  127.0 8.3 %shard_map.201 = (bf16[2,256,1024]{2,1,0:T(8,128)(2,1)}, bf16[2,256,128]{2,1,0:T(8,128)(2,1)}, f32[2,16,256]{2,1,0:T(8,128)}, bf16[1,256,1024]{2,1,0:T(8,128)(2,...) custom-call(s32[1]{0:T(128)S(6)} %copy.22.length, bf16[256,2048]{1,0:T(8,128)(2,1)} %bitcast.15, ...), custom_call_target="tpu_custom_call" | custom-call | flops 1000000000 | bytes 4000000 | tf_op jit(solution)/shard_map/pallas_call | solution.py:346
  (10 shorter events, 0.0 us)
Async XLA Ops:
  6.0 38.3 %all-to-all-start = ((bf16[16,16,2048]{2,1,0:T(8,128)(2,1)}), bf16[16,16,2048]{2,1,0:T(8,128)(2,1)S(1)}, u32[]{:S(2)}, u32[]{:S(2)}) async-start(bf16[16,16,2048]{2,1,0:T(8,128)(2,1)} %bitcast.19), calls=%async_computation | async-start | bytes 2097152 | tf_op jit(solution)/shard_map/all_to_all | solution.py:365
  17.5 6.0 %collective-permute-start = (bf16[3,32,1024]{2,1,0:T(8,128)(2,1)}, bf16[3,32,1024]{2,1,0:T(8,128)(2,1)S(1)}, u32[]{:S(2)}, u32[]{:S(2)}) collective-permute-start(bf16[3,32,1024]{2,1,0:T(8,128)(2,1)} %get-tuple-element.44), channel_id=1, source_target_pairs={{0,1},{1,0},{2,3},{3,2},{4,5},{5,4},{6,7},{7,6},{8,9},{9,8},{10,11... | collective-permute-start | bytes 589832 | tf_op jit(solution)/shard_map/ppermute | solution.py:360
  18.6 7.5 %collective-permute-start.1 = (bf16[3,32,1024]{2,1,0:T(8,128)(2,1)}, bf16[3,32,1024]{2,1,0:T(8,128)(2,1)S(1)}, u32[]{:S(2)}, u32[]{:S(2)}) collective-permute-start(bf16[3,32,1024]{2,1,0:T(8,128)(2,1)} %get-tuple-element.45), channel_id=1, source_target_pairs={{0,2},{1,3},{2,0},{3,1},{4,6},{5,7},{6,4},{7,5},{8,10},{9,11},{10,... | collective-permute-start | bytes 589832 | tf_op jit(solution)/shard_map/ppermute | solution.py:360
  19.8 10.7 %collective-permute-start.2 = (bf16[3,32,1024]{2,1,0:T(8,128)(2,1)}, bf16[3,32,1024]{2,1,0:T(8,128)(2,1)S(1)}, u32[]{:S(2)}, u32[]{:S(2)}) collective-permute-start(bf16[3,32,1024]{2,1,0:T(8,128)(2,1)} %get-tuple-element.46), channel_id=1, source_target_pairs={{0,3},{1,2},{2,1},{3,0},{4,7},{5,6},{6,5},{7,4},{8,11},{9,10},{10,... | collective-permute-start | bytes 589832 | tf_op jit(solution)/shard_map/ppermute | solution.py:360
  20.3 15.5 %collective-permute-start.3 = (bf16[3,32,1024]{2,1,0:T(8,128)(2,1)}, bf16[3,32,1024]{2,1,0:T(8,128)(2,1)S(1)}, u32[]{:S(2)}, u32[]{:S(2)}) collective-permute-start(bf16[3,32,1024]{2,1,0:T(8,128)(2,1)} %get-tuple-element.47), channel_id=1, source_target_pairs={{0,4},{1,5},{2,6},{3,7},{4,0},{5,1},{6,2},{7,3},{8,12},{9,13},{10,... | collective-permute-start | bytes 589832 | tf_op jit(solution)/shard_map/ppermute | solution.py:360
  23.0 17.3 %collective-permute-start.4 = (bf16[3,32,1024]{2,1,0:T(8,128)(2,1)}, bf16[3,32,1024]{2,1,0:T(8,128)(2,1)S(1)}, u32[]{:S(2)}, u32[]{:S(2)}) collective-permute-start(bf16[3,32,1024]{2,1,0:T(8,128)(2,1)} %get-tuple-element.48), channel_id=1, source_target_pairs={{0,5},{1,4},{2,7},{3,6},{4,1},{5,0},{6,3},{7,2},{8,13},{9,12},{10,... | collective-permute-start | bytes 589832 | tf_op jit(solution)/shard_map/ppermute | solution.py:360
  23.6 20.7 %copy-start.2 = (bf16[3,32,1024]{2,1,0:T(8,128)(2,1)}, bf16[3,32,1024]{2,1,0:T(8,128)(2,1)S(1)}, u32[]{:S(2)}) copy-start(bf16[3,32,1024]{2,1,0:T(8,128)(2,1)S(1)} %collective-permute-done.refs_1_) | copy-start | bytes 589828
  23.6 16.8 %collective-permute-start.5 = (bf16[3,32,1024]{2,1,0:T(8,128)(2,1)}, bf16[3,32,1024]{2,1,0:T(8,128)(2,1)S(1)}, u32[]{:S(2)}, u32[]{:S(2)}) collective-permute-start(bf16[3,32,1024]{2,1,0:T(8,128)(2,1)} %get-tuple-element.49), channel_id=1, source_target_pairs={{0,6},{1,7},{2,4},{3,5},{4,2},{5,3},{6,0},{7,1},{8,14},{9,15},{10,... | collective-permute-start | bytes 589832 | tf_op jit(solution)/shard_map/ppermute | solution.py:360
  26.0 18.2 %copy-start.3 = (bf16[3,32,1024]{2,1,0:T(8,128)(2,1)}, bf16[3,32,1024]{2,1,0:T(8,128)(2,1)S(1)}, u32[]{:S(2)}) copy-start(bf16[3,32,1024]{2,1,0:T(8,128)(2,1)S(1)} %collective-permute-done.1.refs_2_) | copy-start | bytes 589828
  26.1 18.2 %collective-permute-start.6 = (bf16[3,32,1024]{2,1,0:T(8,128)(2,1)}, bf16[3,32,1024]{2,1,0:T(8,128)(2,1)S(1)}, u32[]{:S(2)}, u32[]{:S(2)}) collective-permute-start(bf16[3,32,1024]{2,1,0:T(8,128)(2,1)} %get-tuple-element.50), channel_id=1, source_target_pairs={{0,7},{1,6},{2,5},{3,4},{4,3},{5,2},{6,1},{7,0},{8,15},{9,14},{10,... | collective-permute-start | bytes 589832 | tf_op jit(solution)/shard_map/ppermute | solution.py:360
  30.5 13.8 %copy-start.4 = (bf16[3,32,1024]{2,1,0:T(8,128)(2,1)}, bf16[3,32,1024]{2,1,0:T(8,128)(2,1)S(1)}, u32[]{:S(2)}) copy-start(bf16[3,32,1024]{2,1,0:T(8,128)(2,1)S(1)} %collective-permute-done.2.refs_3_) | copy-start | bytes 589828
  35.8 8.5 %copy-start.5 = (bf16[3,32,1024]{2,1,0:T(8,128)(2,1)}, bf16[3,32,1024]{2,1,0:T(8,128)(2,1)S(1)}, u32[]{:S(2)}) copy-start(bf16[3,32,1024]{2,1,0:T(8,128)(2,1)S(1)} %collective-permute-done.3.refs_4_) | copy-start | bytes 589828
  40.3 4.0 %copy-start.6 = (bf16[3,32,1024]{2,1,0:T(8,128)(2,1)}, bf16[3,32,1024]{2,1,0:T(8,128)(2,1)S(1)}, u32[]{:S(2)}) copy-start(bf16[3,32,1024]{2,1,0:T(8,128)(2,1)S(1)} %collective-permute-done.4.refs_5_) | copy-start | bytes 589828
  40.3 4.0 %copy-start.7 = (bf16[3,32,1024]{2,1,0:T(8,128)(2,1)}, bf16[3,32,1024]{2,1,0:T(8,128)(2,1)S(1)}, u32[]{:S(2)}) copy-start(bf16[3,32,1024]{2,1,0:T(8,128)(2,1)S(1)} %collective-permute-done.5.refs_6_) | copy-start | bytes 589828
  44.3 0.7 copy-start.8
  44.3 1.0 copy-start
  75.6 50.5 %all-to-all-start.2 = ((bf16[16,16,1536]{2,1,0:T(8,128)(2,1)}), bf16[16,16,1536]{2,1,0:T(8,128)(2,1)S(1)}, u32[]{:S(2)}, u32[]{:S(2)}) async-start(bf16[16,16,1536]{2,1,0:T(8,128)(2,1)} %bitcast.18), calls=%async_computation.2 | async-start | bytes 1572864 | tf_op jit(solution)/shard_map/all_to_all | solution.py:365
  94.6 6.6 %collective-permute-start.7 = (bf16[3,32,1024]{2,1,0:T(8,128)(2,1)}, bf16[3,32,1024]{2,1,0:T(8,128)(2,1)S(1)}, u32[]{:S(2)}, u32[]{:S(2)}) collective-permute-start(bf16[3,32,1024]{2,1,0:T(8,128)(2,1)} %get-tuple-element.60), channel_id=1, source_target_pairs={{0,1},{1,0},{2,3},{3,2},{4,5},{5,4},{6,7},{7,6},{8,9},{9,8},{10,11... | collective-permute-start | bytes 589832 | tf_op jit(solution)/shard_map/ppermute | solution.py:360
  96.3 7.5 %collective-permute-start.8 = (bf16[3,32,1024]{2,1,0:T(8,128)(2,1)}, bf16[3,32,1024]{2,1,0:T(8,128)(2,1)S(1)}, u32[]{:S(2)}, u32[]{:S(2)}) collective-permute-start(bf16[3,32,1024]{2,1,0:T(8,128)(2,1)} %get-tuple-element.61), channel_id=1, source_target_pairs={{0,2},{1,3},{2,0},{3,1},{4,6},{5,7},{6,4},{7,5},{8,10},{9,11},{10,... | collective-permute-start | bytes 589832 | tf_op jit(solution)/shard_map/ppermute | solution.py:360
  96.3 15.2 %collective-permute-start.9 = (bf16[3,32,1024]{2,1,0:T(8,128)(2,1)}, bf16[3,32,1024]{2,1,0:T(8,128)(2,1)S(1)}, u32[]{:S(2)}, u32[]{:S(2)}) collective-permute-start(bf16[3,32,1024]{2,1,0:T(8,128)(2,1)} %get-tuple-element.62), channel_id=1, source_target_pairs={{0,3},{1,2},{2,1},{3,0},{4,7},{5,6},{6,5},{7,4},{8,11},{9,10},{10,... | collective-permute-start | bytes 589832 | tf_op jit(solution)/shard_map/ppermute | solution.py:360
  98.0 15.5 %collective-permute-start.10 = (bf16[3,32,1024]{2,1,0:T(8,128)(2,1)}, bf16[3,32,1024]{2,1,0:T(8,128)(2,1)S(1)}, u32[]{:S(2)}, u32[]{:S(2)}) collective-permute-start(bf16[3,32,1024]{2,1,0:T(8,128)(2,1)} %get-tuple-element.63), channel_id=1, source_target_pairs={{0,4},{1,5},{2,6},{3,7},{4,0},{5,1},{6,2},{7,3},{8,12},{9,13},{10,... | collective-permute-start | bytes 589832 | tf_op jit(solution)/shard_map/ppermute | solution.py:360
  100.0 18.0 %collective-permute-start.11 = (bf16[3,32,1024]{2,1,0:T(8,128)(2,1)}, bf16[3,32,1024]{2,1,0:T(8,128)(2,1)S(1)}, u32[]{:S(2)}, u32[]{:S(2)}) collective-permute-start(bf16[3,32,1024]{2,1,0:T(8,128)(2,1)} %get-tuple-element.64), channel_id=1, source_target_pairs={{0,5},{1,4},{2,7},{3,6},{4,1},{5,0},{6,3},{7,2},{8,13},{9,12},{10,... | collective-permute-start | bytes 589832 | tf_op jit(solution)/shard_map/ppermute | solution.py:360
  101.3 10.1 %copy-start.9 = (bf16[3,32,1024]{2,1,0:T(8,128)(2,1)}, bf16[3,32,1024]{2,1,0:T(8,128)(2,1)S(1)}, u32[]{:S(2)}) copy-start(bf16[3,32,1024]{2,1,0:T(8,128)(2,1)S(1)} %collective-permute-done.7.refs_1_) | copy-start | bytes 589828
  101.3 16.8 %collective-permute-start.12 = (bf16[3,32,1024]{2,1,0:T(8,128)(2,1)}, bf16[3,32,1024]{2,1,0:T(8,128)(2,1)S(1)}, u32[]{:S(2)}, u32[]{:S(2)}) collective-permute-start(bf16[3,32,1024]{2,1,0:T(8,128)(2,1)} %get-tuple-element.65), channel_id=1, source_target_pairs={{0,6},{1,7},{2,4},{3,5},{4,2},{5,3},{6,0},{7,1},{8,14},{9,15},{10,... | collective-permute-start | bytes 589832 | tf_op jit(solution)/shard_map/ppermute | solution.py:360
  103.8 7.7 %copy-start.10 = (bf16[3,32,1024]{2,1,0:T(8,128)(2,1)}, bf16[3,32,1024]{2,1,0:T(8,128)(2,1)S(1)}, u32[]{:S(2)}) copy-start(bf16[3,32,1024]{2,1,0:T(8,128)(2,1)S(1)} %collective-permute-done.8.refs_2_) | copy-start | bytes 589828
  103.8 18.2 %collective-permute-start.13 = (bf16[3,32,1024]{2,1,0:T(8,128)(2,1)}, bf16[3,32,1024]{2,1,0:T(8,128)(2,1)S(1)}, u32[]{:S(2)}, u32[]{:S(2)}) collective-permute-start(bf16[3,32,1024]{2,1,0:T(8,128)(2,1)} %get-tuple-element.66), channel_id=1, source_target_pairs={{0,7},{1,6},{2,5},{3,4},{4,3},{5,2},{6,1},{7,0},{8,15},{9,14},{10,... | collective-permute-start | bytes 589832 | tf_op jit(solution)/shard_map/ppermute | solution.py:360
  111.5 10.5 %copy-start.11 = (bf16[3,32,1024]{2,1,0:T(8,128)(2,1)}, bf16[3,32,1024]{2,1,0:T(8,128)(2,1)S(1)}, u32[]{:S(2)}) copy-start(bf16[3,32,1024]{2,1,0:T(8,128)(2,1)S(1)} %collective-permute-done.9.refs_3_) | copy-start | bytes 589828
  113.5 8.5 %copy-start.12 = (bf16[3,32,1024]{2,1,0:T(8,128)(2,1)}, bf16[3,32,1024]{2,1,0:T(8,128)(2,1)S(1)}, u32[]{:S(2)}) copy-start(bf16[3,32,1024]{2,1,0:T(8,128)(2,1)S(1)} %collective-permute-done.10.refs_4_) | copy-start | bytes 589828
  118.1 3.9 %copy-start.13 = (bf16[3,32,1024]{2,1,0:T(8,128)(2,1)}, bf16[3,32,1024]{2,1,0:T(8,128)(2,1)S(1)}, u32[]{:S(2)}) copy-start(bf16[3,32,1024]{2,1,0:T(8,128)(2,1)S(1)} %collective-permute-done.11.refs_5_) | copy-start | bytes 589828
  118.1 3.9 %copy-start.14 = (bf16[3,32,1024]{2,1,0:T(8,128)(2,1)}, bf16[3,32,1024]{2,1,0:T(8,128)(2,1)S(1)}, u32[]{:S(2)}) copy-start(bf16[3,32,1024]{2,1,0:T(8,128)(2,1)S(1)} %collective-permute-done.12.refs_6_) | copy-start | bytes 589828
  122.0 0.7 copy-start.15
  126.1 0.9 copy-start.1
where the time goes:
time: 136 us; the launch traced here: 135 us
  Pallas kernels  46.2 us (34%)
  starting transfers between devices  35.7 us (26%)
  waiting for transfers between devices  25.8 us (19%)
  blocking collectives  23.6 us (17%)
  local copies, waits for them, and re-layouts  2.53 us (2%)
  between operations  1.61 us (1%)
    pallas_call x9, Pallas kernels, call(): pl.pallas_call(kernel, grid=(steps,), in_specs=ins, out_specs=[spec for s...  46.2 us
    ppermute x14, waiting for transfers between devices, exchange(): lax.ppermute(chunks[k], 'head', [(i, i ^ k) for i in range(GROUP)])  25.8 us
    all_to_all x1, blocking collectives, transposed(): lax.all_to_all(message, 'seq', split_axis=0, concat_axis=0, tiled=True)  23.6 us
    ppermute x14, starting transfers between devices, exchange(): lax.ppermute(chunks[k], 'head', [(i, i ^ k) for i in range(GROUP)])  23.5 us
    all_to_all x2, starting transfers between devices, transposed(): lax.all_to_all(message, 'seq', split_axis=0, concat_axis=0, tiled=True)  12.2 us
  transfers between devices with their start and end apart: 16, of which 7 were waited for; matrix products, arithmetic and copies ran while one was open for 0% of the time, Pallas kernels for 20%

commit v1 on v0

--- a/solution.py
+++ b/solution.py
@@ -102,7 +102,7 @@
 def scattered(out, state, first):
     for d in range(SHARDS):
         rows, lanes = piece(d)
-        out[16 * d : 16 * d + 16, first : first + HALF] = state[rows, lanes].astype(BF16)
+        out[16 * d : 16 * d + 16, pl.ds(first, HALF)] = state[rows, lanes].astype(BF16)
 
 
 def gathered(m, place):
@@ -119,82 +119,114 @@
 
 def reach_kernel(length, pr, pd, pc, ar, ad, ac, out, factors):
     b = pl.program_id(0)
-
-    @pl.when(b < 3)
-    def _():
-        answer = b == 2
-        read = jnp.where(answer, ar[0], pr[0])
-        decay = jnp.where(answer, ad[0], pd[0])
-        alive = jnp.where(answer, length[0], B)
-        cot = live_rows(jnp.where(answer, ac[0], pc[0]).astype(F32), alive)
-        growth = grown(decay)
-        scattered(out, tn(read, (cot * growth).astype(BF16)), 0)
-        last = growth[B - 1 : B, :]
-        high = last.astype(BF16).astype(F32)
-        row = iota((16, L), 0) - 2 * b
-        part = jnp.where(row == 0, high, jnp.where(row == 1, last - high, 0.0))
-        factors[...] = jnp.where(b == 0, part, jnp.where(answer, factors[...], factors[...] + part))
-
-    @pl.when(b == 3)
-    def _():
-        for d in range(SHARDS):
-            out[16 * d : 16 * d + 16, :] = factors[:, piece(d)[1]].astype(BF16)
-
-
-def split_kernel(me, pt, at, *outs):
-    b = pl.program_id(0)
+    answer = b == 2
+    read = jnp.where(answer, ar[0], pr[0])
+    decay = jnp.where(answer, ad[0], pd[0])
+    alive = jnp.where(answer, length[0], B)
+    cot = live_rows(jnp.where(answer, ac[0], pc[0]).astype(F32), alive)
+    growth = grown(decay)
+    scattered(out, tn(read, (cot * growth).astype(BF16)), pl.multiple_of(b * HALF, HALF))
+    last = growth[B - 1 : B, :]
+    high = last.astype(BF16).astype(F32)
+
+    @pl.when(b < 2)
+    def _():
+        factors[pl.ds(2 * b, 1), :] = high
+        factors[pl.ds(2 * b + 1, 1), :] = last - high
+
+    @pl.when(answer)
+    def _():
+        for half in range(2):
+            lanes = [slice(HALF * half + N * j, HALF * half + N * j + N) for j in range(4)]
+            part = jnp.concatenate([factors[i : i + 1, lane] for i in range(4) for lane in lanes], axis=0)
+            for d in range(half, SHARDS, 2):
+                out[16 * d : 16 * d + 16, 3 * HALF :] = part.astype(BF16)
+
+
+def split_kernel(me, pt, at, *refs):
+    outs, (stage, came, went) = refs[:GROUP], refs[GROUP:]
+    coming, going = [], []
+    for k in (4, 5, 2, 3, 6, 7, 1, 0):
+        there = pl.multiple_of((me[0] ^ k) * L, L)
+        coming.append(
+            (
+                pltpu.make_async_copy(pt.at[:, :, pl.ds(there, L)], stage.at[k, 0:2], came.at[2 * k]),
+                pltpu.make_async_copy(at.at[:, :, pl.ds(there, L)], stage.at[k, 2:3], came.at[2 * k + 1]),
+            )
+        )
+        going.append(pltpu.make_async_copy(stage.at[k], outs[k], went.at[k]))
+    for first, second in coming:
+        first.start()
+        second.start()
+    for (first, second), third in zip(coming, going):
+        first.wait()
+        second.wait()
+        third.start()
+    for copy in going:
+        copy.wait()
+
+
+def join_kernel(me, *refs):
+    ins, (pt, at, stage, came, went) = refs[:GROUP], refs[GROUP:]
+    coming, going = [], []
     for k in range(GROUP):
         there = pl.multiple_of((me[0] ^ k) * L, L)
-        outs[k][0] = jnp.where(b == 2, at[0, :, pl.ds(there, L)], pt[0, :, pl.ds(there, L)])
-
-
-def join_kernel(me, *refs):
-    b = pl.program_id(0)
-    ins, (pt, at) = refs[:GROUP], refs[GROUP:]
-    for k in range(GROUP):
-        there = pl.multiple_of((me[0] ^ k) * L, L)
-
-        @pl.when(b < 2)
-        def _():
-            pt[0, :, pl.ds(there, L)] = ins[k][0]
-
-        @pl.when(b == 2)
-        def _():
-            at[0, :, pl.ds(there, L)] = ins[k][0]
-
-
-def shard_factor(factors, k, q):
-    part = factors[16 * k : 16 * k + 16, :].astype(F32)
-    row = iota((16, HALF), 0) - 2 * q
-    return jnp.sum(jnp.where((row == 0) | (row == 1), part, 0.0), axis=0, keepdims=True)
+        coming.append(pltpu.make_async_copy(ins[k], stage.at[k], came.at[k]))
+        going.append(
+            (
+                pltpu.make_async_copy(stage.at[k, 0:2], pt.at[:, :, pl.ds(there, L)], went.at[2 * k]),
+                pltpu.make_async_copy(stage.at[k, 2:3], at.at[:, :, pl.ds(there, L)], went.at[2 * k + 1]),
+            )
+        )
+    for copy in coming:
+        copy.start()
+    for first, (second, third) in zip(coming, going):
+        first.wait()
+        second.start()
+        third.start()
+    for second, third in going:
+        second.wait()
+        third.wait()
+
+
+def shard_factor(packed, k, q):
+    part = packed[16 * k : 16 * k + 16, :].astype(F32)
+    rows = [part[8 * q + j : 8 * q + j + 1] + part[8 * q + 4 + j : 8 * q + 5 + j] for j in range(4)]
+    return jnp.concatenate(rows, axis=1)
 
 
 def owner_of(sizes, k):
     return (sizes[0] <= k).astype(jnp.int32) + (sizes[0] + sizes[1] <= k).astype(jnp.int32)
 
 
-def close_kernel(me, sizes, reach, answers, factors, pw, pd, *refs):
-    q = pl.program_id(0)
+def local_kernel(me, message, pw, pd, *refs):
     chunks, (out, x) = refs[:GROUP], refs[GROUP:]
     assembled(me, chunks, x)
     weighted = (x[...].astype(F32) * closing_weight(pd[0])).astype(BF16)
-    scattered(out, tn(pw[0], weighted), HALF)
-    grad = jnp.zeros((16, HALF), F32)
-    for k in range(SHARDS):
-        part = answers[16 * k : 16 * k + 16, :].astype(F32)
-        grad = grad + part * (owner_of(sizes, k) == q).astype(F32)
-    for k in reversed(range(SHARDS)):
-        out[16 * k : 16 * k + 16, :HALF] = grad.astype(BF16)
-        grad = reach[16 * k : 16 * k + 16, :].astype(F32) + shard_factor(factors, k, q) * grad
-
-
-def start_kernel(sizes, factors, first, second, out):
+    scattered(out, tn(pw[0], weighted), 0)
+
+
+def turn_kernel(sizes, reach, answers, packed, out, factors):
+    for q in range(2):
+        grad = jnp.zeros((16, HALF), F32)
+        for k in range(SHARDS):
+            part = answers[16 * k : 16 * k + 16, :].astype(F32)
+            grad = grad + part * (owner_of(sizes, k) == q).astype(F32)
+        for k in reversed(range(SHARDS)):
+            out[16 * k : 16 * k + 16, q * HALF : (q + 1) * HALF] = grad.astype(BF16)
+            factor = shard_factor(packed, k, q)
+            factors[16 * q + k : 16 * q + k + 1, :] = factor
+            grad = reach[16 * k : 16 * k + 16, q * HALF : (q + 1) * HALF].astype(F32) + factor * grad
+
+
+def start_kernel(sizes, factors, m2, out):
     ends = []
-    for q, local in enumerate((first, second)):
+    for q in range(2):
         state = jnp.zeros((16, HALF), F32)
         for k in range(SHARDS):
             out[16 * k : 16 * k + 16, q * HALF : (q + 1) * HALF] = state.astype(BF16)
-            state = shard_factor(factors, k, q) * state + local[16 * k : 16 * k + 16, :].astype(F32)
+            local = m2[16 * k : 16 * k + 16, (2 + q) * HALF : (3 + q) * HALF].astype(F32)
+            state = factors[16 * q + k : 16 * q + k + 1, :] * state + local
         ends.append(state)
     for k in range(SHARDS):
         owner = owner_of(sizes, k)
@@ -252,14 +284,23 @@
         adw[0] = dw.astype(BF16)
 
 
-def token_kernel(me, m2, pw, pd, dxi, *refs):
-    outs, (ends, full) = refs[:GROUP], refs[GROUP:]
+def token_kernel(me, m2, pw, pd, dxi, dwi, *refs):
+    chunks, outs = refs[:GROUP], refs[GROUP : 2 * GROUP]
+    pdw, z, closing, ends, full, x = refs[2 * GROUP :]
     b = pl.program_id(0)
 
     @pl.when(b < 2)
     def _():
         gathered(m2, ends)
-        full[...] = (dxi[0].astype(F32) + nn(pw[0], ends[...]) * closing_weight(pd[0])).astype(BF16)
+        assembled(me, chunks, x)
+        xs = x[...].astype(F32)
+        to_close = closing_weight(pd[0])
+        tail = nn(pw[0], ends[...]) * to_close
+        full[...] = (dxi[0].astype(F32) + tail).astype(BF16)
+        pdw[0] = (dwi[0] + nt((xs * to_close).astype(BF16), ends[...])).astype(BF16)
+        tail = tail * xs
+        closing[0] = jnp.broadcast_to(jnp.sum(tail, axis=0, keepdims=True), (8, L))
+        z[0] = head_sums(tail)
 
     @pl.when(b == 2)
     def _():
@@ -268,19 +309,6 @@
     for k in range(GROUP):
         there = pl.multiple_of((me[0] ^ k) * ROWS, ROWS)
         outs[k][0] = full[pl.ds(there, ROWS), :]
-
-
-def write_kernel(me, m2, pw, pd, dwi, *refs):
-    chunks, (pdw, z, closing, x, ends) = refs[:GROUP], refs[GROUP:]
-    assembled(me, chunks, x)
-    gathered(m2, ends)
-    xs = x[...].astype(F32)
-    to_close = closing_weight(pd[0])
-    weighted = (xs * to_close).astype(BF16)
-    pdw[0] = (dwi[0] + nt(weighted, ends[...])).astype(BF16)
-    tail = xs * (nn(pw[0], ends[...]) * to_close)
-    closing[0] = jnp.broadcast_to(jnp.sum(tail, axis=0, keepdims=True), (8, L))
-    z[0] = head_sums(tail)
 
 
 def output_kernel(
@@ -320,6 +348,8 @@
 
 
 SMEM = pl.BlockSpec(memory_space=pltpu.SMEM)
+VMEM = pl.BlockSpec(memory_space=pltpu.VMEM)
+ANY = pl.BlockSpec(memory_space=pl.ANY)
 
 
 def own(*dims):
@@ -342,7 +372,7 @@
     return jax.ShapeDtypeStruct(dims, dtype)
 
 
-def call(kernel, steps, ins, outs, args, scratch=(), flops=1e9):
+def call(kernel, steps, ins, outs, args, scratch=(), flops=1e9, alias=None, limit=None):
     return pl.pallas_call(
         kernel,
         grid=(steps,),
@@ -350,15 +380,18 @@
         out_specs=[spec for spec, _ in outs],
         out_shape=[struct for _, struct in outs],
         scratch_shapes=scratch,
+        input_output_aliases=alias or {},
+        compiler_params=pltpu.CompilerParams(vmem_limit_bytes=limit) if limit else None,
         cost_estimate=pl.CostEstimate(flops=int(flops), bytes_accessed=4000000, transcendentals=0),
     )(*args)
 
 
 def exchange(chunks):
-    sent = [chunks[0]]
-    for k in range(1, GROUP):
-        sent.append(lax.ppermute(chunks[k], "head", [(i, i ^ k) for i in range(GROUP)]))
-    return sent
+    sent = {0: chunks[0]}
+    for offsets in ((4, 5), (2, 3, 6, 7), (1,)):
+        for k in offsets:
+            sent[k] = lax.ppermute(chunks[k], "head", [(i, i ^ k) for i in range(GROUP)])
+    return [sent[k] for k in range(GROUP)]
 
 
 def transposed(message):
@@ -375,31 +408,44 @@
     answer_side = [one(B, N), one(H, B), one(B, L)]
     (m1,) = call(
         reach_kernel,
-        4,
+        3,
         [SMEM, *prompt_side, *answer_side],
-        [(column(HALF, lambda b: b), shape((B, 4 * HALF)))],
+        [(column(3 * HALF + N, lambda b: 0), shape((B, 3 * HALF + N)))],
         (length, pr, pd, pc, ar, ad, ac),
-        (pltpu.VMEM((16, L), F32),),
+        (pltpu.VMEM((8, L), F32),),
     )
     m1 = transposed(m1)
-    cut = call(split_kernel, 3, [SMEM, own(ROWS, GROUP * L), one(ROWS, GROUP * L)], chunk, (me, pt, at))
+    cut = call(
+        split_kernel,
+        1,
+        [SMEM, ANY, ANY],
+        [(ANY, shape((3, ROWS, L)))] * GROUP,
+        (me, pt, at),
+        (
+            pltpu.VMEM((GROUP, 3, ROWS, L), BF16),
+            pltpu.SemaphoreType.DMA((2 * GROUP,)),
+            pltpu.SemaphoreType.DMA((GROUP,)),
+        ),
+    )
     cut = exchange(cut)
+    m2, factors = call(
+        turn_kernel,
+        1,
+        [SMEM, column(2 * HALF, lambda q: 0), column(HALF, lambda q: 2), column(N, lambda q: 12)],
+        [
+            (column(2 * HALF, lambda q: 0), shape((B, 4 * HALF))),
+            (pl.BlockSpec((2 * SHARDS, HALF), lambda q: (0, 0)), shape((2 * SHARDS, HALF), F32)),
+        ],
+        (sizes, m1, m1, m1),
+    )
     (m2,) = call(
-        close_kernel,
+        local_kernel,
         2,
-        [
-            SMEM,
-            SMEM,
-            column(HALF, lambda q: q),
-            column(HALF, lambda q: 2),
-            column(HALF, lambda q: 3),
-            each(B, N),
-            each(H, B),
-            *pieces,
-        ],
-        [(column(2 * HALF, lambda q: q), shape((B, 4 * HALF)))],
-        (me, sizes, m1, m1, m1, pw, pd, *cut),
+        [SMEM, ANY, each(B, N), each(H, B), *pieces],
+        [(column(HALF, lambda q: 2 + q), shape((B, 4 * HALF)))],
+        (me, m2, pw, pd, *cut),
         (block,),
+        alias={1: 0},
     )
     m2 = transposed(m2)
     yi, dxi, dri, dwi, adw, zi = call(
@@ -421,38 +467,41 @@
     (m3,) = call(
         start_kernel,
         1,
-        [SMEM, column(HALF, lambda b: 3), column(HALF, lambda b: 1), column(HALF, lambda b: 3)],
-        [(column(3 * HALF, lambda b: 0), shape((B, 3 * HALF)))],
-        (sizes, m1, m2, m2),
+        [SMEM, VMEM, VMEM],
+        [(VMEM, shape((B, 3 * HALF)))],
+        (sizes, factors, m2),
+        limit=4 << 20,
     )
     m3 = transposed(m3)
-    back = call(
+    made = call(
         token_kernel,
         3,
-        [SMEM, column(HALF, lambda b: 2 * jnp.minimum(b, 1)), own(B, N), own(H, B), each(B, L)],
-        chunk,
-        (me, m2, pw, pd, dxi),
-        (state, block),
-    )
-    back = exchange(back)
-    pdw, z, closing = call(
-        write_kernel,
-        2,
-        [SMEM, column(HALF, lambda q: 2 * q), each(B, N), each(H, B), each(B, N), *pieces],
         [
-            (each(B, N), shape((2, B, N))),
-            (each(B, H), shape((2, B, H), F32)),
-            (each(8, L), shape((2, 8, L), F32)),
+            SMEM,
+            column(HALF, lambda b: jnp.minimum(b, 1)),
+            own(B, N),
+            own(H, B),
+            each(B, L),
+            own(B, N),
+            *[own(ROWS, L)] * GROUP,
         ],
-        (me, m2, pw, pd, dwi, *cut),
-        (block, state),
-    )
+        [
+            *chunk,
+            (own(B, N), shape((2, B, N))),
+            (own(B, H), shape((2, B, H), F32)),
+            (own(8, L), shape((2, 8, L), F32)),
+        ],
+        (me, m2, pw, pd, dxi, dwi, *cut),
+        (state, block, block),
+    )
+    pdw, z, closing = made[GROUP:]
+    back = exchange(made[:GROUP])
     py, pdr, pdd, ay, adr, add = call(
         output_kernel,
         3,
         [
             SMEM,
-            column(HALF, lambda b: 2 * jnp.minimum(b, 1)),
+            column(HALF, lambda b: jnp.minimum(b, 1)),
             column(HALF, lambda b: b),
             *prompt_side,
             *answer_side,
@@ -475,13 +524,15 @@
     )
     pdx, adx = call(
         join_kernel,
-        3,
-        [SMEM, *pieces],
-        [
-            (own(ROWS, GROUP * L), shape((2, ROWS, GROUP * L))),
-            (one(ROWS, GROUP * L), shape((1, ROWS, GROUP * L))),
-        ],
+        1,
+        [SMEM] + [ANY] * GROUP,
+        [(ANY, shape((2, ROWS, GROUP * L))), (ANY, shape((1, ROWS, GROUP * L)))],
         (me, *back),
+        (
+            pltpu.VMEM((GROUP, 3, ROWS, L), BF16),
+            pltpu.SemaphoreType.DMA((GROUP,)),
+            pltpu.SemaphoreType.DMA((2 * GROUP,)),
+        ),
     )
     return py, pdx, pdw, pdr, pdd, ay, adx, adw, adr, add
 

time: 136 us -> 128 us (0.941)
  Pallas kernels: 46.2 us -> 41.9 us
  starting transfers between devices: 35.7 us -> 33.5 us
  waiting for transfers between devices: 25.8 us -> 23.6 us
    pallas_call x9, Pallas kernels: 46.2 us -> 41.9 us  [call(): pl.pallas_call(kernel, grid=(steps,), in_specs=ins, out_specs=[spec for s...]
    ppermute x14, waiting for transfers between devices: 25.8 us -> 23.5 us  [exchange(): lax.ppermute(chunks[k], 'head', [(i, i ^ k) for i in range(GROUP)])]
    ppermute x14, starting transfers between devices: 23.5 us -> 21.3 us  [exchange(): lax.ppermute(chunks[k], 'head', [(i, i ^ k) for i in range(GROUP)])]
    unnamed x32 -> x38, local copies, waits for them, and re-layouts: 2.53 us -> 3.24 us
  transfers between devices with their start and end apart: 16 -> 16, of which waited for: 7 -> 8; matrix products, arithmetic and copies ran while one was open for 0% -> 0% of each run, Pallas kernels for 20% -> 18%
where the time goes in v1:
time: 128 us; the launch traced here: 127 us
  Pallas kernels  41.9 us (33%)
  starting transfers between devices  33.5 us (26%)
  blocking collectives  23.7 us (19%)
  waiting for transfers between devices  23.6 us (18%)
  local copies, waits for them, and re-layouts  3.24 us (3%)
  between operations  1.44 us (1%)
    pallas_call x9, Pallas kernels, call(): pl.pallas_call(kernel, grid=(steps,), in_specs=ins, out_specs=[spec for s...  41.9 us
    all_to_all x1, blocking collectives, transposed(): lax.all_to_all(message, 'seq', split_axis=0, concat_axis=0, tiled=True)  23.7 us
    ppermute x14, waiting for transfers between devices, exchange(): lax.ppermute(chunks[k], 'head', [(i, i ^ k) for i in range(GROUP)])  23.5 us
    ppermute x14, starting transfers between devices, exchange(): lax.ppermute(chunks[k], 'head', [(i, i ^ k) for i in range(GROUP)])  21.3 us
    all_to_all x2, starting transfers between devices, transposed(): lax.all_to_all(message, 'seq', split_axis=0, concat_axis=0, tiled=True)  12.2 us
    unnamed x38, local copies, waits for them, and re-layouts  3.24 us
  transfers between devices with their start and end apart: 16, of which 8 were waited for; matrix products, arithmetic and copies ran while one was open for 0% of the time, Pallas kernels for 18%

profile of v1, /device:TPU:1, one launch (start us, length us, event | category | flops | bytes accessed | tf_op | source)
XLA Modules:
  0.0 127.3 jit_solution(232273093439424374)
XLA Ops:
  1.3 4.8 %shard_map.195 = bf16[256,1664]{1,0:T(8,128)(2,1)} custom-call(s32[1]{0:T(128)S(6)} %copy.24.length, bf16[2,256,128]{2,1,0:T(8,128)(2,1)} %pr.5, f32[2,16,256]{2,1,0:T(8,128)} %pd.9, bf16[2,256,1024]{2,1,0:T(8,128)(2,1)} %pc.5, bf16[1,256,128]{2,1,0:T(8,128)(2,1)} %ar.5, f32[1,16,256]{2,1,0:T(8,128)} %ad.5, bf16[1,256,1024]{2,1,0:T(8,128)(2,1)} %ac.5), custom_call_target="tpu_custom_call" | custom-call | flops 1000000000 | bytes 4000000 | tf_op jit(solution)/shard_map/pallas_call | solution.py:376
  6.1 8.6 %all-to-all-start = ((bf16[16,16,1664]{2,1,0:T(8,128)(2,1)}), bf16[16,16,1664]{2,1,0:T(8,128)(2,1)S(1)}, u32[]{:S(2)}, u32[]{:S(2)}) async-start(bf16[16,16,1664]{2,1,0:T(8,128)(2,1)} %bitcast.15), calls=%async_computation | async-start | bytes 1703936 | tf_op jit(solution)/shard_map/all_to_all | solution.py:398
  14.7 2.3 %shard_map.197 = (bf16[3,32,1024]{2,1,0:T(8,128)(2,1)}, bf16[3,32,1024]{2,1,0:T(8,128)(2,1)}, bf16[3,32,1024]{2,1,0:T(8,128)(2,1)}, bf16[3,32,1024]{2,1,0:T(8,12...) custom-call(s32[1]{0:T(128)} %bitcast.me, ...), custom_call_target="tpu_custom_call" | custom-call | flops 1000000000 | bytes 4000000 | tf_op jit(solution)/shard_map/pallas_call | solution.py:376
  17.0 1.0 collective-permute-start
  18.1 1.2 collective-permute-start.1
  19.3 0.5 collective-permute-start.2
  19.8 2.7 %collective-permute-start.3 = (bf16[3,32,1024]{2,1,0:T(8,128)(2,1)}, bf16[3,32,1024]{2,1,0:T(8,128)(2,1)S(1)}, u32[]{:S(2)}, u32[]{:S(2)}) collective-permute-start(bf16[3,32,1024]{2,1,0:T(8,128)(2,1)} %get-tuple-element.50), channel_id=1, source_target_pairs={{0,4},{1,5},{2,6},{3,7},{4,0},{5,1},{6,2},{7,3},{8,12},{9,13},{10,... | collective-permute-start | bytes 589832 | tf_op jit(solution)/shard_map/ppermute | solution.py:393
  22.5 0.5 collective-permute-start.4
  23.1 0.0 collective-permute-done.refs_1_
  23.1 2.5 %collective-permute-start.5 = (bf16[3,32,1024]{2,1,0:T(8,128)(2,1)}, bf16[3,32,1024]{2,1,0:T(8,128)(2,1)S(1)}, u32[]{:S(2)}, u32[]{:S(2)}) collective-permute-start(bf16[3,32,1024]{2,1,0:T(8,128)(2,1)} %get-tuple-element.52), channel_id=1, source_target_pairs={{0,6},{1,7},{2,4},{3,5},{4,2},{5,3},{6,0},{7,1},{8,14},{9,15},{10,... | collective-permute-start | bytes 589832 | tf_op jit(solution)/shard_map/ppermute | solution.py:393
  25.6 0.0 collective-permute-done.1.refs_2_
  25.6 3.0 %collective-permute-start.6 = (bf16[3,32,1024]{2,1,0:T(8,128)(2,1)}, bf16[3,32,1024]{2,1,0:T(8,128)(2,1)S(1)}, u32[]{:S(2)}, u32[]{:S(2)}) collective-permute-start(bf16[3,32,1024]{2,1,0:T(8,128)(2,1)} %get-tuple-element.53), channel_id=1, source_target_pairs={{0,7},{1,6},{2,5},{3,4},{4,3},{5,2},{6,1},{7,0},{8,15},{9,14},{10,... | collective-permute-start | bytes 589832 | tf_op jit(solution)/shard_map/ppermute | solution.py:393
  28.5 0.1 all-to-all-done
  28.6 0.9 copy-done.4
  29.5 2.2 %shard_map.196 = (bf16[256,2048]{1,0:T(8,128)(2,1)}, f32[32,512]{1,0:T(8,128)}) custom-call(s32[2]{0:T(128)} %sizes.3, bf16[256,1664]{1,0:T(8,128)(2,1)} %bitcast.12, bf16[256,1664]{1,0:T(8,128)(2,1)} %bitcast.13, bf16[256,1664]{1,0:T(8,128)(2,1)} %bitcast.14), custom_call_target="tpu_custom_call" | custom-call | flops 1000000000 | bytes 4000000 | tf_op jit(solution)/shard_map/pallas_call | solution.py:376
  31.8 0.0 collective-permute-done.2.refs_3_
  31.8 3.6 %collective-permute-done.3.refs_4_ = bf16[3,32,1024]{2,1,0:T(8,128)(2,1)S(1)} collective-permute-done((bf16[3,32,1024]{2,1,0:T(8,128)(2,1)}, bf16[3,32,1024]{2,1,0:T(8,128)(2,1)S(1)}, u32[]{:S(2)}, u32[]{:S(2)}) %collective-permute-start.3) | collective-permute-done | bytes 196640 | tf_op jit(solution)/shard_map/ppermute | solution.py:393
  35.3 4.5 %collective-permute-done.4.refs_5_ = bf16[3,32,1024]{2,1,0:T(8,128)(2,1)S(1)} collective-permute-done((bf16[3,32,1024]{2,1,0:T(8,128)(2,1)}, bf16[3,32,1024]{2,1,0:T(8,128)(2,1)S(1)}, u32[]{:S(2)}, u32[]{:S(2)}) %collective-permute-start.4) | collective-permute-done | bytes 196640 | tf_op jit(solution)/shard_map/ppermute | solution.py:393
  39.8 0.0 collective-permute-done.5.refs_6_
  39.9 3.9 %collective-permute-done.6.refs_7_ = bf16[3,32,1024]{2,1,0:T(8,128)(2,1)S(1)} collective-permute-done((bf16[3,32,1024]{2,1,0:T(8,128)(2,1)}, bf16[3,32,1024]{2,1,0:T(8,128)(2,1)S(1)}, u32[]{:S(2)}, u32[]{:S(2)}) %collective-permute-start.6) | collective-permute-done | bytes 196640 | tf_op jit(solution)/shard_map/ppermute | solution.py:393
  43.8 0.0 copy-done.5
  43.8 0.0 copy-done.6
  43.8 0.0 copy-done.7
  43.8 0.0 copy-done.8
  43.8 0.0 copy-done.9
  43.8 0.0 copy-done.10
  43.8 0.6 copy-done.11
  44.4 3.7 %shard_map.198 = bf16[256,2048]{1,0:T(8,128)(2,1)} custom-call(s32[1]{0:T(128)} %bitcast.me, bf16[256,2048]{1,0:T(8,128)(2,1)} %get-tuple-element.45.message, bf16[2,256,128]{2,1,0:T(8,128)(2,1)} %pw.5, f32[2,16,256]{2,1,0:T(8,128)} %pd.9, bf16[3,32,1024]{2,1,0:T(8,128)(2,1)} %get-tuple-element.46.refs_0_, ...), custom_call_target="tpu_custom_call", output_to_operand_aliasing={{}: (1, {})} | custom-call | flops 1000000000 | bytes 4000000 | tf_op jit(solution)/shard_map/pallas_call | solution.py:376
  48.1 0.0 copy-start.2
  48.1 23.7 %all_to_all.33 = bf16[16,16,2048]{2,1,0:T(8,128)(2,1)S(1)} all-to-all(bf16[16,16,2048]{2,1,0:T(8,128)(2,1)} %bitcast.10), channel_id=1, replica_groups=mesh['seq'=16,'head'=8] {'seq'}, dimensions={0} | all-to-all | bytes 2097152 | tf_op jit(solution)/shard_map/all_to_all | solution.py:398
  71.8 0.0 copy-done.1
  71.8 0.0 copy-done.2
  71.8 1.6 %shard_map.199 = bf16[256,1536]{1,0:T(8,128)(2,1)} custom-call(s32[2]{0:T(128)S(1)} %copy-done.1, f32[32,512]{1,0:T(8,128)S(1)} %copy-done.2, bf16[256,2048]{1,0:T(8,128)(2,1)S(1)} %bitcast.7), custom_call_target="tpu_custom_call" | custom-call | flops 1000000000 | bytes 4000000 | tf_op jit(solution)/shard_map/pallas_call | solution.py:376
  73.4 0.0 copy-done
  73.4 3.6 %all-to-all-start.2 = ((bf16[16,16,1536]{2,1,0:T(8,128)(2,1)}), bf16[16,16,1536]{2,1,0:T(8,128)(2,1)S(1)}, u32[]{:S(2)}, u32[]{:S(2)}) async-start(bf16[16,16,1536]{2,1,0:T(8,128)(2,1)} %bitcast.5), calls=%async_computation.2 | async-start | bytes 1572864 | tf_op jit(solution)/shard_map/all_to_all | solution.py:398
  77.0 11.2 %shard_map.200 = (bf16[3,256,1024]{2,1,0:T(8,128)(2,1)}, bf16[3,256,1024]{2,1,0:T(8,128)(2,1)}, f32[3,256,128]{2,1,0:T(8,128)}, f32[2,256,128]{2,1,0:T(8,128)}, ...) custom-call(s32[1]{0:T(128)S(6)} %copy.24.length, s32[1]{0:T(128)} %bitcast.me, bf16[2,256,128]{2,1,0:T(8,128)(2,1)} %pw.5, ...), custom_call_target="tpu_custom_call" | custom-call | flops 8000000000 | bytes 4000000 | tf_op jit(solution)/shard_map/pallas_call | solution.py:376
  88.2 5.4 %shard_map.201 = (bf16[3,32,1024]{2,1,0:T(8,128)(2,1)}, bf16[3,32,1024]{2,1,0:T(8,128)(2,1)}, bf16[3,32,1024]{2,1,0:T(8,128)(2,1)}, bf16[3,32,1024]{2,1,0:T(8,12...) custom-call(s32[1]{0:T(128)} %bitcast.me, ...), custom_call_target="tpu_custom_call" | custom-call | flops 1000000000 | bytes 4000000 | tf_op jit(solution)/shard_map/pallas_call | solution.py:376
  93.6 1.6 %collective-permute-start.10 = (bf16[3,32,1024]{2,1,0:T(8,128)(2,1)}, bf16[3,32,1024]{2,1,0:T(8,128)(2,1)S(1)}, u32[]{:S(2)}, u32[]{:S(2)}) collective-permute-start(bf16[3,32,1024]{2,1,0:T(8,128)(2,1)} %get-tuple-element.67), channel_id=1, source_target_pairs={{0,4},{1,5},{2,6},{3,7},{4,0},{5,1},{6,2},{7,3},{8,12},{9,13},{10,... | collective-permute-start | bytes 589832 | tf_op jit(solution)/shard_map/ppermute | solution.py:393
  95.3 3.2 %collective-permute-start.11 = (bf16[3,32,1024]{2,1,0:T(8,128)(2,1)}, bf16[3,32,1024]{2,1,0:T(8,128)(2,1)S(1)}, u32[]{:S(2)}, u32[]{:S(2)}) collective-permute-start(bf16[3,32,1024]{2,1,0:T(8,128)(2,1)} %get-tuple-element.68), channel_id=1, source_target_pairs={{0,5},{1,4},{2,7},{3,6},{4,1},{5,0},{6,3},{7,2},{8,13},{9,12},{10,... | collective-permute-start | bytes 589832 | tf_op jit(solution)/shard_map/ppermute | solution.py:393
  98.4 2.5 %collective-permute-start.12 = (bf16[3,32,1024]{2,1,0:T(8,128)(2,1)}, bf16[3,32,1024]{2,1,0:T(8,128)(2,1)S(1)}, u32[]{:S(2)}, u32[]{:S(2)}) collective-permute-start(bf16[3,32,1024]{2,1,0:T(8,128)(2,1)} %get-tuple-element.69), channel_id=1, source_target_pairs={{0,6},{1,7},{2,4},{3,5},{4,2},{5,3},{6,0},{7,1},{8,14},{9,15},{10,... | collective-permute-start | bytes 589832 | tf_op jit(solution)/shard_map/ppermute | solution.py:393
  100.9 0.0 collective-permute-start.13
  100.9 0.6 collective-permute-start.7
  101.5 0.0 collective-permute-done.10.refs_4_
  101.5 0.0 collective-permute-start.8
  101.5 4.9 %collective-permute-done.11.refs_5_ = bf16[3,32,1024]{2,1,0:T(8,128)(2,1)S(1)} collective-permute-done((bf16[3,32,1024]{2,1,0:T(8,128)(2,1)}, bf16[3,32,1024]{2,1,0:T(8,128)(2,1)S(1)}, u32[]{:S(2)}, u32[]{:S(2)}) %collective-permute-start.11) | collective-permute-done | bytes 196640 | tf_op jit(solution)/shard_map/ppermute | solution.py:393
  106.4 2.0 %collective-permute-start.9 = (bf16[3,32,1024]{2,1,0:T(8,128)(2,1)}, bf16[3,32,1024]{2,1,0:T(8,128)(2,1)S(1)}, u32[]{:S(2)}, u32[]{:S(2)}) collective-permute-start(bf16[3,32,1024]{2,1,0:T(8,128)(2,1)} %get-tuple-element.66), channel_id=1, source_target_pairs={{0,3},{1,2},{2,1},{3,0},{4,7},{5,6},{6,5},{7,4},{8,11},{9,10},{10,... | collective-permute-start | bytes 589832 | tf_op jit(solution)/shard_map/ppermute | solution.py:393
  108.4 2.3 %collective-permute-done.12.refs_6_ = bf16[3,32,1024]{2,1,0:T(8,128)(2,1)S(1)} collective-permute-done((bf16[3,32,1024]{2,1,0:T(8,128)(2,1)}, bf16[3,32,1024]{2,1,0:T(8,128)(2,1)S(1)}, u32[]{:S(2)}, u32[]{:S(2)}) %collective-permute-start.12) | collective-permute-done | bytes 196640 | tf_op jit(solution)/shard_map/ppermute | solution.py:393
  110.7 4.2 %collective-permute-done.13.refs_7_ = bf16[3,32,1024]{2,1,0:T(8,128)(2,1)S(1)} collective-permute-done((bf16[3,32,1024]{2,1,0:T(8,128)(2,1)}, bf16[3,32,1024]{2,1,0:T(8,128)(2,1)S(1)}, u32[]{:S(2)}, u32[]{:S(2)}) %collective-permute-start.13) | collective-permute-done | bytes 196640 | tf_op jit(solution)/shard_map/ppermute | solution.py:393
  114.9 0.0 collective-permute-done.7.refs_1_
  114.9 0.0 collective-permute-done.8.refs_2_
  114.9 0.0 copy-start.17
  114.9 0.1 collective-permute-done.9.refs_3_
  115.0 0.0 copy-done.12
  115.0 0.0 copy-done.13
  115.0 0.0 copy-done.14
  115.0 0.6 copy-done.15
  115.6 0.1 copy-done.16
  115.7 0.1 copy-done.17
  115.7 0.1 copy-done.18
  115.8 2.4 %shard_map.203 = (bf16[2,32,8192]{2,1,0:T(8,128)(2,1)}, bf16[1,32,8192]{2,1,0:T(8,128)(2,1)}) custom-call(s32[1]{0:T(128)} %bitcast.me, bf16[3,32,1024]{2,1,0:T(8,128)(2,1)} %get-tuple-element.63.refs_0_, bf16[3,32,1024]{2,1,0:T(8,128)(2,1)} %copy-done.16, bf16[3,32,1024]{2,1,0:T(8,128)(2,1)} %copy-done.17, bf16[3,32,1024]{2,1,0:T(8,128)(2,1)} %copy-done.18, ...), custom_call_target="tpu_custom_call" | custom-call | flops 1000000000 | bytes 4000000 | tf_op jit(solution)/shard_map/pallas_call | solution.py:376
  118.2 0.0 all-to-all-done.2
  118.2 0.0 copy-start.3
  118.2 0.9 copy-done.3
  119.0 8.3 %shard_map.202 = (bf16[2,256,1024]{2,1,0:T(8,128)(2,1)}, bf16[2,256,128]{2,1,0:T(8,128)(2,1)}, f32[2,16,256]{2,1,0:T(8,128)}, bf16[1,256,1024]{2,1,0:T(8,128)(2,...) custom-call(s32[1]{0:T(128)S(6)} %copy.24.length, bf16[256,2048]{1,0:T(8,128)(2,1)} %bitcast.9, ...), custom_call_target="tpu_custom_call" | custom-call | flops 1000000000 | bytes 4000000 | tf_op jit(solution)/shard_map/pallas_call | solution.py:376
  (16 shorter events, 0.0 us)
Async XLA Ops:
  6.1 22.5 %all-to-all-start = ((bf16[16,16,1664]{2,1,0:T(8,128)(2,1)}), bf16[16,16,1664]{2,1,0:T(8,128)(2,1)S(1)}, u32[]{:S(2)}, u32[]{:S(2)}) async-start(bf16[16,16,1664]{2,1,0:T(8,128)(2,1)} %bitcast.15), calls=%async_computation | async-start | bytes 1703936 | tf_op jit(solution)/shard_map/all_to_all | solution.py:398
  17.0 6.0 %collective-permute-start = (bf16[3,32,1024]{2,1,0:T(8,128)(2,1)}, bf16[3,32,1024]{2,1,0:T(8,128)(2,1)S(1)}, u32[]{:S(2)}, u32[]{:S(2)}) collective-permute-start(bf16[3,32,1024]{2,1,0:T(8,128)(2,1)} %get-tuple-element.47), channel_id=1, source_target_pairs={{0,1},{1,0},{2,3},{3,2},{4,5},{5,4},{6,7},{7,6},{8,9},{9,8},{10,11... | collective-permute-start | bytes 589832 | tf_op jit(solution)/shard_map/ppermute | solution.py:393
  18.1 7.5 %collective-permute-start.1 = (bf16[3,32,1024]{2,1,0:T(8,128)(2,1)}, bf16[3,32,1024]{2,1,0:T(8,128)(2,1)S(1)}, u32[]{:S(2)}, u32[]{:S(2)}) collective-permute-start(bf16[3,32,1024]{2,1,0:T(8,128)(2,1)} %get-tuple-element.48), channel_id=1, source_target_pairs={{0,2},{1,3},{2,0},{3,1},{4,6},{5,7},{6,4},{7,5},{8,10},{9,11},{10,... | collective-permute-start | bytes 589832 | tf_op jit(solution)/shard_map/ppermute | solution.py:393
  19.3 12.5 %collective-permute-start.2 = (bf16[3,32,1024]{2,1,0:T(8,128)(2,1)}, bf16[3,32,1024]{2,1,0:T(8,128)(2,1)S(1)}, u32[]{:S(2)}, u32[]{:S(2)}) collective-permute-start(bf16[3,32,1024]{2,1,0:T(8,128)(2,1)} %get-tuple-element.49), channel_id=1, source_target_pairs={{0,3},{1,2},{2,1},{3,0},{4,7},{5,6},{6,5},{7,4},{8,11},{9,10},{10,... | collective-permute-start | bytes 589832 | tf_op jit(solution)/shard_map/ppermute | solution.py:393
  19.8 15.5 %collective-permute-start.3 = (bf16[3,32,1024]{2,1,0:T(8,128)(2,1)}, bf16[3,32,1024]{2,1,0:T(8,128)(2,1)S(1)}, u32[]{:S(2)}, u32[]{:S(2)}) collective-permute-start(bf16[3,32,1024]{2,1,0:T(8,128)(2,1)} %get-tuple-element.50), channel_id=1, source_target_pairs={{0,4},{1,5},{2,6},{3,7},{4,0},{5,1},{6,2},{7,3},{8,12},{9,13},{10,... | collective-permute-start | bytes 589832 | tf_op jit(solution)/shard_map/ppermute | solution.py:393
  22.5 17.3 %collective-permute-start.4 = (bf16[3,32,1024]{2,1,0:T(8,128)(2,1)}, bf16[3,32,1024]{2,1,0:T(8,128)(2,1)S(1)}, u32[]{:S(2)}, u32[]{:S(2)}) collective-permute-start(bf16[3,32,1024]{2,1,0:T(8,128)(2,1)} %get-tuple-element.51), channel_id=1, source_target_pairs={{0,5},{1,4},{2,7},{3,6},{4,1},{5,0},{6,3},{7,2},{8,13},{9,12},{10,... | collective-permute-start | bytes 589832 | tf_op jit(solution)/shard_map/ppermute | solution.py:393
  23.1 20.7 %copy-start.5 = (bf16[3,32,1024]{2,1,0:T(8,128)(2,1)}, bf16[3,32,1024]{2,1,0:T(8,128)(2,1)S(1)}, u32[]{:S(2)}) copy-start(bf16[3,32,1024]{2,1,0:T(8,128)(2,1)S(1)} %collective-permute-done.refs_1_) | copy-start | bytes 589828
  23.1 16.8 %collective-permute-start.5 = (bf16[3,32,1024]{2,1,0:T(8,128)(2,1)}, bf16[3,32,1024]{2,1,0:T(8,128)(2,1)S(1)}, u32[]{:S(2)}, u32[]{:S(2)}) collective-permute-start(bf16[3,32,1024]{2,1,0:T(8,128)(2,1)} %get-tuple-element.52), channel_id=1, source_target_pairs={{0,6},{1,7},{2,4},{3,5},{4,2},{5,3},{6,0},{7,1},{8,14},{9,15},{10,... | collective-permute-start | bytes 589832 | tf_op jit(solution)/shard_map/ppermute | solution.py:393
  25.6 18.2 %copy-start.6 = (bf16[3,32,1024]{2,1,0:T(8,128)(2,1)}, bf16[3,32,1024]{2,1,0:T(8,128)(2,1)S(1)}, u32[]{:S(2)}) copy-start(bf16[3,32,1024]{2,1,0:T(8,128)(2,1)S(1)} %collective-permute-done.1.refs_2_) | copy-start | bytes 589828
  25.6 18.2 %collective-permute-start.6 = (bf16[3,32,1024]{2,1,0:T(8,128)(2,1)}, bf16[3,32,1024]{2,1,0:T(8,128)(2,1)S(1)}, u32[]{:S(2)}, u32[]{:S(2)}) collective-permute-start(bf16[3,32,1024]{2,1,0:T(8,128)(2,1)} %get-tuple-element.53), channel_id=1, source_target_pairs={{0,7},{1,6},{2,5},{3,4},{4,3},{5,2},{6,1},{7,0},{8,15},{9,14},{10,... | collective-permute-start | bytes 589832 | tf_op jit(solution)/shard_map/ppermute | solution.py:393
  28.6 0.9 copy-start.4
  31.8 12.0 %copy-start.7 = (bf16[3,32,1024]{2,1,0:T(8,128)(2,1)}, bf16[3,32,1024]{2,1,0:T(8,128)(2,1)S(1)}, u32[]{:S(2)}) copy-start(bf16[3,32,1024]{2,1,0:T(8,128)(2,1)S(1)} %collective-permute-done.2.refs_3_) | copy-start | bytes 589828
  35.3 8.5 %copy-start.8 = (bf16[3,32,1024]{2,1,0:T(8,128)(2,1)}, bf16[3,32,1024]{2,1,0:T(8,128)(2,1)S(1)}, u32[]{:S(2)}) copy-start(bf16[3,32,1024]{2,1,0:T(8,128)(2,1)S(1)} %collective-permute-done.3.refs_4_) | copy-start | bytes 589828
  39.8 3.9 %copy-start.9 = (bf16[3,32,1024]{2,1,0:T(8,128)(2,1)}, bf16[3,32,1024]{2,1,0:T(8,128)(2,1)S(1)}, u32[]{:S(2)}) copy-start(bf16[3,32,1024]{2,1,0:T(8,128)(2,1)S(1)} %collective-permute-done.4.refs_5_) | copy-start | bytes 589828
  39.9 3.9 %copy-start.10 = (bf16[3,32,1024]{2,1,0:T(8,128)(2,1)}, bf16[3,32,1024]{2,1,0:T(8,128)(2,1)S(1)}, u32[]{:S(2)}) copy-start(bf16[3,32,1024]{2,1,0:T(8,128)(2,1)S(1)} %collective-permute-done.5.refs_6_) | copy-start | bytes 589828
  43.8 0.7 copy-start.11
  48.1 23.7 %copy-start.1 = (s32[2]{0:T(128)S(1)}, s32[2]{0:T(128)}, u32[]{:S(2)}) copy-start(s32[2]{0:T(128)} %sizes.3) | copy-start | bytes 28
  48.1 23.7 %copy-start.2 = (f32[32,512]{1,0:T(8,128)S(1)}, f32[32,512]{1,0:T(8,128)}, u32[]{:S(2)}) copy-start(f32[32,512]{1,0:T(8,128)} %get-tuple-element.54.factors) | copy-start | bytes 196612
  71.8 1.6 %copy-start = (bf16[16,16,2048]{2,1,0:T(8,128)(2,1)}, bf16[16,16,2048]{2,1,0:T(8,128)(2,1)S(1)}, u32[]{:S(2)}) copy-start(bf16[16,16,2048]{2,1,0:T(8,128)(2,1)S(1)} %all_to_all.33) | copy-start | bytes 3145732
  73.4 44.8 %all-to-all-start.2 = ((bf16[16,16,1536]{2,1,0:T(8,128)(2,1)}), bf16[16,16,1536]{2,1,0:T(8,128)(2,1)S(1)}, u32[]{:S(2)}, u32[]{:S(2)}) async-start(bf16[16,16,1536]{2,1,0:T(8,128)(2,1)} %bitcast.5), calls=%async_computation.2 | async-start | bytes 1572864 | tf_op jit(solution)/shard_map/all_to_all | solution.py:398
  93.6 7.9 %collective-permute-start.10 = (bf16[3,32,1024]{2,1,0:T(8,128)(2,1)}, bf16[3,32,1024]{2,1,0:T(8,128)(2,1)S(1)}, u32[]{:S(2)}, u32[]{:S(2)}) collective-permute-start(bf16[3,32,1024]{2,1,0:T(8,128)(2,1)} %get-tuple-element.67), channel_id=1, source_target_pairs={{0,4},{1,5},{2,6},{3,7},{4,0},{5,1},{6,2},{7,3},{8,12},{9,13},{10,... | collective-permute-start | bytes 589832 | tf_op jit(solution)/shard_map/ppermute | solution.py:393
  95.3 11.1 %collective-permute-start.11 = (bf16[3,32,1024]{2,1,0:T(8,128)(2,1)}, bf16[3,32,1024]{2,1,0:T(8,128)(2,1)S(1)}, u32[]{:S(2)}, u32[]{:S(2)}) collective-permute-start(bf16[3,32,1024]{2,1,0:T(8,128)(2,1)} %get-tuple-element.68), channel_id=1, source_target_pairs={{0,5},{1,4},{2,7},{3,6},{4,1},{5,0},{6,3},{7,2},{8,13},{9,12},{10,... | collective-permute-start | bytes 589832 | tf_op jit(solution)/shard_map/ppermute | solution.py:393
  98.4 12.3 %collective-permute-start.12 = (bf16[3,32,1024]{2,1,0:T(8,128)(2,1)}, bf16[3,32,1024]{2,1,0:T(8,128)(2,1)S(1)}, u32[]{:S(2)}, u32[]{:S(2)}) collective-permute-start(bf16[3,32,1024]{2,1,0:T(8,128)(2,1)} %get-tuple-element.69), channel_id=1, source_target_pairs={{0,6},{1,7},{2,4},{3,5},{4,2},{5,3},{6,0},{7,1},{8,14},{9,15},{10,... | collective-permute-start | bytes 589832 | tf_op jit(solution)/shard_map/ppermute | solution.py:393
  100.9 14.0 %collective-permute-start.13 = (bf16[3,32,1024]{2,1,0:T(8,128)(2,1)}, bf16[3,32,1024]{2,1,0:T(8,128)(2,1)S(1)}, u32[]{:S(2)}, u32[]{:S(2)}) collective-permute-start(bf16[3,32,1024]{2,1,0:T(8,128)(2,1)} %get-tuple-element.70), channel_id=1, source_target_pairs={{0,7},{1,6},{2,5},{3,4},{4,3},{5,2},{6,1},{7,0},{8,15},{9,14},{10,... | collective-permute-start | bytes 589832 | tf_op jit(solution)/shard_map/ppermute | solution.py:393
  100.9 14.0 %collective-permute-start.7 = (bf16[3,32,1024]{2,1,0:T(8,128)(2,1)}, bf16[3,32,1024]{2,1,0:T(8,128)(2,1)S(1)}, u32[]{:S(2)}, u32[]{:S(2)}) collective-permute-start(bf16[3,32,1024]{2,1,0:T(8,128)(2,1)} %get-tuple-element.64), channel_id=1, source_target_pairs={{0,1},{1,0},{2,3},{3,2},{4,5},{5,4},{6,7},{7,6},{8,9},{9,8},{10,11... | collective-permute-start | bytes 589832 | tf_op jit(solution)/shard_map/ppermute | solution.py:393
  101.5 13.5 %copy-start.12 = (bf16[3,32,1024]{2,1,0:T(8,128)(2,1)}, bf16[3,32,1024]{2,1,0:T(8,128)(2,1)S(1)}, u32[]{:S(2)}) copy-start(bf16[3,32,1024]{2,1,0:T(8,128)(2,1)S(1)} %collective-permute-done.10.refs_4_) | copy-start | bytes 589828
  101.5 13.4 %collective-permute-start.8 = (bf16[3,32,1024]{2,1,0:T(8,128)(2,1)}, bf16[3,32,1024]{2,1,0:T(8,128)(2,1)S(1)}, u32[]{:S(2)}, u32[]{:S(2)}) collective-permute-start(bf16[3,32,1024]{2,1,0:T(8,128)(2,1)} %get-tuple-element.65), channel_id=1, source_target_pairs={{0,2},{1,3},{2,0},{3,1},{4,6},{5,7},{6,4},{7,5},{8,10},{9,11},{10,... | collective-permute-start | bytes 589832 | tf_op jit(solution)/shard_map/ppermute | solution.py:393
  106.4 8.6 %copy-start.13 = (bf16[3,32,1024]{2,1,0:T(8,128)(2,1)}, bf16[3,32,1024]{2,1,0:T(8,128)(2,1)S(1)}, u32[]{:S(2)}) copy-start(bf16[3,32,1024]{2,1,0:T(8,128)(2,1)S(1)} %collective-permute-done.11.refs_5_) | copy-start | bytes 589828
  106.4 8.6 %collective-permute-start.9 = (bf16[3,32,1024]{2,1,0:T(8,128)(2,1)}, bf16[3,32,1024]{2,1,0:T(8,128)(2,1)S(1)}, u32[]{:S(2)}, u32[]{:S(2)}) collective-permute-start(bf16[3,32,1024]{2,1,0:T(8,128)(2,1)} %get-tuple-element.66), channel_id=1, source_target_pairs={{0,3},{1,2},{2,1},{3,0},{4,7},{5,6},{6,5},{7,4},{8,11},{9,10},{10,... | collective-permute-start | bytes 589832 | tf_op jit(solution)/shard_map/ppermute | solution.py:393
  110.7 4.3 %copy-start.14 = (bf16[3,32,1024]{2,1,0:T(8,128)(2,1)}, bf16[3,32,1024]{2,1,0:T(8,128)(2,1)S(1)}, u32[]{:S(2)}) copy-start(bf16[3,32,1024]{2,1,0:T(8,128)(2,1)S(1)} %collective-permute-done.12.refs_6_) | copy-start | bytes 589828
  114.9 0.7 copy-start.15
  114.9 0.7 copy-start.16
  114.9 0.8 copy-start.17
  115.0 0.8 copy-start.18
  118.2 0.9 copy-start.3

commit v2 on v1

--- a/solution.py
+++ b/solution.py
@@ -85,10 +85,10 @@
 
 
 def head_sums(values):
-    member = (iota((L, H), 0) // HD == iota((L, H), 1)).astype(BF16)
+    member = (iota((H, L), 1) // HD == iota((H, L), 0)).astype(BF16)
     high = values.astype(BF16)
     low = (values - high.astype(F32)).astype(BF16)
-    return nn(high, member) + nn(low, member)
+    return nt(member, high) + nt(member, low)
 
 
 def live_rows(value, length):
@@ -117,76 +117,68 @@
         x[pl.ds(there, ROWS), :] = chunks[k][0]
 
 
-def reach_kernel(length, pr, pd, pc, ar, ad, ac, out, factors):
-    b = pl.program_id(0)
-    answer = b == 2
-    read = jnp.where(answer, ar[0], pr[0])
-    decay = jnp.where(answer, ad[0], pd[0])
-    alive = jnp.where(answer, length[0], B)
-    cot = live_rows(jnp.where(answer, ac[0], pc[0]).astype(F32), alive)
-    growth = grown(decay)
-    scattered(out, tn(read, (cot * growth).astype(BF16)), pl.multiple_of(b * HALF, HALF))
-    last = growth[B - 1 : B, :]
-    high = last.astype(BF16).astype(F32)
-
-    @pl.when(b < 2)
-    def _():
-        factors[pl.ds(2 * b, 1), :] = high
-        factors[pl.ds(2 * b + 1, 1), :] = last - high
-
-    @pl.when(answer)
-    def _():
-        for half in range(2):
-            lanes = [slice(HALF * half + N * j, HALF * half + N * j + N) for j in range(4)]
-            part = jnp.concatenate([factors[i : i + 1, lane] for i in range(4) for lane in lanes], axis=0)
-            for d in range(half, SHARDS, 2):
-                out[16 * d : 16 * d + 16, 3 * HALF :] = part.astype(BF16)
-
-
-def split_kernel(me, pt, at, *refs):
-    outs, (stage, came, went) = refs[:GROUP], refs[GROUP:]
-    coming, going = [], []
-    for k in (4, 5, 2, 3, 6, 7, 1, 0):
-        there = pl.multiple_of((me[0] ^ k) * L, L)
-        coming.append(
-            (
-                pltpu.make_async_copy(pt.at[:, :, pl.ds(there, L)], stage.at[k, 0:2], came.at[2 * k]),
-                pltpu.make_async_copy(at.at[:, :, pl.ds(there, L)], stage.at[k, 2:3], came.at[2 * k + 1]),
-            )
-        )
-        going.append(pltpu.make_async_copy(stage.at[k], outs[k], went.at[k]))
-    for first, second in coming:
-        first.start()
-        second.start()
-    for (first, second), third in zip(coming, going):
-        first.wait()
-        second.wait()
-        third.start()
+def reach_kernel(length, pr, pd, pc, ar, ad, ac, out, reads, decays, cots, stage, factors, came, went):
+    coming = []
+    for b in range(3):
+        group = []
+        for i, (prompt, answer, place) in enumerate(((pd, ad, decays), (pr, ar, reads), (pc, ac, cots))):
+            source = prompt.at[b] if b < 2 else answer.at[0]
+            group.append(pltpu.make_async_copy(source, place.at[b], came.at[3 * b + i]))
+            group[-1].start()
+        coming.append(group)
+    going = []
+    for b in range(3):
+        for copy in coming[b]:
+            copy.wait()
+        cot = cots[b].astype(F32)
+        if b == 2:
+            cot = live_rows(cot, length[0])
+        growth = grown(decays[b])
+        scattered(stage, tn(reads[b], (cot * growth).astype(BF16)), b * HALF)
+        going.append(pltpu.make_async_copy(stage.at[:, pl.ds(b * HALF, HALF)], out.at[:, pl.ds(b * HALF, HALF)], went.at[b]))
+        going[-1].start()
+        if b < 2:
+            last = growth[B - 1 : B, :]
+            high = last.astype(BF16).astype(F32)
+            factors[2 * b : 2 * b + 1, :] = high
+            factors[2 * b + 1 : 2 * b + 2, :] = last - high
+        if b == 1:
+            for half in range(2):
+                lanes = [slice(HALF * half + N * j, HALF * half + N * j + N) for j in range(4)]
+                part = jnp.concatenate([factors[i : i + 1, lane] for i in range(4) for lane in lanes], axis=0)
+                for d in range(half, SHARDS, 2):
+                    stage[16 * d : 16 * d + 16, 3 * HALF :] = part.astype(BF16)
+            tail = pl.ds(3 * HALF, N)
+            going.append(pltpu.make_async_copy(stage.at[:, tail], out.at[:, tail], went.at[3]))
+            going[-1].start()
     for copy in going:
         copy.wait()
 
 
-def join_kernel(me, *refs):
-    ins, (pt, at, stage, came, went) = refs[:GROUP], refs[GROUP:]
-    coming, going = [], []
+def split_kernel(me, pt, at, *refs):
+    outs, came = refs[:GROUP], refs[GROUP]
+    copies = []
     for k in range(GROUP):
         there = pl.multiple_of((me[0] ^ k) * L, L)
-        coming.append(pltpu.make_async_copy(ins[k], stage.at[k], came.at[k]))
-        going.append(
-            (
-                pltpu.make_async_copy(stage.at[k, 0:2], pt.at[:, :, pl.ds(there, L)], went.at[2 * k]),
-                pltpu.make_async_copy(stage.at[k, 2:3], at.at[:, :, pl.ds(there, L)], went.at[2 * k + 1]),
-            )
-        )
-    for copy in coming:
+        copies.append(pltpu.make_async_copy(pt.at[:, :, pl.ds(there, L)], outs[k].at[0:2], came.at[2 * k]))
+        copies.append(pltpu.make_async_copy(at.at[:, :, pl.ds(there, L)], outs[k].at[2:3], came.at[2 * k + 1]))
+    for copy in copies:
         copy.start()
-    for first, (second, third) in zip(coming, going):
-        first.wait()
-        second.start()
-        third.start()
-    for second, third in going:
-        second.wait()
-        third.wait()
+    for copy in copies:
+        copy.wait()
+
+
+def join_kernel(me, *refs):
+    ins, (pt, at, went) = refs[:GROUP], refs[GROUP:]
+    copies = []
+    for k in range(GROUP):
+        there = pl.multiple_of((me[0] ^ k) * L, L)
+        copies.append(pltpu.make_async_copy(ins[k].at[0:2], pt.at[:, :, pl.ds(there, L)], went.at[2 * k]))
+        copies.append(pltpu.make_async_copy(ins[k].at[2:3], at.at[:, :, pl.ds(there, L)], went.at[2 * k + 1]))
+    for copy in copies:
+        copy.start()
+    for copy in copies:
+        copy.wait()
 
 
 def shard_factor(packed, k, q):
@@ -235,7 +227,8 @@
 
 
 def inside_kernel(length, me, pw, pr, pd, pc, aw, ar, ad, ac, *refs):
-    chunks, (y_out, dx_out, dr_out, dw_out, adw, z_out, x, zs) = refs[:GROUP], refs[GROUP:]
+    chunks, outs = refs[:GROUP], refs[GROUP : 2 * GROUP]
+    y_out, dx_out, dr_out, dw_out, adw, z_out, x, zs, full = refs[2 * GROUP :]
     b = pl.program_id(0)
     answer = b == 2
     write = jnp.where(answer, aw[0], pw[0])
@@ -268,7 +261,7 @@
         y = jnp.where(first, ys[0], ys[1])
         dx = jnp.concatenate(dxs, axis=0).T
         y_out[0, :, lanes] = y.astype(BF16)
-        dx_out[0, :, lanes] = dx.astype(BF16)
+        full[:, lanes] = dx.astype(BF16)
         zs[:, lanes] = cs * y - xs.astype(F32) * dx
     z_out[0] = head_sums(zs[...])
     grad = grad.astype(BF16)
@@ -277,35 +270,30 @@
 
     @pl.when(b < 2)
     def _():
+        dx_out[0] = full[...]
         dw_out[0] = dw
 
     @pl.when(answer)
     def _():
         adw[0] = dw.astype(BF16)
+        for k in range(GROUP):
+            there = pl.multiple_of((me[0] ^ k) * ROWS, ROWS)
+            outs[k][0] = full[pl.ds(there, ROWS), :]
 
 
 def token_kernel(me, m2, pw, pd, dxi, dwi, *refs):
-    chunks, outs = refs[:GROUP], refs[GROUP : 2 * GROUP]
-    pdw, z, closing, ends, full, x = refs[2 * GROUP :]
-    b = pl.program_id(0)
-
-    @pl.when(b < 2)
-    def _():
-        gathered(m2, ends)
-        assembled(me, chunks, x)
-        xs = x[...].astype(F32)
-        to_close = closing_weight(pd[0])
-        tail = nn(pw[0], ends[...]) * to_close
-        full[...] = (dxi[0].astype(F32) + tail).astype(BF16)
-        pdw[0] = (dwi[0] + nt((xs * to_close).astype(BF16), ends[...])).astype(BF16)
-        tail = tail * xs
-        closing[0] = jnp.broadcast_to(jnp.sum(tail, axis=0, keepdims=True), (8, L))
-        z[0] = head_sums(tail)
-
-    @pl.when(b == 2)
-    def _():
-        full[...] = dxi[0]
-
+    chunks, outs = refs[:GROUP], refs[2 * GROUP : 3 * GROUP]
+    pdw, z, closing, ends, full, x = refs[3 * GROUP :]
+    gathered(m2, ends)
+    assembled(me, chunks, x)
+    xs = x[...].astype(F32)
+    to_close = closing_weight(pd[0])
+    tail = nn(pw[0], ends[...]) * to_close
+    full[...] = (dxi[0].astype(F32) + tail).astype(BF16)
+    pdw[0] = (dwi[0] + nt((xs * to_close).astype(BF16), ends[...])).astype(BF16)
+    tail = tail * xs
+    closing[0] = jnp.broadcast_to(jnp.sum(tail, axis=0, keepdims=True), (8, L))
+    z[0] = head_sums(tail)
     for k in range(GROUP):
         there = pl.multiple_of((me[0] ^ k) * ROWS, ROWS)
         outs[k][0] = full[pl.ds(there, ROWS), :]
@@ -327,7 +315,7 @@
     dr = dri[0] + nt((cot * growth).astype(BF16), start[...])
     zs = zi[0] + head_sums(cot * outside) - jnp.where(answer, 0.0, z[0])
     tri = lower()
-    dd = sum(tn(part, tri) for part in terms(zs))
+    dd = sum(nn(part, tri) for part in terms(zs))
 
     @pl.when(b < 2)
     def _():
@@ -408,24 +396,31 @@
     answer_side = [one(B, N), one(H, B), one(B, L)]
     (m1,) = call(
         reach_kernel,
-        3,
-        [SMEM, *prompt_side, *answer_side],
-        [(column(3 * HALF + N, lambda b: 0), shape((B, 3 * HALF + N)))],
+        1,
+        [SMEM] + [ANY] * 6,
+        [(ANY, shape((B, 3 * HALF + N)))],
         (length, pr, pd, pc, ar, ad, ac),
-        (pltpu.VMEM((8, L), F32),),
+        (
+            pltpu.VMEM((3, B, N), BF16),
+            pltpu.VMEM((3, H, B), F32),
+            pltpu.VMEM((3, B, L), BF16),
+            pltpu.VMEM((B, 3 * HALF + N), BF16),
+            pltpu.VMEM((8, L), F32),
+            pltpu.SemaphoreType.DMA((9,)),
+            pltpu.SemaphoreType.DMA((4,)),
+        ),
     )
     m1 = transposed(m1)
     cut = call(
         split_kernel,
         1,
         [SMEM, ANY, ANY],
-        [(ANY, shape((3, ROWS, L)))] * GROUP,
+        [(VMEM, shape((3, ROWS, L)))] * GROUP,
         (me, pt, at),
         (
-            pltpu.VMEM((GROUP, 3, ROWS, L), BF16),
             pltpu.SemaphoreType.DMA((2 * GROUP,)),
-            pltpu.SemaphoreType.DMA((GROUP,)),
         ),
+        limit=4 << 20,
     )
     cut = exchange(cut)
     m2, factors = call(
@@ -437,6 +432,7 @@
             (pl.BlockSpec((2 * SHARDS, HALF), lambda q: (0, 0)), shape((2 * SHARDS, HALF), F32)),
         ],
         (sizes, m1, m1, m1),
+        limit=8 << 20,
     )
     (m2,) = call(
         local_kernel,
@@ -446,53 +442,44 @@
         (me, m2, pw, pd, *cut),
         (block,),
         alias={1: 0},
+        limit=12 << 20,
     )
     m2 = transposed(m2)
-    yi, dxi, dri, dwi, adw, zi = call(
+    made = call(
         inside_kernel,
         3,
         [SMEM, SMEM, own(B, N), *prompt_side, one(B, N), *answer_side, *pieces],
         [
+            *[(pl.BlockSpec((1, ROWS, L), lambda b: (2, 0, 0)), shape((3, ROWS, L)))] * GROUP,
             (each(B, L), shape((3, B, L))),
-            (each(B, L), shape((3, B, L))),
+            (own(B, L), shape((2, B, L))),
             (each(B, N), shape((3, B, N), F32)),
             (own(B, N), shape((2, B, N), F32)),
             (one(B, N), shape((1, B, N))),
-            (each(B, H), shape((3, B, H), F32)),
+            (each(H, B), shape((3, H, B), F32)),
         ],
         (length, me, pw, pr, pd, pc, aw, ar, ad, ac, *cut),
-        (block, pltpu.VMEM((B, L), F32)),
+        (block, pltpu.VMEM((B, L), F32), block),
         8e9,
     )
+    yi, dxi, dri, dwi, adw, zi = made[GROUP:]
     (m3,) = call(
-        start_kernel,
-        1,
-        [SMEM, VMEM, VMEM],
-        [(VMEM, shape((B, 3 * HALF)))],
-        (sizes, factors, m2),
-        limit=4 << 20,
+        start_kernel, 1, [SMEM, VMEM, VMEM], [(VMEM, shape((B, 3 * HALF)))], (sizes, factors, m2), limit=4 << 20
     )
     m3 = transposed(m3)
     made = call(
         token_kernel,
-        3,
-        [
-            SMEM,
-            column(HALF, lambda b: jnp.minimum(b, 1)),
-            own(B, N),
-            own(H, B),
-            each(B, L),
-            own(B, N),
-            *[own(ROWS, L)] * GROUP,
-        ],
+        2,
+        [SMEM, column(HALF, lambda q: q), each(B, N), each(H, B), each(B, L), each(B, N), *pieces, *[ANY] * GROUP],
         [
             *chunk,
-            (own(B, N), shape((2, B, N))),
-            (own(B, H), shape((2, B, H), F32)),
-            (own(8, L), shape((2, 8, L), F32)),
+            (each(B, N), shape((2, B, N))),
+            (each(H, B), shape((2, H, B), F32)),
+            (each(8, L), shape((2, 8, L), F32)),
         ],
-        (me, m2, pw, pd, dxi, dwi, *cut),
+        (me, m2, pw, pd, dxi, dwi, *cut, *made[:GROUP]),
         (state, block, block),
+        alias={6 + GROUP + k: k for k in range(GROUP)},
     )
     pdw, z, closing = made[GROUP:]
     back = exchange(made[:GROUP])
@@ -507,8 +494,8 @@
             *answer_side,
             each(B, L),
             each(B, N),
-            each(B, H),
-            own(B, H),
+            each(H, B),
+            own(H, B),
             own(8, L),
         ],
         [
@@ -525,14 +512,13 @@
     pdx, adx = call(
         join_kernel,
         1,
-        [SMEM] + [ANY] * GROUP,
+        [SMEM] + [VMEM] * GROUP,
         [(ANY, shape((2, ROWS, GROUP * L))), (ANY, shape((1, ROWS, GROUP * L)))],
         (me, *back),
         (
-            pltpu.VMEM((GROUP, 3, ROWS, L), BF16),
-            pltpu.SemaphoreType.DMA((GROUP,)),
             pltpu.SemaphoreType.DMA((2 * GROUP,)),
         ),
+        limit=4 << 20,
     )
     return py, pdx, pdw, pdr, pdd, ay, adx, adw, adr, add
 

time: 128 us -> 122 us (0.953)
  Pallas kernels: 41.9 us -> 35.5 us
  waiting for transfers between devices: 23.6 us -> 25.8 us
  local copies, waits for them, and re-layouts: 3.24 us -> 1.86 us
    pallas_call x9, Pallas kernels: 41.9 us -> 35.5 us  [call(): pl.pallas_call(kernel, grid=(steps,), in_specs=ins, out_specs=[spec for s...]
    unnamed x38 -> x32, local copies, waits for them, and re-layouts: 3.24 us -> 1.86 us
    all_to_all x2, waiting for transfers between devices: 0.11 us -> 1.41 us  [transposed(): lax.all_to_all(message, 'seq', split_axis=0, concat_axis=0, tiled=True)]
  transfers between devices with their start and end apart: 16 -> 16, of which waited for: 8 -> 8; matrix products, arithmetic and copies ran while one was open for 0% -> 0% of each run, Pallas kernels for 18% -> 16%
where the time goes in v2:
time: 122 us; the launch traced here: 121 us
  Pallas kernels  35.5 us (29%)
  starting transfers between devices  33.5 us (27%)
  waiting for transfers between devices  25.8 us (21%)
  blocking collectives  23.3 us (19%)
  local copies, waits for them, and re-layouts  1.86 us (2%)
  between operations  1.52 us (1%)
    pallas_call x9, Pallas kernels, call(): pl.pallas_call(kernel, grid=(steps,), in_specs=ins, out_specs=[spec for s...  35.5 us
    ppermute x14, waiting for transfers between devices, exchange(): lax.ppermute(chunks[k], 'head', [(i, i ^ k) for i in range(GROUP)])  24.4 us
    all_to_all x1, blocking collectives, transposed(): lax.all_to_all(message, 'seq', split_axis=0, concat_axis=0, tiled=True)  23.3 us
    ppermute x14, starting transfers between devices, exchange(): lax.ppermute(chunks[k], 'head', [(i, i ^ k) for i in range(GROUP)])  21.1 us
    all_to_all x2, starting transfers between devices, transposed(): lax.all_to_all(message, 'seq', split_axis=0, concat_axis=0, tiled=True)  12.3 us
  transfers between devices with their start and end apart: 16, of which 8 were waited for; matrix products, arithmetic and copies ran while one was open for 0% of the time, Pallas kernels for 16%

profile of v2, /device:TPU:1, one launch (start us, length us, event | category | flops | bytes accessed | tf_op | source)
XLA Modules:
  0.0 121.5 jit_solution(15221288695958327315)
XLA Ops:
  1.3 4.3 %shard_map.195 = bf16[256,1664]{1,0:T(8,128)(2,1)} custom-call(s32[1]{0:T(128)S(6)} %copy.40.length, bf16[2,256,128]{2,1,0:T(8,128)(2,1)} %pr.5, f32[2,16,256]{2,1,0:T(8,128)} %pd.9, bf16[2,256,1024]{2,1,0:T(8,128)(2,1)} %pc.5, bf16[1,256,128]{2,1,0:T(8,128)(2,1)} %ar.5, f32[1,16,256]{2,1,0:T(8,128)} %ad.5, bf16[1,256,1024]{2,1,0:T(8,128)(2,1)} %ac.5), custom_call_target="tpu_custom_call" | custom-call | flops 1000000000 | bytes 4000000 | tf_op jit(solution)/shard_map/pallas_call | solution.py:364
  5.6 0.0 copy-start.12
  5.6 0.0 copy-start.13
  5.6 8.7 %all-to-all-start = ((bf16[16,16,1664]{2,1,0:T(8,128)(2,1)}), bf16[16,16,1664]{2,1,0:T(8,128)(2,1)S(1)}, u32[]{:S(2)}, u32[]{:S(2)}) async-start(bf16[16,16,1664]{2,1,0:T(8,128)(2,1)} %bitcast.15), calls=%async_computation | async-start | bytes 1703936 | tf_op jit(solution)/shard_map/all_to_all | solution.py:386
  14.4 0.0 copy-done.12
  14.4 0.0 copy-done.13
  14.4 0.0 copy-start.14
  14.4 1.2 shard_map.197
  15.6 0.0 copy-start.1
  15.7 1.0 collective-permute-start
  16.7 1.2 collective-permute-start.1
  17.9 0.5 collective-permute-start.2
  18.4 2.7 %collective-permute-start.3 = (bf16[3,32,1024]{2,1,0:T(8,128)(2,1)S(1)}, bf16[3,32,1024]{2,1,0:T(8,128)(2,1)S(1)}, u32[]{:S(2)}, u32[]{:S(2)}) collective-permute-start(bf16[3,32,1024]{2,1,0:T(8,128)(2,1)S(1)} %get-tuple-element.58), channel_id=1, source_target_pairs={{0,4},{1,5},{2,6},{3,7},{4,0},{5,1},{6,2},{7,3},{8,12},{9,13},{10,... | collective-permute-start | bytes 589832 | tf_op jit(solution)/shard_map/ppermute | solution.py:381
  21.2 0.5 collective-permute-start.4
  21.7 0.0 collective-permute-done.refs_1_
  21.7 2.5 %collective-permute-start.5 = (bf16[3,32,1024]{2,1,0:T(8,128)(2,1)S(1)}, bf16[3,32,1024]{2,1,0:T(8,128)(2,1)S(1)}, u32[]{:S(2)}, u32[]{:S(2)}) collective-permute-start(bf16[3,32,1024]{2,1,0:T(8,128)(2,1)S(1)} %get-tuple-element.60), channel_id=1, source_target_pairs={{0,6},{1,7},{2,4},{3,5},{4,2},{5,3},{6,0},{7,1},{8,14},{9,15},{10,... | collective-permute-start | bytes 589832 | tf_op jit(solution)/shard_map/ppermute | solution.py:381
  24.2 0.0 collective-permute-done.1.refs_2_
  24.2 2.7 %collective-permute-start.6 = (bf16[3,32,1024]{2,1,0:T(8,128)(2,1)S(1)}, bf16[3,32,1024]{2,1,0:T(8,128)(2,1)S(1)}, u32[]{:S(2)}, u32[]{:S(2)}) collective-permute-start(bf16[3,32,1024]{2,1,0:T(8,128)(2,1)S(1)} %get-tuple-element.61), channel_id=1, source_target_pairs={{0,7},{1,6},{2,5},{3,4},{4,3},{5,2},{6,1},{7,0},{8,15},{9,14},{10,... | collective-permute-start | bytes 589832 | tf_op jit(solution)/shard_map/ppermute | solution.py:381
  26.9 1.4 %all-to-all-done = bf16[16,16,1664]{2,1,0:T(8,128)(2,1)S(1)} async-done(((bf16[16,16,1664]{2,1,0:T(8,128)(2,1)}), bf16[16,16,1664]{2,1,0:T(8,128)(2,1)S(1)}, u32[]{:S(2)}, u32[]{:S(2)}) %all-to-all-start) | async-done | bytes 852000 | tf_op jit(solution)/shard_map/all_to_all | solution.py:386
  28.3 0.0 copy-done.14
  28.3 0.9 shard_map.196
  29.2 0.0 collective-permute-done.2.refs_3_
  29.2 0.0 copy-start.4
  29.2 4.5 %collective-permute-done.3.refs_4_ = bf16[3,32,1024]{2,1,0:T(8,128)(2,1)S(1)} collective-permute-done((bf16[3,32,1024]{2,1,0:T(8,128)(2,1)S(1)}, bf16[3,32,1024]{2,1,0:T(8,128)(2,1)S(1)}, u32[]{:S(2)}, u32[]{:S(2)}) %collective-permute-start.3) | collective-permute-done | bytes 196640 | tf_op jit(solution)/shard_map/ppermute | solution.py:381
  33.7 4.5 %collective-permute-done.4.refs_5_ = bf16[3,32,1024]{2,1,0:T(8,128)(2,1)S(1)} collective-permute-done((bf16[3,32,1024]{2,1,0:T(8,128)(2,1)S(1)}, bf16[3,32,1024]{2,1,0:T(8,128)(2,1)S(1)}, u32[]{:S(2)}, u32[]{:S(2)}) %collective-permute-start.4) | collective-permute-done | bytes 196640 | tf_op jit(solution)/shard_map/ppermute | solution.py:381
  38.3 0.0 collective-permute-done.5.refs_6_
  38.3 3.9 %collective-permute-done.6.refs_7_ = bf16[3,32,1024]{2,1,0:T(8,128)(2,1)S(1)} collective-permute-done((bf16[3,32,1024]{2,1,0:T(8,128)(2,1)S(1)}, bf16[3,32,1024]{2,1,0:T(8,128)(2,1)S(1)}, u32[]{:S(2)}, u32[]{:S(2)}) %collective-permute-start.6) | collective-permute-done | bytes 196640 | tf_op jit(solution)/shard_map/ppermute | solution.py:381
  42.2 0.0 copy-done.1
  42.2 0.0 copy-done.2
  42.2 0.0 copy-done.3
  42.2 0.0 copy-done.9
  42.2 0.0 copy-done.10
  42.2 1.9 %shard_map.198 = bf16[256,2048]{1,0:T(8,128)(2,1)S(1)} custom-call(s32[1]{0:T(128)} %bitcast.me, bf16[256,2048]{1,0:T(8,128)(2,1)S(1)} %get-tuple-element.53.message, bf16[2,256,128]{2,1,0:T(8,128)(2,1)S(1)} %copy-done.9, f32[2,16,256]{2,1,0:T(8,128)S(1)} %copy-done.10, ...), custom_call_target="tpu_custom_call", output_to_operand_aliasing={{}: (1, {})} | custom-call | flops 1000000000 | bytes 4000000 | tf_op jit(solution)/shard_map/pallas_call | solution.py:364
  44.1 0.0 copy-done.4
  44.1 0.0 copy-done.5
  44.1 0.0 copy-done.6
  44.1 0.0 copy-done.7
  44.1 0.0 copy-done.8
  44.1 23.3 %all_to_all.33 = bf16[16,16,2048]{2,1,0:T(8,128)(2,1)S(1)} all-to-all(bf16[16,16,2048]{2,1,0:T(8,128)(2,1)S(1)} %bitcast.10), channel_id=1, replica_groups=mesh['seq'=16,'head'=8] {'seq'}, dimensions={0} | all-to-all | bytes 2097152 | tf_op jit(solution)/shard_map/all_to_all | solution.py:386
  67.5 1.6 %shard_map.199 = bf16[256,1536]{1,0:T(8,128)(2,1)} custom-call(s32[2]{0:T(128)S(1)} %copy-done.14, f32[32,512]{1,0:T(8,128)S(1)} %get-tuple-element.62.factors, bf16[256,2048]{1,0:T(8,128)(2,1)S(1)} %bitcast.7), custom_call_target="tpu_custom_call" | custom-call | flops 1000000000 | bytes 4000000 | tf_op jit(solution)/shard_map/pallas_call | solution.py:364
  69.1 0.0 copy-done
  69.1 3.6 %all-to-all-start.2 = ((bf16[16,16,1536]{2,1,0:T(8,128)(2,1)}), bf16[16,16,1536]{2,1,0:T(8,128)(2,1)S(1)}, u32[]{:S(2)}, u32[]{:S(2)}) async-start(bf16[16,16,1536]{2,1,0:T(8,128)(2,1)} %bitcast.5), calls=%async_computation.2 | async-start | bytes 1572864 | tf_op jit(solution)/shard_map/all_to_all | solution.py:386
  72.7 11.4 %shard_map.200 = (bf16[3,32,1024]{2,1,0:T(8,128)(2,1)}, bf16[3,32,1024]{2,1,0:T(8,128)(2,1)}, bf16[3,32,1024]{2,1,0:T(8,128)(2,1)}, bf16[3,32,1024]{2,1,0:T(8,12...) custom-call(s32[1]{0:T(128)S(6)} %copy.40.length, ...), custom_call_target="tpu_custom_call" | custom-call | flops 8000000000 | bytes 4000000 | tf_op jit(solution)/shard_map/pallas_call | solution.py:364
  84.1 4.8 %shard_map.201 = (bf16[3,32,1024]{2,1,0:T(8,128)(2,1)}, bf16[3,32,1024]{2,1,0:T(8,128)(2,1)}, bf16[3,32,1024]{2,1,0:T(8,128)(2,1)}, bf16[3,32,1024]{2,1,0:T(8,12...) custom-call(s32[1]{0:T(128)} %bitcast.me, ...), custom_call_target="tpu_custom_call", output_to_operand_aliasing={{0}: (14, {}), {1}: (15, {}), {2}: (16, {}), {3}: (17, {}),... | custom-call | flops 1000000000 | bytes 4000000 | tf_op jit(solution)/shard_map/pallas_call | solution.py:364
  88.9 1.6 %collective-permute-start.10 = (bf16[3,32,1024]{2,1,0:T(8,128)(2,1)}, bf16[3,32,1024]{2,1,0:T(8,128)(2,1)S(1)}, u32[]{:S(2)}, u32[]{:S(2)}) collective-permute-start(bf16[3,32,1024]{2,1,0:T(8,128)(2,1)} %get-tuple-element.83), channel_id=1, source_target_pairs={{0,4},{1,5},{2,6},{3,7},{4,0},{5,1},{6,2},{7,3},{8,12},{9,13},{10,... | collective-permute-start | bytes 589832 | tf_op jit(solution)/shard_map/ppermute | solution.py:381
  90.5 3.2 %collective-permute-start.11 = (bf16[3,32,1024]{2,1,0:T(8,128)(2,1)}, bf16[3,32,1024]{2,1,0:T(8,128)(2,1)S(1)}, u32[]{:S(2)}, u32[]{:S(2)}) collective-permute-start(bf16[3,32,1024]{2,1,0:T(8,128)(2,1)} %get-tuple-element.84), channel_id=1, source_target_pairs={{0,5},{1,4},{2,7},{3,6},{4,1},{5,0},{6,3},{7,2},{8,13},{9,12},{10,... | collective-permute-start | bytes 589832 | tf_op jit(solution)/shard_map/ppermute | solution.py:381
  93.7 2.5 %collective-permute-start.12 = (bf16[3,32,1024]{2,1,0:T(8,128)(2,1)}, bf16[3,32,1024]{2,1,0:T(8,128)(2,1)S(1)}, u32[]{:S(2)}, u32[]{:S(2)}) collective-permute-start(bf16[3,32,1024]{2,1,0:T(8,128)(2,1)} %get-tuple-element.85), channel_id=1, source_target_pairs={{0,6},{1,7},{2,4},{3,5},{4,2},{5,3},{6,0},{7,1},{8,14},{9,15},{10,... | collective-permute-start | bytes 589832 | tf_op jit(solution)/shard_map/ppermute | solution.py:381
  96.2 0.0 collective-permute-start.13
  96.2 0.6 collective-permute-start.7
  96.8 0.0 collective-permute-done.10.refs_4_
  96.8 0.0 collective-permute-start.8
  96.8 4.9 %collective-permute-done.11.refs_5_ = bf16[3,32,1024]{2,1,0:T(8,128)(2,1)S(1)} collective-permute-done((bf16[3,32,1024]{2,1,0:T(8,128)(2,1)}, bf16[3,32,1024]{2,1,0:T(8,128)(2,1)S(1)}, u32[]{:S(2)}, u32[]{:S(2)}) %collective-permute-start.11) | collective-permute-done | bytes 196640 | tf_op jit(solution)/shard_map/ppermute | solution.py:381
  101.7 2.0 %collective-permute-start.9 = (bf16[3,32,1024]{2,1,0:T(8,128)(2,1)}, bf16[3,32,1024]{2,1,0:T(8,128)(2,1)S(1)}, u32[]{:S(2)}, u32[]{:S(2)}) collective-permute-start(bf16[3,32,1024]{2,1,0:T(8,128)(2,1)} %get-tuple-element.82), channel_id=1, source_target_pairs={{0,3},{1,2},{2,1},{3,0},{4,7},{5,6},{6,5},{7,4},{8,11},{9,10},{10,... | collective-permute-start | bytes 589832 | tf_op jit(solution)/shard_map/ppermute | solution.py:381
  103.7 2.3 %collective-permute-done.12.refs_6_ = bf16[3,32,1024]{2,1,0:T(8,128)(2,1)S(1)} collective-permute-done((bf16[3,32,1024]{2,1,0:T(8,128)(2,1)}, bf16[3,32,1024]{2,1,0:T(8,128)(2,1)S(1)}, u32[]{:S(2)}, u32[]{:S(2)}) %collective-permute-start.12) | collective-permute-done | bytes 196640 | tf_op jit(solution)/shard_map/ppermute | solution.py:381
  106.0 4.2 %collective-permute-done.13.refs_7_ = bf16[3,32,1024]{2,1,0:T(8,128)(2,1)S(1)} collective-permute-done((bf16[3,32,1024]{2,1,0:T(8,128)(2,1)}, bf16[3,32,1024]{2,1,0:T(8,128)(2,1)S(1)}, u32[]{:S(2)}, u32[]{:S(2)}) %collective-permute-start.13) | collective-permute-done | bytes 196640 | tf_op jit(solution)/shard_map/ppermute | solution.py:381
  110.2 0.0 collective-permute-done.7.refs_1_
  110.2 0.0 collective-permute-done.8.refs_2_
  110.2 0.1 collective-permute-done.9.refs_3_
  110.3 0.9 copy-done.11
  111.2 1.3 %shard_map.203 = (bf16[2,32,8192]{2,1,0:T(8,128)(2,1)}, bf16[1,32,8192]{2,1,0:T(8,128)(2,1)}) custom-call(s32[1]{0:T(128)} %bitcast.me, bf16[3,32,1024]{2,1,0:T(8,128)(2,1)S(1)} %copy-done.11, bf16[3,32,1024]{2,1,0:T(8,128)(2,1)S(1)} %collective-permute-done.7.refs_1_, bf16[3,32,1024]{2,1,0:T(8,128)(2,1)S(1)} %collective-permute-done.8.refs_2_, ...), custom_call_target="tpu_custom_call" | custom-call | flops 1000000000 | bytes 4000000 | tf_op jit(solution)/shard_map/pallas_call | solution.py:364
  112.5 0.0 all-to-all-done.2
  112.5 0.0 copy-start.15
  112.5 0.9 copy-done.15
  113.4 8.1 %shard_map.202 = (bf16[2,256,1024]{2,1,0:T(8,128)(2,1)}, bf16[2,256,128]{2,1,0:T(8,128)(2,1)}, f32[2,16,256]{2,1,0:T(8,128)}, bf16[1,256,1024]{2,1,0:T(8,128)(2,...) custom-call(s32[1]{0:T(128)S(6)} %copy.40.length, bf16[256,2048]{1,0:T(8,128)(2,1)} %bitcast.9, ...), custom_call_target="tpu_custom_call" | custom-call | flops 1000000000 | bytes 4000000 | tf_op jit(solution)/shard_map/pallas_call | solution.py:364
  (10 shorter events, 0.0 us)
Async XLA Ops:
  5.6 8.8 %copy-start.12 = (bf16[2,32,8192]{2,1,0:T(8,128)(2,1)S(1)}, bf16[2,32,8192]{2,1,0:T(8,128)(2,1)}, u32[]{:S(2)}) copy-start(bf16[2,32,8192]{2,1,0:T(8,128)(2,1)} %pt.1) | copy-start | bytes 3145732
  5.6 8.8 %copy-start.13 = (bf16[1,32,8192]{2,1,0:T(8,128)(2,1)S(1)}, bf16[1,32,8192]{2,1,0:T(8,128)(2,1)}, u32[]{:S(2)}) copy-start(bf16[1,32,8192]{2,1,0:T(8,128)(2,1)} %at.1) | copy-start | bytes 1572868
  5.6 22.7 %all-to-all-start = ((bf16[16,16,1664]{2,1,0:T(8,128)(2,1)}), bf16[16,16,1664]{2,1,0:T(8,128)(2,1)S(1)}, u32[]{:S(2)}, u32[]{:S(2)}) async-start(bf16[16,16,1664]{2,1,0:T(8,128)(2,1)} %bitcast.15), calls=%async_computation | async-start | bytes 1703936 | tf_op jit(solution)/shard_map/all_to_all | solution.py:386
  14.4 13.9 %copy-start.14 = (s32[2]{0:T(128)S(1)}, s32[2]{0:T(128)}, u32[]{:S(2)}) copy-start(s32[2]{0:T(128)} %sizes.3) | copy-start | bytes 28
  15.6 26.5 %copy-start.1 = (bf16[3,32,1024]{2,1,0:T(8,128)(2,1)}, bf16[3,32,1024]{2,1,0:T(8,128)(2,1)S(1)}, u32[]{:S(2)}) copy-start(bf16[3,32,1024]{2,1,0:T(8,128)(2,1)S(1)} %get-tuple-element.54.refs_0_) | copy-start | bytes 589828
  15.7 6.0 %collective-permute-start = (bf16[3,32,1024]{2,1,0:T(8,128)(2,1)S(1)}, bf16[3,32,1024]{2,1,0:T(8,128)(2,1)S(1)}, u32[]{:S(2)}, u32[]{:S(2)}) collective-permute-start(bf16[3,32,1024]{2,1,0:T(8,128)(2,1)S(1)} %get-tuple-element.55), channel_id=1, source_target_pairs={{0,1},{1,0},{2,3},{3,2},{4,5},{5,4},{6,7},{7,6},{8,9},{9,8},{10,11... | collective-permute-start | bytes 589832 | tf_op jit(solution)/shard_map/ppermute | solution.py:381
  16.7 7.5 %collective-permute-start.1 = (bf16[3,32,1024]{2,1,0:T(8,128)(2,1)S(1)}, bf16[3,32,1024]{2,1,0:T(8,128)(2,1)S(1)}, u32[]{:S(2)}, u32[]{:S(2)}) collective-permute-start(bf16[3,32,1024]{2,1,0:T(8,128)(2,1)S(1)} %get-tuple-element.56), channel_id=1, source_target_pairs={{0,2},{1,3},{2,0},{3,1},{4,6},{5,7},{6,4},{7,5},{8,10},{9,11},{10,... | collective-permute-start | bytes 589832 | tf_op jit(solution)/shard_map/ppermute | solution.py:381
  17.9 11.3 %collective-permute-start.2 = (bf16[3,32,1024]{2,1,0:T(8,128)(2,1)}, bf16[3,32,1024]{2,1,0:T(8,128)(2,1)S(1)}, u32[]{:S(2)}, u32[]{:S(2)}) collective-permute-start(bf16[3,32,1024]{2,1,0:T(8,128)(2,1)} %get-tuple-element.57), channel_id=1, source_target_pairs={{0,3},{1,2},{2,1},{3,0},{4,7},{5,6},{6,5},{7,4},{8,11},{9,10},{10,... | collective-permute-start | bytes 589832 | tf_op jit(solution)/shard_map/ppermute | solution.py:381
  18.4 15.3 %collective-permute-start.3 = (bf16[3,32,1024]{2,1,0:T(8,128)(2,1)S(1)}, bf16[3,32,1024]{2,1,0:T(8,128)(2,1)S(1)}, u32[]{:S(2)}, u32[]{:S(2)}) collective-permute-start(bf16[3,32,1024]{2,1,0:T(8,128)(2,1)S(1)} %get-tuple-element.58), channel_id=1, source_target_pairs={{0,4},{1,5},{2,6},{3,7},{4,0},{5,1},{6,2},{7,3},{8,12},{9,13},{10,... | collective-permute-start | bytes 589832 | tf_op jit(solution)/shard_map/ppermute | solution.py:381
  21.2 17.1 %collective-permute-start.4 = (bf16[3,32,1024]{2,1,0:T(8,128)(2,1)S(1)}, bf16[3,32,1024]{2,1,0:T(8,128)(2,1)S(1)}, u32[]{:S(2)}, u32[]{:S(2)}) collective-permute-start(bf16[3,32,1024]{2,1,0:T(8,128)(2,1)S(1)} %get-tuple-element.59), channel_id=1, source_target_pairs={{0,5},{1,4},{2,7},{3,6},{4,1},{5,0},{6,3},{7,2},{8,13},{9,12},{10,... | collective-permute-start | bytes 589832 | tf_op jit(solution)/shard_map/ppermute | solution.py:381
  21.7 20.5 %copy-start.2 = (bf16[3,32,1024]{2,1,0:T(8,128)(2,1)}, bf16[3,32,1024]{2,1,0:T(8,128)(2,1)S(1)}, u32[]{:S(2)}) copy-start(bf16[3,32,1024]{2,1,0:T(8,128)(2,1)S(1)} %collective-permute-done.refs_1_) | copy-start | bytes 589828
  21.7 16.6 %collective-permute-start.5 = (bf16[3,32,1024]{2,1,0:T(8,128)(2,1)S(1)}, bf16[3,32,1024]{2,1,0:T(8,128)(2,1)S(1)}, u32[]{:S(2)}, u32[]{:S(2)}) collective-permute-start(bf16[3,32,1024]{2,1,0:T(8,128)(2,1)S(1)} %get-tuple-element.60), channel_id=1, source_target_pairs={{0,6},{1,7},{2,4},{3,5},{4,2},{5,3},{6,0},{7,1},{8,14},{9,15},{10,... | collective-permute-start | bytes 589832 | tf_op jit(solution)/shard_map/ppermute | solution.py:381
  24.2 18.0 %copy-start.3 = (bf16[3,32,1024]{2,1,0:T(8,128)(2,1)}, bf16[3,32,1024]{2,1,0:T(8,128)(2,1)S(1)}, u32[]{:S(2)}) copy-start(bf16[3,32,1024]{2,1,0:T(8,128)(2,1)S(1)} %collective-permute-done.1.refs_2_) | copy-start | bytes 589828
  24.2 18.0 %collective-permute-start.6 = (bf16[3,32,1024]{2,1,0:T(8,128)(2,1)S(1)}, bf16[3,32,1024]{2,1,0:T(8,128)(2,1)S(1)}, u32[]{:S(2)}, u32[]{:S(2)}) collective-permute-start(bf16[3,32,1024]{2,1,0:T(8,128)(2,1)S(1)} %get-tuple-element.61), channel_id=1, source_target_pairs={{0,7},{1,6},{2,5},{3,4},{4,3},{5,2},{6,1},{7,0},{8,15},{9,14},{10,... | collective-permute-start | bytes 589832 | tf_op jit(solution)/shard_map/ppermute | solution.py:381
  28.3 13.9 %copy-start.9 = (bf16[2,256,128]{2,1,0:T(8,128)(2,1)S(1)}, bf16[2,256,128]{2,1,0:T(8,128)(2,1)}, u32[]{:S(2)}) copy-start(bf16[2,256,128]{2,1,0:T(8,128)(2,1)} %pw.5) | copy-start | bytes 393220
  28.3 13.9 %copy-start.10 = (f32[2,16,256]{2,1,0:T(8,128)S(1)}, f32[2,16,256]{2,1,0:T(8,128)}, u32[]{:S(2)}) copy-start(f32[2,16,256]{2,1,0:T(8,128)} %pd.9) | copy-start | bytes 98308
  29.2 14.9 %copy-start.4 = (bf16[3,32,1024]{2,1,0:T(8,128)(2,1)}, bf16[3,32,1024]{2,1,0:T(8,128)(2,1)S(1)}, u32[]{:S(2)}) copy-start(bf16[3,32,1024]{2,1,0:T(8,128)(2,1)S(1)} %collective-permute-done.2.refs_3_) | copy-start | bytes 589828
  33.7 10.4 %copy-start.5 = (bf16[3,32,1024]{2,1,0:T(8,128)(2,1)}, bf16[3,32,1024]{2,1,0:T(8,128)(2,1)S(1)}, u32[]{:S(2)}) copy-start(bf16[3,32,1024]{2,1,0:T(8,128)(2,1)S(1)} %collective-permute-done.3.refs_4_) | copy-start | bytes 589828
  38.2 5.9 %copy-start.6 = (bf16[3,32,1024]{2,1,0:T(8,128)(2,1)}, bf16[3,32,1024]{2,1,0:T(8,128)(2,1)S(1)}, u32[]{:S(2)}) copy-start(bf16[3,32,1024]{2,1,0:T(8,128)(2,1)S(1)} %collective-permute-done.4.refs_5_) | copy-start | bytes 589828
  38.3 5.9 %copy-start.7 = (bf16[3,32,1024]{2,1,0:T(8,128)(2,1)}, bf16[3,32,1024]{2,1,0:T(8,128)(2,1)S(1)}, u32[]{:S(2)}) copy-start(bf16[3,32,1024]{2,1,0:T(8,128)(2,1)S(1)} %collective-permute-done.5.refs_6_) | copy-start | bytes 589828
  42.2 2.0 %copy-start.8 = (bf16[3,32,1024]{2,1,0:T(8,128)(2,1)}, bf16[3,32,1024]{2,1,0:T(8,128)(2,1)S(1)}, u32[]{:S(2)}) copy-start(bf16[3,32,1024]{2,1,0:T(8,128)(2,1)S(1)} %collective-permute-done.6.refs_7_) | copy-start | bytes 589828
  67.4 1.6 %copy-start = (bf16[16,16,2048]{2,1,0:T(8,128)(2,1)}, bf16[16,16,2048]{2,1,0:T(8,128)(2,1)S(1)}, u32[]{:S(2)}) copy-start(bf16[16,16,2048]{2,1,0:T(8,128)(2,1)S(1)} %all_to_all.33) | copy-start | bytes 3145732
  69.1 43.4 %all-to-all-start.2 = ((bf16[16,16,1536]{2,1,0:T(8,128)(2,1)}), bf16[16,16,1536]{2,1,0:T(8,128)(2,1)S(1)}, u32[]{:S(2)}, u32[]{:S(2)}) async-start(bf16[16,16,1536]{2,1,0:T(8,128)(2,1)} %bitcast.5), calls=%async_computation.2 | async-start | bytes 1572864 | tf_op jit(solution)/shard_map/all_to_all | solution.py:386
  88.9 7.9 %collective-permute-start.10 = (bf16[3,32,1024]{2,1,0:T(8,128)(2,1)}, bf16[3,32,1024]{2,1,0:T(8,128)(2,1)S(1)}, u32[]{:S(2)}, u32[]{:S(2)}) collective-permute-start(bf16[3,32,1024]{2,1,0:T(8,128)(2,1)} %get-tuple-element.83), channel_id=1, source_target_pairs={{0,4},{1,5},{2,6},{3,7},{4,0},{5,1},{6,2},{7,3},{8,12},{9,13},{10,... | collective-permute-start | bytes 589832 | tf_op jit(solution)/shard_map/ppermute | solution.py:381
  90.5 11.1 %collective-permute-start.11 = (bf16[3,32,1024]{2,1,0:T(8,128)(2,1)}, bf16[3,32,1024]{2,1,0:T(8,128)(2,1)S(1)}, u32[]{:S(2)}, u32[]{:S(2)}) collective-permute-start(bf16[3,32,1024]{2,1,0:T(8,128)(2,1)} %get-tuple-element.84), channel_id=1, source_target_pairs={{0,5},{1,4},{2,7},{3,6},{4,1},{5,0},{6,3},{7,2},{8,13},{9,12},{10,... | collective-permute-start | bytes 589832 | tf_op jit(solution)/shard_map/ppermute | solution.py:381
  93.7 12.3 %collective-permute-start.12 = (bf16[3,32,1024]{2,1,0:T(8,128)(2,1)}, bf16[3,32,1024]{2,1,0:T(8,128)(2,1)S(1)}, u32[]{:S(2)}, u32[]{:S(2)}) collective-permute-start(bf16[3,32,1024]{2,1,0:T(8,128)(2,1)} %get-tuple-element.85), channel_id=1, source_target_pairs={{0,6},{1,7},{2,4},{3,5},{4,2},{5,3},{6,0},{7,1},{8,14},{9,15},{10,... | collective-permute-start | bytes 589832 | tf_op jit(solution)/shard_map/ppermute | solution.py:381
  96.2 14.0 %collective-permute-start.13 = (bf16[3,32,1024]{2,1,0:T(8,128)(2,1)}, bf16[3,32,1024]{2,1,0:T(8,128)(2,1)S(1)}, u32[]{:S(2)}, u32[]{:S(2)}) collective-permute-start(bf16[3,32,1024]{2,1,0:T(8,128)(2,1)} %get-tuple-element.86), channel_id=1, source_target_pairs={{0,7},{1,6},{2,5},{3,4},{4,3},{5,2},{6,1},{7,0},{8,15},{9,14},{10,... | collective-permute-start | bytes 589832 | tf_op jit(solution)/shard_map/ppermute | solution.py:381
  96.2 14.0 %collective-permute-start.7 = (bf16[3,32,1024]{2,1,0:T(8,128)(2,1)}, bf16[3,32,1024]{2,1,0:T(8,128)(2,1)S(1)}, u32[]{:S(2)}, u32[]{:S(2)}) collective-permute-start(bf16[3,32,1024]{2,1,0:T(8,128)(2,1)} %get-tuple-element.80), channel_id=1, source_target_pairs={{0,1},{1,0},{2,3},{3,2},{4,5},{5,4},{6,7},{7,6},{8,9},{9,8},{10,11... | collective-permute-start | bytes 589832 | tf_op jit(solution)/shard_map/ppermute | solution.py:381
  96.8 13.4 %collective-permute-start.8 = (bf16[3,32,1024]{2,1,0:T(8,128)(2,1)}, bf16[3,32,1024]{2,1,0:T(8,128)(2,1)S(1)}, u32[]{:S(2)}, u32[]{:S(2)}) collective-permute-start(bf16[3,32,1024]{2,1,0:T(8,128)(2,1)} %get-tuple-element.81), channel_id=1, source_target_pairs={{0,2},{1,3},{2,0},{3,1},{4,6},{5,7},{6,4},{7,5},{8,10},{9,11},{10,... | collective-permute-start | bytes 589832 | tf_op jit(solution)/shard_map/ppermute | solution.py:381
  101.7 8.6 %collective-permute-start.9 = (bf16[3,32,1024]{2,1,0:T(8,128)(2,1)}, bf16[3,32,1024]{2,1,0:T(8,128)(2,1)S(1)}, u32[]{:S(2)}, u32[]{:S(2)}) collective-permute-start(bf16[3,32,1024]{2,1,0:T(8,128)(2,1)} %get-tuple-element.82), channel_id=1, source_target_pairs={{0,3},{1,2},{2,1},{3,0},{4,7},{5,6},{6,5},{7,4},{8,11},{9,10},{10,... | collective-permute-start | bytes 589832 | tf_op jit(solution)/shard_map/ppermute | solution.py:381
  110.3 0.9 copy-start.11
  112.5 0.9 copy-start.15

commit v3 on v2

--- a/solution.py
+++ b/solution.py
@@ -117,7 +117,8 @@
         x[pl.ds(there, ROWS), :] = chunks[k][0]
 
 
-def reach_kernel(length, pr, pd, pc, ar, ad, ac, out, reads, decays, cots, stage, factors, came, went):
+def reach_kernel(length, pr, pd, pc, ar, ad, ac, out, done, reads, decays, cots, stage, factors, came, went):
+    done[...] = jnp.zeros((8, N), F32)
     coming = []
     for b in range(3):
         group = []
@@ -155,7 +156,7 @@
         copy.wait()
 
 
-def split_kernel(me, pt, at, *refs):
+def split_kernel(me, pt, at, done, *refs):
     outs, came = refs[:GROUP], refs[GROUP]
     copies = []
     for k in range(GROUP):
@@ -394,11 +395,11 @@
     pieces = [each(ROWS, L)] * GROUP
     prompt_side = [own(B, N), own(H, B), own(B, L)]
     answer_side = [one(B, N), one(H, B), one(B, L)]
-    (m1,) = call(
+    m1, done = call(
         reach_kernel,
         1,
         [SMEM] + [ANY] * 6,
-        [(ANY, shape((B, 3 * HALF + N)))],
+        [(ANY, shape((B, 3 * HALF + N))), (VMEM, shape((8, N), F32))],
         (length, pr, pd, pc, ar, ad, ac),
         (
             pltpu.VMEM((3, B, N), BF16),
@@ -414,9 +415,9 @@
     cut = call(
         split_kernel,
         1,
-        [SMEM, ANY, ANY],
+        [SMEM, ANY, ANY, ANY],
         [(VMEM, shape((3, ROWS, L)))] * GROUP,
-        (me, pt, at),
+        (me, pt, at, done),
         (
             pltpu.SemaphoreType.DMA((2 * GROUP,)),
         ),

time: 122 us -> 123 us (level)
  no operation moved by 1% of the time
where the time goes in v3:
time: 123 us; the launch traced here: 122 us
  Pallas kernels  36.1 us (29%)
  starting transfers between devices  33.5 us (27%)
  waiting for transfers between devices  25.8 us (21%)
  blocking collectives  23.3 us (19%)
  local copies, waits for them, and re-layouts  1.87 us (2%)
  between operations  1.54 us (1%)
    pallas_call x9, Pallas kernels, call(): pl.pallas_call(kernel, grid=(steps,), in_specs=ins, out_specs=[spec for s...  36.1 us
    ppermute x14, waiting for transfers between devices, exchange(): lax.ppermute(chunks[k], 'head', [(i, i ^ k) for i in range(GROUP)])  24.4 us
    all_to_all x1, blocking collectives, transposed(): lax.all_to_all(message, 'seq', split_axis=0, concat_axis=0, tiled=True)  23.3 us
    ppermute x14, starting transfers between devices, exchange(): lax.ppermute(chunks[k], 'head', [(i, i ^ k) for i in range(GROUP)])  21.1 us
    all_to_all x2, starting transfers between devices, transposed(): lax.all_to_all(message, 'seq', split_axis=0, concat_axis=0, tiled=True)  12.3 us
  transfers between devices with their start and end apart: 16, of which 8 were waited for; matrix products, arithmetic and copies ran while one was open for 0% of the time, Pallas kernels for 16%

profile of v3, /device:TPU:1, one launch (start us, length us, event | category | flops | bytes accessed | tf_op | source)
XLA Modules:
  0.0 122.1 jit_solution(16627036635459858451)
XLA Ops:
  1.3 4.9 %shard_map.195 = (bf16[256,1664]{1,0:T(8,128)(2,1)}, f32[8,128]{1,0:T(8,128)}) custom-call(s32[1]{0:T(128)S(6)} %copy.40.length, bf16[2,256,128]{2,1,0:T(8,128)(2,1)} %pr.5, f32[2,16,256]{2,1,0:T(8,128)} %pd.9, bf16[2,256,1024]{2,1,0:T(8,128)(2,1)} %pc.5, bf16[1,256,128]{2,1,0:T(8,128)(2,1)} %ar.5, f32[1,16,256]{2,1,0:T(8,128)} %ad.5, bf16[1,256,1024]{2,1,0:T(8,128)(2,1)} %ac.5), custom_call_target="tpu_custom_call" | custom-call | flops 1000000000 | bytes 4000000 | tf_op jit(solution)/shard_map/pallas_call | solution.py:365
  6.2 0.0 copy-start.12
  6.2 0.0 copy-start.13
  6.2 0.0 copy-start.15
  6.2 8.7 %all-to-all-start = ((bf16[16,16,1664]{2,1,0:T(8,128)(2,1)}), bf16[16,16,1664]{2,1,0:T(8,128)(2,1)S(1)}, u32[]{:S(2)}, u32[]{:S(2)}) async-start(bf16[16,16,1664]{2,1,0:T(8,128)(2,1)} %bitcast.15), calls=%async_computation | async-start | bytes 1703936 | tf_op jit(solution)/shard_map/all_to_all | solution.py:387
  15.0 0.0 copy-done.12
  15.0 0.0 copy-done.13
  15.0 0.0 copy-done.15
  15.0 0.0 copy-start.14
  15.0 1.2 shard_map.197
  16.3 0.0 copy-start.1
  16.3 1.0 collective-permute-start
  17.3 1.2 collective-permute-start.1
  18.5 0.5 collective-permute-start.2
  19.0 2.7 %collective-permute-start.3 = (bf16[3,32,1024]{2,1,0:T(8,128)(2,1)S(1)}, bf16[3,32,1024]{2,1,0:T(8,128)(2,1)S(1)}, u32[]{:S(2)}, u32[]{:S(2)}) collective-permute-start(bf16[3,32,1024]{2,1,0:T(8,128)(2,1)S(1)} %get-tuple-element.62), channel_id=1, source_target_pairs={{0,4},{1,5},{2,6},{3,7},{4,0},{5,1},{6,2},{7,3},{8,12},{9,13},{10,... | collective-permute-start | bytes 589832 | tf_op jit(solution)/shard_map/ppermute | solution.py:382
  21.8 0.5 collective-permute-start.4
  22.3 0.0 collective-permute-done.refs_1_
  22.3 2.5 %collective-permute-start.5 = (bf16[3,32,1024]{2,1,0:T(8,128)(2,1)S(1)}, bf16[3,32,1024]{2,1,0:T(8,128)(2,1)S(1)}, u32[]{:S(2)}, u32[]{:S(2)}) collective-permute-start(bf16[3,32,1024]{2,1,0:T(8,128)(2,1)S(1)} %get-tuple-element.64), channel_id=1, source_target_pairs={{0,6},{1,7},{2,4},{3,5},{4,2},{5,3},{6,0},{7,1},{8,14},{9,15},{10,... | collective-permute-start | bytes 589832 | tf_op jit(solution)/shard_map/ppermute | solution.py:382
  24.8 0.0 collective-permute-done.1.refs_2_
  24.8 2.7 %collective-permute-start.6 = (bf16[3,32,1024]{2,1,0:T(8,128)(2,1)S(1)}, bf16[3,32,1024]{2,1,0:T(8,128)(2,1)S(1)}, u32[]{:S(2)}, u32[]{:S(2)}) collective-permute-start(bf16[3,32,1024]{2,1,0:T(8,128)(2,1)S(1)} %get-tuple-element.65), channel_id=1, source_target_pairs={{0,7},{1,6},{2,5},{3,4},{4,3},{5,2},{6,1},{7,0},{8,15},{9,14},{10,... | collective-permute-start | bytes 589832 | tf_op jit(solution)/shard_map/ppermute | solution.py:382
  27.5 1.4 %all-to-all-done = bf16[16,16,1664]{2,1,0:T(8,128)(2,1)S(1)} async-done(((bf16[16,16,1664]{2,1,0:T(8,128)(2,1)}), bf16[16,16,1664]{2,1,0:T(8,128)(2,1)S(1)}, u32[]{:S(2)}, u32[]{:S(2)}) %all-to-all-start) | async-done | bytes 852000 | tf_op jit(solution)/shard_map/all_to_all | solution.py:387
  28.9 0.0 copy-done.14
  28.9 0.9 shard_map.196
  29.8 0.0 collective-permute-done.2.refs_3_
  29.8 0.0 copy-start.4
  29.8 4.5 %collective-permute-done.3.refs_4_ = bf16[3,32,1024]{2,1,0:T(8,128)(2,1)S(1)} collective-permute-done((bf16[3,32,1024]{2,1,0:T(8,128)(2,1)S(1)}, bf16[3,32,1024]{2,1,0:T(8,128)(2,1)S(1)}, u32[]{:S(2)}, u32[]{:S(2)}) %collective-permute-start.3) | collective-permute-done | bytes 196640 | tf_op jit(solution)/shard_map/ppermute | solution.py:382
  34.3 4.5 %collective-permute-done.4.refs_5_ = bf16[3,32,1024]{2,1,0:T(8,128)(2,1)S(1)} collective-permute-done((bf16[3,32,1024]{2,1,0:T(8,128)(2,1)S(1)}, bf16[3,32,1024]{2,1,0:T(8,128)(2,1)S(1)}, u32[]{:S(2)}, u32[]{:S(2)}) %collective-permute-start.4) | collective-permute-done | bytes 196640 | tf_op jit(solution)/shard_map/ppermute | solution.py:382
  38.9 0.0 collective-permute-done.5.refs_6_
  38.9 3.9 %collective-permute-done.6.refs_7_ = bf16[3,32,1024]{2,1,0:T(8,128)(2,1)S(1)} collective-permute-done((bf16[3,32,1024]{2,1,0:T(8,128)(2,1)S(1)}, bf16[3,32,1024]{2,1,0:T(8,128)(2,1)S(1)}, u32[]{:S(2)}, u32[]{:S(2)}) %collective-permute-start.6) | collective-permute-done | bytes 196640 | tf_op jit(solution)/shard_map/ppermute | solution.py:382
  42.8 0.0 copy-done.1
  42.8 0.0 copy-done.2
  42.8 0.0 copy-done.3
  42.8 0.0 copy-done.9
  42.8 0.0 copy-done.10
  42.8 1.9 %shard_map.198 = bf16[256,2048]{1,0:T(8,128)(2,1)S(1)} custom-call(s32[1]{0:T(128)} %bitcast.me, bf16[256,2048]{1,0:T(8,128)(2,1)S(1)} %get-tuple-element.56.message, bf16[2,256,128]{2,1,0:T(8,128)(2,1)S(1)} %copy-done.9, f32[2,16,256]{2,1,0:T(8,128)S(1)} %copy-done.10, ...), custom_call_target="tpu_custom_call", output_to_operand_aliasing={{}: (1, {})} | custom-call | flops 1000000000 | bytes 4000000 | tf_op jit(solution)/shard_map/pallas_call | solution.py:365
  44.7 0.0 copy-done.4
  44.7 0.0 copy-done.5
  44.7 0.0 copy-done.6
  44.7 0.0 copy-done.7
  44.7 23.3 %all_to_all.33 = bf16[16,16,2048]{2,1,0:T(8,128)(2,1)S(1)} all-to-all(bf16[16,16,2048]{2,1,0:T(8,128)(2,1)S(1)} %bitcast.10), channel_id=1, replica_groups=mesh['seq'=16,'head'=8] {'seq'}, dimensions={0} | all-to-all | bytes 2097152 | tf_op jit(solution)/shard_map/all_to_all | solution.py:387
  68.1 1.6 %shard_map.199 = bf16[256,1536]{1,0:T(8,128)(2,1)} custom-call(s32[2]{0:T(128)S(1)} %copy-done.14, f32[32,512]{1,0:T(8,128)S(1)} %get-tuple-element.66.factors, bf16[256,2048]{1,0:T(8,128)(2,1)S(1)} %bitcast.7), custom_call_target="tpu_custom_call" | custom-call | flops 1000000000 | bytes 4000000 | tf_op jit(solution)/shard_map/pallas_call | solution.py:365
  69.7 0.0 copy-done
  69.7 3.6 %all-to-all-start.2 = ((bf16[16,16,1536]{2,1,0:T(8,128)(2,1)}), bf16[16,16,1536]{2,1,0:T(8,128)(2,1)S(1)}, u32[]{:S(2)}, u32[]{:S(2)}) async-start(bf16[16,16,1536]{2,1,0:T(8,128)(2,1)} %bitcast.5), calls=%async_computation.2 | async-start | bytes 1572864 | tf_op jit(solution)/shard_map/all_to_all | solution.py:387
  73.3 11.4 %shard_map.200 = (bf16[3,32,1024]{2,1,0:T(8,128)(2,1)}, bf16[3,32,1024]{2,1,0:T(8,128)(2,1)}, bf16[3,32,1024]{2,1,0:T(8,128)(2,1)}, bf16[3,32,1024]{2,1,0:T(8,12...) custom-call(s32[1]{0:T(128)S(6)} %copy.40.length, ...), custom_call_target="tpu_custom_call" | custom-call | flops 8000000000 | bytes 4000000 | tf_op jit(solution)/shard_map/pallas_call | solution.py:365
  84.7 4.8 %shard_map.201 = (bf16[3,32,1024]{2,1,0:T(8,128)(2,1)}, bf16[3,32,1024]{2,1,0:T(8,128)(2,1)}, bf16[3,32,1024]{2,1,0:T(8,128)(2,1)}, bf16[3,32,1024]{2,1,0:T(8,12...) custom-call(s32[1]{0:T(128)} %bitcast.me, ...), custom_call_target="tpu_custom_call", output_to_operand_aliasing={{0}: (14, {}), {1}: (15, {}), {2}: (16, {}), {3}: (17, {}),... | custom-call | flops 1000000000 | bytes 4000000 | tf_op jit(solution)/shard_map/pallas_call | solution.py:365
  89.5 1.6 %collective-permute-start.10 = (bf16[3,32,1024]{2,1,0:T(8,128)(2,1)}, bf16[3,32,1024]{2,1,0:T(8,128)(2,1)S(1)}, u32[]{:S(2)}, u32[]{:S(2)}) collective-permute-start(bf16[3,32,1024]{2,1,0:T(8,128)(2,1)} %get-tuple-element.87), channel_id=1, source_target_pairs={{0,4},{1,5},{2,6},{3,7},{4,0},{5,1},{6,2},{7,3},{8,12},{9,13},{10,... | collective-permute-start | bytes 589832 | tf_op jit(solution)/shard_map/ppermute | solution.py:382
  91.1 3.2 %collective-permute-start.11 = (bf16[3,32,1024]{2,1,0:T(8,128)(2,1)}, bf16[3,32,1024]{2,1,0:T(8,128)(2,1)S(1)}, u32[]{:S(2)}, u32[]{:S(2)}) collective-permute-start(bf16[3,32,1024]{2,1,0:T(8,128)(2,1)} %get-tuple-element.88), channel_id=1, source_target_pairs={{0,5},{1,4},{2,7},{3,6},{4,1},{5,0},{6,3},{7,2},{8,13},{9,12},{10,... | collective-permute-start | bytes 589832 | tf_op jit(solution)/shard_map/ppermute | solution.py:382
  94.3 2.5 %collective-permute-start.12 = (bf16[3,32,1024]{2,1,0:T(8,128)(2,1)}, bf16[3,32,1024]{2,1,0:T(8,128)(2,1)S(1)}, u32[]{:S(2)}, u32[]{:S(2)}) collective-permute-start(bf16[3,32,1024]{2,1,0:T(8,128)(2,1)} %get-tuple-element.89), channel_id=1, source_target_pairs={{0,6},{1,7},{2,4},{3,5},{4,2},{5,3},{6,0},{7,1},{8,14},{9,15},{10,... | collective-permute-start | bytes 589832 | tf_op jit(solution)/shard_map/ppermute | solution.py:382
  96.8 0.0 collective-permute-start.13
  96.8 0.6 collective-permute-start.7
  97.4 0.0 collective-permute-done.10.refs_4_
  97.4 0.0 collective-permute-start.8
  97.4 4.9 %collective-permute-done.11.refs_5_ = bf16[3,32,1024]{2,1,0:T(8,128)(2,1)S(1)} collective-permute-done((bf16[3,32,1024]{2,1,0:T(8,128)(2,1)}, bf16[3,32,1024]{2,1,0:T(8,128)(2,1)S(1)}, u32[]{:S(2)}, u32[]{:S(2)}) %collective-permute-start.11) | collective-permute-done | bytes 196640 | tf_op jit(solution)/shard_map/ppermute | solution.py:382
  102.3 2.0 %collective-permute-start.9 = (bf16[3,32,1024]{2,1,0:T(8,128)(2,1)}, bf16[3,32,1024]{2,1,0:T(8,128)(2,1)S(1)}, u32[]{:S(2)}, u32[]{:S(2)}) collective-permute-start(bf16[3,32,1024]{2,1,0:T(8,128)(2,1)} %get-tuple-element.86), channel_id=1, source_target_pairs={{0,3},{1,2},{2,1},{3,0},{4,7},{5,6},{6,5},{7,4},{8,11},{9,10},{10,... | collective-permute-start | bytes 589832 | tf_op jit(solution)/shard_map/ppermute | solution.py:382
  104.3 2.3 %collective-permute-done.12.refs_6_ = bf16[3,32,1024]{2,1,0:T(8,128)(2,1)S(1)} collective-permute-done((bf16[3,32,1024]{2,1,0:T(8,128)(2,1)}, bf16[3,32,1024]{2,1,0:T(8,128)(2,1)S(1)}, u32[]{:S(2)}, u32[]{:S(2)}) %collective-permute-start.12) | collective-permute-done | bytes 196640 | tf_op jit(solution)/shard_map/ppermute | solution.py:382
  106.6 4.2 %collective-permute-done.13.refs_7_ = bf16[3,32,1024]{2,1,0:T(8,128)(2,1)S(1)} collective-permute-done((bf16[3,32,1024]{2,1,0:T(8,128)(2,1)}, bf16[3,32,1024]{2,1,0:T(8,128)(2,1)S(1)}, u32[]{:S(2)}, u32[]{:S(2)}) %collective-permute-start.13) | collective-permute-done | bytes 196640 | tf_op jit(solution)/shard_map/ppermute | solution.py:382
  110.8 0.0 collective-permute-done.7.refs_1_
  110.8 0.0 collective-permute-done.8.refs_2_
  110.8 0.1 collective-permute-done.9.refs_3_
  110.9 0.9 copy-done.11
  111.8 1.3 %shard_map.203 = (bf16[2,32,8192]{2,1,0:T(8,128)(2,1)}, bf16[1,32,8192]{2,1,0:T(8,128)(2,1)}) custom-call(s32[1]{0:T(128)} %bitcast.me, bf16[3,32,1024]{2,1,0:T(8,128)(2,1)S(1)} %copy-done.11, bf16[3,32,1024]{2,1,0:T(8,128)(2,1)S(1)} %collective-permute-done.7.refs_1_, bf16[3,32,1024]{2,1,0:T(8,128)(2,1)S(1)} %collective-permute-done.8.refs_2_, ...), custom_call_target="tpu_custom_call" | custom-call | flops 1000000000 | bytes 4000000 | tf_op jit(solution)/shard_map/pallas_call | solution.py:365
  113.1 0.0 all-to-all-done.2
  113.1 0.9 copy-done.16
  114.0 8.1 %shard_map.202 = (bf16[2,256,1024]{2,1,0:T(8,128)(2,1)}, bf16[2,256,128]{2,1,0:T(8,128)(2,1)}, f32[2,16,256]{2,1,0:T(8,128)}, bf16[1,256,1024]{2,1,0:T(8,128)(2,...) custom-call(s32[1]{0:T(128)S(6)} %copy.40.length, bf16[256,2048]{1,0:T(8,128)(2,1)} %bitcast.9, ...), custom_call_target="tpu_custom_call" | custom-call | flops 1000000000 | bytes 4000000 | tf_op jit(solution)/shard_map/pallas_call | solution.py:365
  (12 shorter events, 0.0 us)
Async XLA Ops:
  6.2 8.8 %copy-start.12 = (bf16[2,32,8192]{2,1,0:T(8,128)(2,1)S(1)}, bf16[2,32,8192]{2,1,0:T(8,128)(2,1)}, u32[]{:S(2)}) copy-start(bf16[2,32,8192]{2,1,0:T(8,128)(2,1)} %pt.1) | copy-start | bytes 3145732
  6.2 8.8 %copy-start.13 = (bf16[1,32,8192]{2,1,0:T(8,128)(2,1)S(1)}, bf16[1,32,8192]{2,1,0:T(8,128)(2,1)}, u32[]{:S(2)}) copy-start(bf16[1,32,8192]{2,1,0:T(8,128)(2,1)} %at.1) | copy-start | bytes 1572868
  6.2 8.8 %copy-start.15 = (f32[8,128]{1,0:T(8,128)S(1)}, f32[8,128]{1,0:T(8,128)}, u32[]{:S(2)}) copy-start(f32[8,128]{1,0:T(8,128)} %get-tuple-element.57.done) | copy-start | bytes 12292
  6.2 22.7 %all-to-all-start = ((bf16[16,16,1664]{2,1,0:T(8,128)(2,1)}), bf16[16,16,1664]{2,1,0:T(8,128)(2,1)S(1)}, u32[]{:S(2)}, u32[]{:S(2)}) async-start(bf16[16,16,1664]{2,1,0:T(8,128)(2,1)} %bitcast.15), calls=%async_computation | async-start | bytes 1703936 | tf_op jit(solution)/shard_map/all_to_all | solution.py:387
  15.0 13.9 %copy-start.14 = (s32[2]{0:T(128)S(1)}, s32[2]{0:T(128)}, u32[]{:S(2)}) copy-start(s32[2]{0:T(128)} %sizes.3) | copy-start | bytes 28
  16.3 26.5 %copy-start.1 = (bf16[3,32,1024]{2,1,0:T(8,128)(2,1)}, bf16[3,32,1024]{2,1,0:T(8,128)(2,1)S(1)}, u32[]{:S(2)}) copy-start(bf16[3,32,1024]{2,1,0:T(8,128)(2,1)S(1)} %get-tuple-element.58.refs_0_) | copy-start | bytes 589828
  16.3 6.0 %collective-permute-start = (bf16[3,32,1024]{2,1,0:T(8,128)(2,1)S(1)}, bf16[3,32,1024]{2,1,0:T(8,128)(2,1)S(1)}, u32[]{:S(2)}, u32[]{:S(2)}) collective-permute-start(bf16[3,32,1024]{2,1,0:T(8,128)(2,1)S(1)} %get-tuple-element.59), channel_id=1, source_target_pairs={{0,1},{1,0},{2,3},{3,2},{4,5},{5,4},{6,7},{7,6},{8,9},{9,8},{10,11... | collective-permute-start | bytes 589832 | tf_op jit(solution)/shard_map/ppermute | solution.py:382
  17.3 7.5 %collective-permute-start.1 = (bf16[3,32,1024]{2,1,0:T(8,128)(2,1)S(1)}, bf16[3,32,1024]{2,1,0:T(8,128)(2,1)S(1)}, u32[]{:S(2)}, u32[]{:S(2)}) collective-permute-start(bf16[3,32,1024]{2,1,0:T(8,128)(2,1)S(1)} %get-tuple-element.60), channel_id=1, source_target_pairs={{0,2},{1,3},{2,0},{3,1},{4,6},{5,7},{6,4},{7,5},{8,10},{9,11},{10,... | collective-permute-start | bytes 589832 | tf_op jit(solution)/shard_map/ppermute | solution.py:382
  18.5 11.3 %collective-permute-start.2 = (bf16[3,32,1024]{2,1,0:T(8,128)(2,1)}, bf16[3,32,1024]{2,1,0:T(8,128)(2,1)S(1)}, u32[]{:S(2)}, u32[]{:S(2)}) collective-permute-start(bf16[3,32,1024]{2,1,0:T(8,128)(2,1)} %get-tuple-element.61), channel_id=1, source_target_pairs={{0,3},{1,2},{2,1},{3,0},{4,7},{5,6},{6,5},{7,4},{8,11},{9,10},{10,... | collective-permute-start | bytes 589832 | tf_op jit(solution)/shard_map/ppermute | solution.py:382
  19.0 15.3 %collective-permute-start.3 = (bf16[3,32,1024]{2,1,0:T(8,128)(2,1)S(1)}, bf16[3,32,1024]{2,1,0:T(8,128)(2,1)S(1)}, u32[]{:S(2)}, u32[]{:S(2)}) collective-permute-start(bf16[3,32,1024]{2,1,0:T(8,128)(2,1)S(1)} %get-tuple-element.62), channel_id=1, source_target_pairs={{0,4},{1,5},{2,6},{3,7},{4,0},{5,1},{6,2},{7,3},{8,12},{9,13},{10,... | collective-permute-start | bytes 589832 | tf_op jit(solution)/shard_map/ppermute | solution.py:382
  21.8 17.1 %collective-permute-start.4 = (bf16[3,32,1024]{2,1,0:T(8,128)(2,1)S(1)}, bf16[3,32,1024]{2,1,0:T(8,128)(2,1)S(1)}, u32[]{:S(2)}, u32[]{:S(2)}) collective-permute-start(bf16[3,32,1024]{2,1,0:T(8,128)(2,1)S(1)} %get-tuple-element.63), channel_id=1, source_target_pairs={{0,5},{1,4},{2,7},{3,6},{4,1},{5,0},{6,3},{7,2},{8,13},{9,12},{10,... | collective-permute-start | bytes 589832 | tf_op jit(solution)/shard_map/ppermute | solution.py:382
  22.3 20.5 %copy-start.2 = (bf16[3,32,1024]{2,1,0:T(8,128)(2,1)}, bf16[3,32,1024]{2,1,0:T(8,128)(2,1)S(1)}, u32[]{:S(2)}) copy-start(bf16[3,32,1024]{2,1,0:T(8,128)(2,1)S(1)} %collective-permute-done.refs_1_) | copy-start | bytes 589828
  22.3 16.6 %collective-permute-start.5 = (bf16[3,32,1024]{2,1,0:T(8,128)(2,1)S(1)}, bf16[3,32,1024]{2,1,0:T(8,128)(2,1)S(1)}, u32[]{:S(2)}, u32[]{:S(2)}) collective-permute-start(bf16[3,32,1024]{2,1,0:T(8,128)(2,1)S(1)} %get-tuple-element.64), channel_id=1, source_target_pairs={{0,6},{1,7},{2,4},{3,5},{4,2},{5,3},{6,0},{7,1},{8,14},{9,15},{10,... | collective-permute-start | bytes 589832 | tf_op jit(solution)/shard_map/ppermute | solution.py:382
  24.8 18.0 %copy-start.3 = (bf16[3,32,1024]{2,1,0:T(8,128)(2,1)}, bf16[3,32,1024]{2,1,0:T(8,128)(2,1)S(1)}, u32[]{:S(2)}) copy-start(bf16[3,32,1024]{2,1,0:T(8,128)(2,1)S(1)} %collective-permute-done.1.refs_2_) | copy-start | bytes 589828
  24.8 18.0 %collective-permute-start.6 = (bf16[3,32,1024]{2,1,0:T(8,128)(2,1)S(1)}, bf16[3,32,1024]{2,1,0:T(8,128)(2,1)S(1)}, u32[]{:S(2)}, u32[]{:S(2)}) collective-permute-start(bf16[3,32,1024]{2,1,0:T(8,128)(2,1)S(1)} %get-tuple-element.65), channel_id=1, source_target_pairs={{0,7},{1,6},{2,5},{3,4},{4,3},{5,2},{6,1},{7,0},{8,15},{9,14},{10,... | collective-permute-start | bytes 589832 | tf_op jit(solution)/shard_map/ppermute | solution.py:382
  28.9 13.9 %copy-start.9 = (bf16[2,256,128]{2,1,0:T(8,128)(2,1)S(1)}, bf16[2,256,128]{2,1,0:T(8,128)(2,1)}, u32[]{:S(2)}) copy-start(bf16[2,256,128]{2,1,0:T(8,128)(2,1)} %pw.5) | copy-start | bytes 393220
  28.9 13.9 %copy-start.10 = (f32[2,16,256]{2,1,0:T(8,128)S(1)}, f32[2,16,256]{2,1,0:T(8,128)}, u32[]{:S(2)}) copy-start(f32[2,16,256]{2,1,0:T(8,128)} %pd.9) | copy-start | bytes 98308
  29.8 14.9 %copy-start.4 = (bf16[3,32,1024]{2,1,0:T(8,128)(2,1)}, bf16[3,32,1024]{2,1,0:T(8,128)(2,1)S(1)}, u32[]{:S(2)}) copy-start(bf16[3,32,1024]{2,1,0:T(8,128)(2,1)S(1)} %collective-permute-done.2.refs_3_) | copy-start | bytes 589828
  34.3 10.4 %copy-start.5 = (bf16[3,32,1024]{2,1,0:T(8,128)(2,1)}, bf16[3,32,1024]{2,1,0:T(8,128)(2,1)S(1)}, u32[]{:S(2)}) copy-start(bf16[3,32,1024]{2,1,0:T(8,128)(2,1)S(1)} %collective-permute-done.3.refs_4_) | copy-start | bytes 589828
  38.9 5.9 %copy-start.6 = (bf16[3,32,1024]{2,1,0:T(8,128)(2,1)}, bf16[3,32,1024]{2,1,0:T(8,128)(2,1)S(1)}, u32[]{:S(2)}) copy-start(bf16[3,32,1024]{2,1,0:T(8,128)(2,1)S(1)} %collective-permute-done.4.refs_5_) | copy-start | bytes 589828
  38.9 5.9 %copy-start.7 = (bf16[3,32,1024]{2,1,0:T(8,128)(2,1)}, bf16[3,32,1024]{2,1,0:T(8,128)(2,1)S(1)}, u32[]{:S(2)}) copy-start(bf16[3,32,1024]{2,1,0:T(8,128)(2,1)S(1)} %collective-permute-done.5.refs_6_) | copy-start | bytes 589828
  42.8 2.0 %copy-start.8 = (bf16[3,32,1024]{2,1,0:T(8,128)(2,1)}, bf16[3,32,1024]{2,1,0:T(8,128)(2,1)S(1)}, u32[]{:S(2)}) copy-start(bf16[3,32,1024]{2,1,0:T(8,128)(2,1)S(1)} %collective-permute-done.6.refs_7_) | copy-start | bytes 589828
  68.1 1.6 %copy-start = (bf16[16,16,2048]{2,1,0:T(8,128)(2,1)}, bf16[16,16,2048]{2,1,0:T(8,128)(2,1)S(1)}, u32[]{:S(2)}) copy-start(bf16[16,16,2048]{2,1,0:T(8,128)(2,1)S(1)} %all_to_all.33) | copy-start | bytes 3145732
  69.7 43.4 %all-to-all-start.2 = ((bf16[16,16,1536]{2,1,0:T(8,128)(2,1)}), bf16[16,16,1536]{2,1,0:T(8,128)(2,1)S(1)}, u32[]{:S(2)}, u32[]{:S(2)}) async-start(bf16[16,16,1536]{2,1,0:T(8,128)(2,1)} %bitcast.5), calls=%async_computation.2 | async-start | bytes 1572864 | tf_op jit(solution)/shard_map/all_to_all | solution.py:387
  89.5 7.9 %collective-permute-start.10 = (bf16[3,32,1024]{2,1,0:T(8,128)(2,1)}, bf16[3,32,1024]{2,1,0:T(8,128)(2,1)S(1)}, u32[]{:S(2)}, u32[]{:S(2)}) collective-permute-start(bf16[3,32,1024]{2,1,0:T(8,128)(2,1)} %get-tuple-element.87), channel_id=1, source_target_pairs={{0,4},{1,5},{2,6},{3,7},{4,0},{5,1},{6,2},{7,3},{8,12},{9,13},{10,... | collective-permute-start | bytes 589832 | tf_op jit(solution)/shard_map/ppermute | solution.py:382
  91.1 11.1 %collective-permute-start.11 = (bf16[3,32,1024]{2,1,0:T(8,128)(2,1)}, bf16[3,32,1024]{2,1,0:T(8,128)(2,1)S(1)}, u32[]{:S(2)}, u32[]{:S(2)}) collective-permute-start(bf16[3,32,1024]{2,1,0:T(8,128)(2,1)} %get-tuple-element.88), channel_id=1, source_target_pairs={{0,5},{1,4},{2,7},{3,6},{4,1},{5,0},{6,3},{7,2},{8,13},{9,12},{10,... | collective-permute-start | bytes 589832 | tf_op jit(solution)/shard_map/ppermute | solution.py:382
  94.3 12.3 %collective-permute-start.12 = (bf16[3,32,1024]{2,1,0:T(8,128)(2,1)}, bf16[3,32,1024]{2,1,0:T(8,128)(2,1)S(1)}, u32[]{:S(2)}, u32[]{:S(2)}) collective-permute-start(bf16[3,32,1024]{2,1,0:T(8,128)(2,1)} %get-tuple-element.89), channel_id=1, source_target_pairs={{0,6},{1,7},{2,4},{3,5},{4,2},{5,3},{6,0},{7,1},{8,14},{9,15},{10,... | collective-permute-start | bytes 589832 | tf_op jit(solution)/shard_map/ppermute | solution.py:382
  96.8 14.0 %collective-permute-start.13 = (bf16[3,32,1024]{2,1,0:T(8,128)(2,1)}, bf16[3,32,1024]{2,1,0:T(8,128)(2,1)S(1)}, u32[]{:S(2)}, u32[]{:S(2)}) collective-permute-start(bf16[3,32,1024]{2,1,0:T(8,128)(2,1)} %get-tuple-element.90), channel_id=1, source_target_pairs={{0,7},{1,6},{2,5},{3,4},{4,3},{5,2},{6,1},{7,0},{8,15},{9,14},{10,... | collective-permute-start | bytes 589832 | tf_op jit(solution)/shard_map/ppermute | solution.py:382
  96.8 14.0 %collective-permute-start.7 = (bf16[3,32,1024]{2,1,0:T(8,128)(2,1)}, bf16[3,32,1024]{2,1,0:T(8,128)(2,1)S(1)}, u32[]{:S(2)}, u32[]{:S(2)}) collective-permute-start(bf16[3,32,1024]{2,1,0:T(8,128)(2,1)} %get-tuple-element.84), channel_id=1, source_target_pairs={{0,1},{1,0},{2,3},{3,2},{4,5},{5,4},{6,7},{7,6},{8,9},{9,8},{10,11... | collective-permute-start | bytes 589832 | tf_op jit(solution)/shard_map/ppermute | solution.py:382
  97.4 13.4 %collective-permute-start.8 = (bf16[3,32,1024]{2,1,0:T(8,128)(2,1)}, bf16[3,32,1024]{2,1,0:T(8,128)(2,1)S(1)}, u32[]{:S(2)}, u32[]{:S(2)}) collective-permute-start(bf16[3,32,1024]{2,1,0:T(8,128)(2,1)} %get-tuple-element.85), channel_id=1, source_target_pairs={{0,2},{1,3},{2,0},{3,1},{4,6},{5,7},{6,4},{7,5},{8,10},{9,11},{10,... | collective-permute-start | bytes 589832 | tf_op jit(solution)/shard_map/ppermute | solution.py:382
  102.3 8.6 %collective-permute-start.9 = (bf16[3,32,1024]{2,1,0:T(8,128)(2,1)}, bf16[3,32,1024]{2,1,0:T(8,128)(2,1)S(1)}, u32[]{:S(2)}, u32[]{:S(2)}) collective-permute-start(bf16[3,32,1024]{2,1,0:T(8,128)(2,1)} %get-tuple-element.86), channel_id=1, source_target_pairs={{0,3},{1,2},{2,1},{3,0},{4,7},{5,6},{6,5},{7,4},{8,11},{9,10},{10,... | collective-permute-start | bytes 589832 | tf_op jit(solution)/shard_map/ppermute | solution.py:382
  110.9 0.9 copy-start.11
  113.1 0.9 copy-start.16

commit v4 on v2

--- a/solution.py
+++ b/solution.py
@@ -117,7 +117,8 @@
         x[pl.ds(there, ROWS), :] = chunks[k][0]
 
 
-def reach_kernel(length, pr, pd, pc, ar, ad, ac, out, reads, decays, cots, stage, factors, came, went):
+def reach_kernel(length, me, pr, pd, pc, ar, ad, ac, out, place, reads, decays, cots, stage, factors, came, went):
+    place[0] = me[0]
     coming = []
     for b in range(3):
         group = []
@@ -394,12 +395,12 @@
     pieces = [each(ROWS, L)] * GROUP
     prompt_side = [own(B, N), own(H, B), own(B, L)]
     answer_side = [one(B, N), one(H, B), one(B, L)]
-    (m1,) = call(
+    m1, place = call(
         reach_kernel,
         1,
-        [SMEM] + [ANY] * 6,
-        [(ANY, shape((B, 3 * HALF + N)))],
-        (length, pr, pd, pc, ar, ad, ac),
+        [SMEM, SMEM] + [ANY] * 6,
+        [(ANY, shape((B, 3 * HALF + N))), (SMEM, shape((1,), jnp.int32))],
+        (length, me, pr, pd, pc, ar, ad, ac),
         (
             pltpu.VMEM((3, B, N), BF16),
             pltpu.VMEM((3, H, B), F32),
@@ -416,7 +417,7 @@
         1,
         [SMEM, ANY, ANY],
         [(VMEM, shape((3, ROWS, L)))] * GROUP,
-        (me, pt, at),
+        (place, pt, at),
         (
             pltpu.SemaphoreType.DMA((2 * GROUP,)),
         ),

time: 122 us -> 123 us (level)
  no operation moved by 1% of the time
where the time goes in v4:
time: 123 us
  Pallas kernels  36.7 us (30%)
  starting transfers between devices  33.5 us (27%)
  waiting for transfers between devices  25.8 us (21%)
  blocking collectives  23.3 us (19%)
  local copies, waits for them, and re-layouts  1.87 us (2%)
  between operations  1.52 us (1%)
    pallas_call x9, Pallas kernels, call(): pl.pallas_call(kernel, grid=(steps,), in_specs=ins, out_specs=[spec for s...  36.7 us
    ppermute x14, waiting for transfers between devices, exchange(): lax.ppermute(chunks[k], 'head', [(i, i ^ k) for i in range(GROUP)])  25.1 us
    all_to_all x1, blocking collectives, transposed(): lax.all_to_all(message, 'seq', split_axis=0, concat_axis=0, tiled=True)  23.3 us
    ppermute x14, starting transfers between devices, exchange(): lax.ppermute(chunks[k], 'head', [(i, i ^ k) for i in range(GROUP)])  21.1 us
    all_to_all x2, starting transfers between devices, transposed(): lax.all_to_all(message, 'seq', split_axis=0, concat_axis=0, tiled=True)  12.3 us
  transfers between devices with their start and end apart: 16, of which 8 were waited for; matrix products, arithmetic and copies ran while one was open for 0% of the time, Pallas kernels for 16%

profile of v4, /device:TPU:1, one launch (start us, length us, event | category | flops | bytes accessed | tf_op | source)
XLA Modules:
  0.0 122.7 jit_solution(11485352156470036682)
XLA Ops:
  1.3 4.8 %shard_map.195 = (bf16[256,1664]{1,0:T(8,128)(2,1)}, s32[1]{0:T(128)}) custom-call(s32[1]{0:T(128)S(6)} %copy.40.length, s32[1]{0:T(128)} %bitcast.me, bf16[2,256,128]{2,1,0:T(8,128)(2,1)} %pr.5, f32[2,16,256]{2,1,0:T(8,128)} %pd.9, bf16[2,256,1024]{2,1,0:T(8,128)(2,1)} %pc.5, bf16[1,256,128]{2,1,0:T(8,128)(2,1)} %ar.5, f32[1,16,256]{2,1,0:T(8,128)} %ad.5, ...), custom_call_target="tpu_custom_call" | custom-call | flops 1000000000 | bytes 4000000 | tf_op jit(solution)/shard_map/pallas_call | solution.py:365
  6.1 0.0 copy-start.12
  6.1 0.0 copy-start.13
  6.2 8.7 %all-to-all-start = ((bf16[16,16,1664]{2,1,0:T(8,128)(2,1)}), bf16[16,16,1664]{2,1,0:T(8,128)(2,1)S(1)}, u32[]{:S(2)}, u32[]{:S(2)}) async-start(bf16[16,16,1664]{2,1,0:T(8,128)(2,1)} %bitcast.15), calls=%async_computation | async-start | bytes 1703936 | tf_op jit(solution)/shard_map/all_to_all | solution.py:387
  14.9 0.0 copy-done.12
  14.9 0.0 copy-done.13
  14.9 0.0 copy-start.14
  14.9 1.9 %shard_map.197 = (bf16[3,32,1024]{2,1,0:T(8,128)(2,1)S(1)}, bf16[3,32,1024]{2,1,0:T(8,128)(2,1)S(1)}, bf16[3,32,1024]{2,1,0:T(8,128)(2,1)S(1)}, bf16[3,32,1024]{...) custom-call(s32[1]{0:T(128)} %get-tuple-element.57.me, ...), custom_call_target="tpu_custom_call" | custom-call | flops 1000000000 | bytes 4000000 | tf_op jit(solution)/shard_map/pallas_call | solution.py:365
  16.8 0.0 copy-start.1
  16.8 1.0 collective-permute-start
  17.8 1.2 collective-permute-start.1
  19.1 0.5 collective-permute-start.2
  19.6 2.7 %collective-permute-start.3 = (bf16[3,32,1024]{2,1,0:T(8,128)(2,1)S(1)}, bf16[3,32,1024]{2,1,0:T(8,128)(2,1)S(1)}, u32[]{:S(2)}, u32[]{:S(2)}) collective-permute-start(bf16[3,32,1024]{2,1,0:T(8,128)(2,1)S(1)} %get-tuple-element.62), channel_id=1, source_target_pairs={{0,4},{1,5},{2,6},{3,7},{4,0},{5,1},{6,2},{7,3},{8,12},{9,13},{10,... | collective-permute-start | bytes 589832 | tf_op jit(solution)/shard_map/ppermute | solution.py:382
  22.3 0.5 collective-permute-start.4
  22.8 0.0 collective-permute-done.refs_1_
  22.8 2.5 %collective-permute-start.5 = (bf16[3,32,1024]{2,1,0:T(8,128)(2,1)S(1)}, bf16[3,32,1024]{2,1,0:T(8,128)(2,1)S(1)}, u32[]{:S(2)}, u32[]{:S(2)}) collective-permute-start(bf16[3,32,1024]{2,1,0:T(8,128)(2,1)S(1)} %get-tuple-element.64), channel_id=1, source_target_pairs={{0,6},{1,7},{2,4},{3,5},{4,2},{5,3},{6,0},{7,1},{8,14},{9,15},{10,... | collective-permute-start | bytes 589832 | tf_op jit(solution)/shard_map/ppermute | solution.py:382
  25.3 0.0 collective-permute-done.1.refs_2_
  25.3 2.7 %collective-permute-start.6 = (bf16[3,32,1024]{2,1,0:T(8,128)(2,1)S(1)}, bf16[3,32,1024]{2,1,0:T(8,128)(2,1)S(1)}, u32[]{:S(2)}, u32[]{:S(2)}) collective-permute-start(bf16[3,32,1024]{2,1,0:T(8,128)(2,1)S(1)} %get-tuple-element.65), channel_id=1, source_target_pairs={{0,7},{1,6},{2,5},{3,4},{4,3},{5,2},{6,1},{7,0},{8,15},{9,14},{10,... | collective-permute-start | bytes 589832 | tf_op jit(solution)/shard_map/ppermute | solution.py:382
  28.1 0.8 all-to-all-done
  28.8 0.0 copy-done.14
  28.8 0.9 shard_map.196
  29.7 0.0 collective-permute-done.2.refs_3_
  29.7 0.0 copy-start.4
  29.7 5.1 %collective-permute-done.3.refs_4_ = bf16[3,32,1024]{2,1,0:T(8,128)(2,1)S(1)} collective-permute-done((bf16[3,32,1024]{2,1,0:T(8,128)(2,1)S(1)}, bf16[3,32,1024]{2,1,0:T(8,128)(2,1)S(1)}, u32[]{:S(2)}, u32[]{:S(2)}) %collective-permute-start.3) | collective-permute-done | bytes 196640 | tf_op jit(solution)/shard_map/ppermute | solution.py:382
  34.9 4.5 %collective-permute-done.4.refs_5_ = bf16[3,32,1024]{2,1,0:T(8,128)(2,1)S(1)} collective-permute-done((bf16[3,32,1024]{2,1,0:T(8,128)(2,1)S(1)}, bf16[3,32,1024]{2,1,0:T(8,128)(2,1)S(1)}, u32[]{:S(2)}, u32[]{:S(2)}) %collective-permute-start.4) | collective-permute-done | bytes 196640 | tf_op jit(solution)/shard_map/ppermute | solution.py:382
  39.4 0.0 collective-permute-done.5.refs_6_
  39.4 3.9 %collective-permute-done.6.refs_7_ = bf16[3,32,1024]{2,1,0:T(8,128)(2,1)S(1)} collective-permute-done((bf16[3,32,1024]{2,1,0:T(8,128)(2,1)S(1)}, bf16[3,32,1024]{2,1,0:T(8,128)(2,1)S(1)}, u32[]{:S(2)}, u32[]{:S(2)}) %collective-permute-start.6) | collective-permute-done | bytes 196640 | tf_op jit(solution)/shard_map/ppermute | solution.py:382
  43.3 0.0 copy-done.1
  43.3 0.0 copy-done.2
  43.3 0.0 copy-done.3
  43.3 0.0 copy-done.9
  43.3 0.0 copy-done.10
  43.4 1.9 %shard_map.198 = bf16[256,2048]{1,0:T(8,128)(2,1)S(1)} custom-call(s32[1]{0:T(128)} %bitcast.me, bf16[256,2048]{1,0:T(8,128)(2,1)S(1)} %get-tuple-element.56.message, bf16[2,256,128]{2,1,0:T(8,128)(2,1)S(1)} %copy-done.9, f32[2,16,256]{2,1,0:T(8,128)S(1)} %copy-done.10, ...), custom_call_target="tpu_custom_call", output_to_operand_aliasing={{}: (1, {})} | custom-call | flops 1000000000 | bytes 4000000 | tf_op jit(solution)/shard_map/pallas_call | solution.py:365
  45.2 0.0 copy-done.4
  45.2 0.0 copy-done.5
  45.3 0.0 copy-done.6
  45.3 0.0 copy-done.7
  45.3 0.0 copy-done.8
  45.3 23.3 %all_to_all.33 = bf16[16,16,2048]{2,1,0:T(8,128)(2,1)S(1)} all-to-all(bf16[16,16,2048]{2,1,0:T(8,128)(2,1)S(1)} %bitcast.10), channel_id=1, replica_groups=mesh['seq'=16,'head'=8] {'seq'}, dimensions={0} | all-to-all | bytes 2097152 | tf_op jit(solution)/shard_map/all_to_all | solution.py:387
  68.6 1.6 %shard_map.199 = bf16[256,1536]{1,0:T(8,128)(2,1)} custom-call(s32[2]{0:T(128)S(1)} %copy-done.14, f32[32,512]{1,0:T(8,128)S(1)} %get-tuple-element.66.factors, bf16[256,2048]{1,0:T(8,128)(2,1)S(1)} %bitcast.7), custom_call_target="tpu_custom_call" | custom-call | flops 1000000000 | bytes 4000000 | tf_op jit(solution)/shard_map/pallas_call | solution.py:365
  70.2 0.0 copy-done
  70.2 3.6 %all-to-all-start.2 = ((bf16[16,16,1536]{2,1,0:T(8,128)(2,1)}), bf16[16,16,1536]{2,1,0:T(8,128)(2,1)S(1)}, u32[]{:S(2)}, u32[]{:S(2)}) async-start(bf16[16,16,1536]{2,1,0:T(8,128)(2,1)} %bitcast.5), calls=%async_computation.2 | async-start | bytes 1572864 | tf_op jit(solution)/shard_map/all_to_all | solution.py:387
  73.9 11.4 %shard_map.200 = (bf16[3,32,1024]{2,1,0:T(8,128)(2,1)}, bf16[3,32,1024]{2,1,0:T(8,128)(2,1)}, bf16[3,32,1024]{2,1,0:T(8,128)(2,1)}, bf16[3,32,1024]{2,1,0:T(8,12...) custom-call(s32[1]{0:T(128)S(6)} %copy.40.length, ...), custom_call_target="tpu_custom_call" | custom-call | flops 8000000000 | bytes 4000000 | tf_op jit(solution)/shard_map/pallas_call | solution.py:365
  85.2 4.9 %shard_map.201 = (bf16[3,32,1024]{2,1,0:T(8,128)(2,1)}, bf16[3,32,1024]{2,1,0:T(8,128)(2,1)}, bf16[3,32,1024]{2,1,0:T(8,128)(2,1)}, bf16[3,32,1024]{2,1,0:T(8,12...) custom-call(s32[1]{0:T(128)} %bitcast.me, ...), custom_call_target="tpu_custom_call", output_to_operand_aliasing={{0}: (14, {}), {1}: (15, {}), {2}: (16, {}), {3}: (17, {}),... | custom-call | flops 1000000000 | bytes 4000000 | tf_op jit(solution)/shard_map/pallas_call | solution.py:365
  90.1 1.6 %collective-permute-start.10 = (bf16[3,32,1024]{2,1,0:T(8,128)(2,1)}, bf16[3,32,1024]{2,1,0:T(8,128)(2,1)S(1)}, u32[]{:S(2)}, u32[]{:S(2)}) collective-permute-start(bf16[3,32,1024]{2,1,0:T(8,128)(2,1)} %get-tuple-element.87), channel_id=1, source_target_pairs={{0,4},{1,5},{2,6},{3,7},{4,0},{5,1},{6,2},{7,3},{8,12},{9,13},{10,... | collective-permute-start | bytes 589832 | tf_op jit(solution)/shard_map/ppermute | solution.py:382
  91.7 3.2 %collective-permute-start.11 = (bf16[3,32,1024]{2,1,0:T(8,128)(2,1)}, bf16[3,32,1024]{2,1,0:T(8,128)(2,1)S(1)}, u32[]{:S(2)}, u32[]{:S(2)}) collective-permute-start(bf16[3,32,1024]{2,1,0:T(8,128)(2,1)} %get-tuple-element.88), channel_id=1, source_target_pairs={{0,5},{1,4},{2,7},{3,6},{4,1},{5,0},{6,3},{7,2},{8,13},{9,12},{10,... | collective-permute-start | bytes 589832 | tf_op jit(solution)/shard_map/ppermute | solution.py:382
  94.9 2.5 %collective-permute-start.12 = (bf16[3,32,1024]{2,1,0:T(8,128)(2,1)}, bf16[3,32,1024]{2,1,0:T(8,128)(2,1)S(1)}, u32[]{:S(2)}, u32[]{:S(2)}) collective-permute-start(bf16[3,32,1024]{2,1,0:T(8,128)(2,1)} %get-tuple-element.89), channel_id=1, source_target_pairs={{0,6},{1,7},{2,4},{3,5},{4,2},{5,3},{6,0},{7,1},{8,14},{9,15},{10,... | collective-permute-start | bytes 589832 | tf_op jit(solution)/shard_map/ppermute | solution.py:382
  97.4 0.0 collective-permute-start.13
  97.4 0.6 collective-permute-start.7
  98.0 0.0 collective-permute-done.10.refs_4_
  98.0 0.0 collective-permute-start.8
  98.0 4.9 %collective-permute-done.11.refs_5_ = bf16[3,32,1024]{2,1,0:T(8,128)(2,1)S(1)} collective-permute-done((bf16[3,32,1024]{2,1,0:T(8,128)(2,1)}, bf16[3,32,1024]{2,1,0:T(8,128)(2,1)S(1)}, u32[]{:S(2)}, u32[]{:S(2)}) %collective-permute-start.11) | collective-permute-done | bytes 196640 | tf_op jit(solution)/shard_map/ppermute | solution.py:382
  102.8 2.0 %collective-permute-start.9 = (bf16[3,32,1024]{2,1,0:T(8,128)(2,1)}, bf16[3,32,1024]{2,1,0:T(8,128)(2,1)S(1)}, u32[]{:S(2)}, u32[]{:S(2)}) collective-permute-start(bf16[3,32,1024]{2,1,0:T(8,128)(2,1)} %get-tuple-element.86), channel_id=1, source_target_pairs={{0,3},{1,2},{2,1},{3,0},{4,7},{5,6},{6,5},{7,4},{8,11},{9,10},{10,... | collective-permute-start | bytes 589832 | tf_op jit(solution)/shard_map/ppermute | solution.py:382
  104.8 2.3 %collective-permute-done.12.refs_6_ = bf16[3,32,1024]{2,1,0:T(8,128)(2,1)S(1)} collective-permute-done((bf16[3,32,1024]{2,1,0:T(8,128)(2,1)}, bf16[3,32,1024]{2,1,0:T(8,128)(2,1)S(1)}, u32[]{:S(2)}, u32[]{:S(2)}) %collective-permute-start.12) | collective-permute-done | bytes 196640 | tf_op jit(solution)/shard_map/ppermute | solution.py:382
  107.2 4.2 %collective-permute-done.13.refs_7_ = bf16[3,32,1024]{2,1,0:T(8,128)(2,1)S(1)} collective-permute-done((bf16[3,32,1024]{2,1,0:T(8,128)(2,1)}, bf16[3,32,1024]{2,1,0:T(8,128)(2,1)S(1)}, u32[]{:S(2)}, u32[]{:S(2)}) %collective-permute-start.13) | collective-permute-done | bytes 196640 | tf_op jit(solution)/shard_map/ppermute | solution.py:382
  111.4 0.0 collective-permute-done.7.refs_1_
  111.4 0.0 collective-permute-done.8.refs_2_
  111.4 0.1 collective-permute-done.9.refs_3_
  111.4 0.9 copy-done.11
  112.4 1.3 %shard_map.203 = (bf16[2,32,8192]{2,1,0:T(8,128)(2,1)}, bf16[1,32,8192]{2,1,0:T(8,128)(2,1)}) custom-call(s32[1]{0:T(128)} %bitcast.me, bf16[3,32,1024]{2,1,0:T(8,128)(2,1)S(1)} %copy-done.11, bf16[3,32,1024]{2,1,0:T(8,128)(2,1)S(1)} %collective-permute-done.7.refs_1_, bf16[3,32,1024]{2,1,0:T(8,128)(2,1)S(1)} %collective-permute-done.8.refs_2_, ...), custom_call_target="tpu_custom_call" | custom-call | flops 1000000000 | bytes 4000000 | tf_op jit(solution)/shard_map/pallas_call | solution.py:365
  113.6 0.0 all-to-all-done.2
  113.7 0.0 copy-start.15
  113.7 0.9 copy-done.15
  114.5 8.1 %shard_map.202 = (bf16[2,256,1024]{2,1,0:T(8,128)(2,1)}, bf16[2,256,128]{2,1,0:T(8,128)(2,1)}, f32[2,16,256]{2,1,0:T(8,128)}, bf16[1,256,1024]{2,1,0:T(8,128)(2,...) custom-call(s32[1]{0:T(128)S(6)} %copy.40.length, bf16[256,2048]{1,0:T(8,128)(2,1)} %bitcast.9, ...), custom_call_target="tpu_custom_call" | custom-call | flops 1000000000 | bytes 4000000 | tf_op jit(solution)/shard_map/pallas_call | solution.py:365
  (10 shorter events, 0.0 us)
Async XLA Ops:
  6.1 8.8 %copy-start.12 = (bf16[2,32,8192]{2,1,0:T(8,128)(2,1)S(1)}, bf16[2,32,8192]{2,1,0:T(8,128)(2,1)}, u32[]{:S(2)}) copy-start(bf16[2,32,8192]{2,1,0:T(8,128)(2,1)} %pt.1) | copy-start | bytes 3145732
  6.1 8.8 %copy-start.13 = (bf16[1,32,8192]{2,1,0:T(8,128)(2,1)S(1)}, bf16[1,32,8192]{2,1,0:T(8,128)(2,1)}, u32[]{:S(2)}) copy-start(bf16[1,32,8192]{2,1,0:T(8,128)(2,1)} %at.1) | copy-start | bytes 1572868
  6.2 22.7 %all-to-all-start = ((bf16[16,16,1664]{2,1,0:T(8,128)(2,1)}), bf16[16,16,1664]{2,1,0:T(8,128)(2,1)S(1)}, u32[]{:S(2)}, u32[]{:S(2)}) async-start(bf16[16,16,1664]{2,1,0:T(8,128)(2,1)} %bitcast.15), calls=%async_computation | async-start | bytes 1703936 | tf_op jit(solution)/shard_map/all_to_all | solution.py:387
  14.9 13.9 %copy-start.14 = (s32[2]{0:T(128)S(1)}, s32[2]{0:T(128)}, u32[]{:S(2)}) copy-start(s32[2]{0:T(128)} %sizes.3) | copy-start | bytes 28
  16.8 26.5 %copy-start.1 = (bf16[3,32,1024]{2,1,0:T(8,128)(2,1)}, bf16[3,32,1024]{2,1,0:T(8,128)(2,1)S(1)}, u32[]{:S(2)}) copy-start(bf16[3,32,1024]{2,1,0:T(8,128)(2,1)S(1)} %get-tuple-element.58.refs_0_) | copy-start | bytes 589828
  16.8 6.0 %collective-permute-start = (bf16[3,32,1024]{2,1,0:T(8,128)(2,1)S(1)}, bf16[3,32,1024]{2,1,0:T(8,128)(2,1)S(1)}, u32[]{:S(2)}, u32[]{:S(2)}) collective-permute-start(bf16[3,32,1024]{2,1,0:T(8,128)(2,1)S(1)} %get-tuple-element.59), channel_id=1, source_target_pairs={{0,1},{1,0},{2,3},{3,2},{4,5},{5,4},{6,7},{7,6},{8,9},{9,8},{10,11... | collective-permute-start | bytes 589832 | tf_op jit(solution)/shard_map/ppermute | solution.py:382
  17.8 7.5 %collective-permute-start.1 = (bf16[3,32,1024]{2,1,0:T(8,128)(2,1)S(1)}, bf16[3,32,1024]{2,1,0:T(8,128)(2,1)S(1)}, u32[]{:S(2)}, u32[]{:S(2)}) collective-permute-start(bf16[3,32,1024]{2,1,0:T(8,128)(2,1)S(1)} %get-tuple-element.60), channel_id=1, source_target_pairs={{0,2},{1,3},{2,0},{3,1},{4,6},{5,7},{6,4},{7,5},{8,10},{9,11},{10,... | collective-permute-start | bytes 589832 | tf_op jit(solution)/shard_map/ppermute | solution.py:382
  19.1 10.7 %collective-permute-start.2 = (bf16[3,32,1024]{2,1,0:T(8,128)(2,1)}, bf16[3,32,1024]{2,1,0:T(8,128)(2,1)S(1)}, u32[]{:S(2)}, u32[]{:S(2)}) collective-permute-start(bf16[3,32,1024]{2,1,0:T(8,128)(2,1)} %get-tuple-element.61), channel_id=1, source_target_pairs={{0,3},{1,2},{2,1},{3,0},{4,7},{5,6},{6,5},{7,4},{8,11},{9,10},{10,... | collective-permute-start | bytes 589832 | tf_op jit(solution)/shard_map/ppermute | solution.py:382
  19.6 15.3 %collective-permute-start.3 = (bf16[3,32,1024]{2,1,0:T(8,128)(2,1)S(1)}, bf16[3,32,1024]{2,1,0:T(8,128)(2,1)S(1)}, u32[]{:S(2)}, u32[]{:S(2)}) collective-permute-start(bf16[3,32,1024]{2,1,0:T(8,128)(2,1)S(1)} %get-tuple-element.62), channel_id=1, source_target_pairs={{0,4},{1,5},{2,6},{3,7},{4,0},{5,1},{6,2},{7,3},{8,12},{9,13},{10,... | collective-permute-start | bytes 589832 | tf_op jit(solution)/shard_map/ppermute | solution.py:382
  22.3 17.1 %collective-permute-start.4 = (bf16[3,32,1024]{2,1,0:T(8,128)(2,1)S(1)}, bf16[3,32,1024]{2,1,0:T(8,128)(2,1)S(1)}, u32[]{:S(2)}, u32[]{:S(2)}) collective-permute-start(bf16[3,32,1024]{2,1,0:T(8,128)(2,1)S(1)} %get-tuple-element.63), channel_id=1, source_target_pairs={{0,5},{1,4},{2,7},{3,6},{4,1},{5,0},{6,3},{7,2},{8,13},{9,12},{10,... | collective-permute-start | bytes 589832 | tf_op jit(solution)/shard_map/ppermute | solution.py:382
  22.8 20.5 %copy-start.2 = (bf16[3,32,1024]{2,1,0:T(8,128)(2,1)}, bf16[3,32,1024]{2,1,0:T(8,128)(2,1)S(1)}, u32[]{:S(2)}) copy-start(bf16[3,32,1024]{2,1,0:T(8,128)(2,1)S(1)} %collective-permute-done.refs_1_) | copy-start | bytes 589828
  22.8 16.6 %collective-permute-start.5 = (bf16[3,32,1024]{2,1,0:T(8,128)(2,1)S(1)}, bf16[3,32,1024]{2,1,0:T(8,128)(2,1)S(1)}, u32[]{:S(2)}, u32[]{:S(2)}) collective-permute-start(bf16[3,32,1024]{2,1,0:T(8,128)(2,1)S(1)} %get-tuple-element.64), channel_id=1, source_target_pairs={{0,6},{1,7},{2,4},{3,5},{4,2},{5,3},{6,0},{7,1},{8,14},{9,15},{10,... | collective-permute-start | bytes 589832 | tf_op jit(solution)/shard_map/ppermute | solution.py:382
  25.3 18.0 %copy-start.3 = (bf16[3,32,1024]{2,1,0:T(8,128)(2,1)}, bf16[3,32,1024]{2,1,0:T(8,128)(2,1)S(1)}, u32[]{:S(2)}) copy-start(bf16[3,32,1024]{2,1,0:T(8,128)(2,1)S(1)} %collective-permute-done.1.refs_2_) | copy-start | bytes 589828
  25.3 18.0 %collective-permute-start.6 = (bf16[3,32,1024]{2,1,0:T(8,128)(2,1)S(1)}, bf16[3,32,1024]{2,1,0:T(8,128)(2,1)S(1)}, u32[]{:S(2)}, u32[]{:S(2)}) collective-permute-start(bf16[3,32,1024]{2,1,0:T(8,128)(2,1)S(1)} %get-tuple-element.65), channel_id=1, source_target_pairs={{0,7},{1,6},{2,5},{3,4},{4,3},{5,2},{6,1},{7,0},{8,15},{9,14},{10,... | collective-permute-start | bytes 589832 | tf_op jit(solution)/shard_map/ppermute | solution.py:382
  28.8 14.5 %copy-start.9 = (bf16[2,256,128]{2,1,0:T(8,128)(2,1)S(1)}, bf16[2,256,128]{2,1,0:T(8,128)(2,1)}, u32[]{:S(2)}) copy-start(bf16[2,256,128]{2,1,0:T(8,128)(2,1)} %pw.5) | copy-start | bytes 393220
  28.8 14.5 %copy-start.10 = (f32[2,16,256]{2,1,0:T(8,128)S(1)}, f32[2,16,256]{2,1,0:T(8,128)}, u32[]{:S(2)}) copy-start(f32[2,16,256]{2,1,0:T(8,128)} %pd.9) | copy-start | bytes 98308
  29.7 15.5 %copy-start.4 = (bf16[3,32,1024]{2,1,0:T(8,128)(2,1)}, bf16[3,32,1024]{2,1,0:T(8,128)(2,1)S(1)}, u32[]{:S(2)}) copy-start(bf16[3,32,1024]{2,1,0:T(8,128)(2,1)S(1)} %collective-permute-done.2.refs_3_) | copy-start | bytes 589828
  34.9 10.4 %copy-start.5 = (bf16[3,32,1024]{2,1,0:T(8,128)(2,1)}, bf16[3,32,1024]{2,1,0:T(8,128)(2,1)S(1)}, u32[]{:S(2)}) copy-start(bf16[3,32,1024]{2,1,0:T(8,128)(2,1)S(1)} %collective-permute-done.3.refs_4_) | copy-start | bytes 589828
  39.4 5.9 %copy-start.6 = (bf16[3,32,1024]{2,1,0:T(8,128)(2,1)}, bf16[3,32,1024]{2,1,0:T(8,128)(2,1)S(1)}, u32[]{:S(2)}) copy-start(bf16[3,32,1024]{2,1,0:T(8,128)(2,1)S(1)} %collective-permute-done.4.refs_5_) | copy-start | bytes 589828
  39.4 5.9 %copy-start.7 = (bf16[3,32,1024]{2,1,0:T(8,128)(2,1)}, bf16[3,32,1024]{2,1,0:T(8,128)(2,1)S(1)}, u32[]{:S(2)}) copy-start(bf16[3,32,1024]{2,1,0:T(8,128)(2,1)S(1)} %collective-permute-done.5.refs_6_) | copy-start | bytes 589828
  43.3 2.0 %copy-start.8 = (bf16[3,32,1024]{2,1,0:T(8,128)(2,1)}, bf16[3,32,1024]{2,1,0:T(8,128)(2,1)S(1)}, u32[]{:S(2)}) copy-start(bf16[3,32,1024]{2,1,0:T(8,128)(2,1)S(1)} %collective-permute-done.6.refs_7_) | copy-start | bytes 589828
  68.6 1.6 %copy-start = (bf16[16,16,2048]{2,1,0:T(8,128)(2,1)}, bf16[16,16,2048]{2,1,0:T(8,128)(2,1)S(1)}, u32[]{:S(2)}) copy-start(bf16[16,16,2048]{2,1,0:T(8,128)(2,1)S(1)} %all_to_all.33) | copy-start | bytes 3145732
  70.2 43.4 %all-to-all-start.2 = ((bf16[16,16,1536]{2,1,0:T(8,128)(2,1)}), bf16[16,16,1536]{2,1,0:T(8,128)(2,1)S(1)}, u32[]{:S(2)}, u32[]{:S(2)}) async-start(bf16[16,16,1536]{2,1,0:T(8,128)(2,1)} %bitcast.5), calls=%async_computation.2 | async-start | bytes 1572864 | tf_op jit(solution)/shard_map/all_to_all | solution.py:387
  90.1 7.9 %collective-permute-start.10 = (bf16[3,32,1024]{2,1,0:T(8,128)(2,1)}, bf16[3,32,1024]{2,1,0:T(8,128)(2,1)S(1)}, u32[]{:S(2)}, u32[]{:S(2)}) collective-permute-start(bf16[3,32,1024]{2,1,0:T(8,128)(2,1)} %get-tuple-element.87), channel_id=1, source_target_pairs={{0,4},{1,5},{2,6},{3,7},{4,0},{5,1},{6,2},{7,3},{8,12},{9,13},{10,... | collective-permute-start | bytes 589832 | tf_op jit(solution)/shard_map/ppermute | solution.py:382
  91.7 11.1 %collective-permute-start.11 = (bf16[3,32,1024]{2,1,0:T(8,128)(2,1)}, bf16[3,32,1024]{2,1,0:T(8,128)(2,1)S(1)}, u32[]{:S(2)}, u32[]{:S(2)}) collective-permute-start(bf16[3,32,1024]{2,1,0:T(8,128)(2,1)} %get-tuple-element.88), channel_id=1, source_target_pairs={{0,5},{1,4},{2,7},{3,6},{4,1},{5,0},{6,3},{7,2},{8,13},{9,12},{10,... | collective-permute-start | bytes 589832 | tf_op jit(solution)/shard_map/ppermute | solution.py:382
  94.9 12.3 %collective-permute-start.12 = (bf16[3,32,1024]{2,1,0:T(8,128)(2,1)}, bf16[3,32,1024]{2,1,0:T(8,128)(2,1)S(1)}, u32[]{:S(2)}, u32[]{:S(2)}) collective-permute-start(bf16[3,32,1024]{2,1,0:T(8,128)(2,1)} %get-tuple-element.89), channel_id=1, source_target_pairs={{0,6},{1,7},{2,4},{3,5},{4,2},{5,3},{6,0},{7,1},{8,14},{9,15},{10,... | collective-permute-start | bytes 589832 | tf_op jit(solution)/shard_map/ppermute | solution.py:382
  97.4 14.0 %collective-permute-start.13 = (bf16[3,32,1024]{2,1,0:T(8,128)(2,1)}, bf16[3,32,1024]{2,1,0:T(8,128)(2,1)S(1)}, u32[]{:S(2)}, u32[]{:S(2)}) collective-permute-start(bf16[3,32,1024]{2,1,0:T(8,128)(2,1)} %get-tuple-element.90), channel_id=1, source_target_pairs={{0,7},{1,6},{2,5},{3,4},{4,3},{5,2},{6,1},{7,0},{8,15},{9,14},{10,... | collective-permute-start | bytes 589832 | tf_op jit(solution)/shard_map/ppermute | solution.py:382
  97.4 14.0 %collective-permute-start.7 = (bf16[3,32,1024]{2,1,0:T(8,128)(2,1)}, bf16[3,32,1024]{2,1,0:T(8,128)(2,1)S(1)}, u32[]{:S(2)}, u32[]{:S(2)}) collective-permute-start(bf16[3,32,1024]{2,1,0:T(8,128)(2,1)} %get-tuple-element.84), channel_id=1, source_target_pairs={{0,1},{1,0},{2,3},{3,2},{4,5},{5,4},{6,7},{7,6},{8,9},{9,8},{10,11... | collective-permute-start | bytes 589832 | tf_op jit(solution)/shard_map/ppermute | solution.py:382
  98.0 13.4 %collective-permute-start.8 = (bf16[3,32,1024]{2,1,0:T(8,128)(2,1)}, bf16[3,32,1024]{2,1,0:T(8,128)(2,1)S(1)}, u32[]{:S(2)}, u32[]{:S(2)}) collective-permute-start(bf16[3,32,1024]{2,1,0:T(8,128)(2,1)} %get-tuple-element.85), channel_id=1, source_target_pairs={{0,2},{1,3},{2,0},{3,1},{4,6},{5,7},{6,4},{7,5},{8,10},{9,11},{10,... | collective-permute-start | bytes 589832 | tf_op jit(solution)/shard_map/ppermute | solution.py:382
  102.8 8.6 %collective-permute-start.9 = (bf16[3,32,1024]{2,1,0:T(8,128)(2,1)}, bf16[3,32,1024]{2,1,0:T(8,128)(2,1)S(1)}, u32[]{:S(2)}, u32[]{:S(2)}) collective-permute-start(bf16[3,32,1024]{2,1,0:T(8,128)(2,1)} %get-tuple-element.86), channel_id=1, source_target_pairs={{0,3},{1,2},{2,1},{3,0},{4,7},{5,6},{6,5},{7,4},{8,11},{9,10},{10,... | collective-permute-start | bytes 589832 | tf_op jit(solution)/shard_map/ppermute | solution.py:382
  111.4 0.9 copy-start.11
  113.7 0.9 copy-start.15
